TPU v7x, 32 devices: a whole 2x2x4 slice. The times are simulated.
32 devices in a mesh: row: 16 (over z, x, core), col: 2 (over y).
Axes of the slice: x: 2, y: 2, z: 4, core: 2. Of those that a mesh axis runs over, the one named last changes fastest.
Arguments:
- features: bfloat16 [16384, 512], P(('row', 'col')), may hold values from -6 to 6
- factor: float32 [16384, 1024], P(('row', 'col')), may hold values from -0.03 to 0.03
- ip_weights: float32 [16384], P(('row', 'col')), may hold values from 0.1 to 30
- pivot_owner: int32 [256], replicated, may hold values from 0 to 31, as said below
- pivot_position: int32 [256], replicated, may hold values from 0 to 511, as said below
Outputs:
- new_columns: float32 [16384, 256], P(('row', 'col'))
- gram_rows: float32 [256, 1280], replicated
Inputs may be any that keep to these rules, and one draw needn't show every extreme that they name: `pivot_owner`: each device owns at most 18 pivots, and some device owns exactly 18. `pivot_position`: pivots with the same owner have different positions.
All inputs are finite; a program needn't handle non-finite values.
Results may differ from a plain program's by a relative error of at most 0.0003.
Values may be sent and summed in bfloat16 or wider, within the bound.
No kernel may reach another device: no remote copies, remote signals or barrier semaphores. Data moves between devices by JAX's collectives and lax.ppermute only.
A program may use at most 64 MiB of HBM per device.

v0:
```python
from functools import partial

import jax
import jax.numpy as jnp
from jax import lax
from jax.experimental import pallas as pl
from jax.experimental.pallas import tpu as pltpu
from jax.sharding import PartitionSpec as P


HIGHEST = lax.Precision.HIGHEST
f32 = jnp.float32
bf16 = jnp.bfloat16
i32 = jnp.int32
PANEL = 32
STEPS = 2.0**20


def dot(a, b, left, right, precision=None):
    return lax.dot_general(
        a, b, (((left,), (right,)), ((), ())), precision=precision, preferred_element_type=f32
    )


def nn(a, b, precision=None):
    return dot(a, b, 1, 0, precision)


def nt(a, b, precision=None):
    return dot(a, b, 1, 1, precision)


def tn(a, b, precision=None):
    return dot(a, b, 0, 0, precision)


def split(a):
    high = a.astype(bf16)
    low = (a - high.astype(f32)).astype(bf16)
    return high, low


def near(x):
    return pltpu.with_memory_space_constraint(x, pltpu.VMEM)


def call(kernel, outs, *args, smem=0, scratch=(), flops=10**9):
    specs = [pl.BlockSpec(memory_space=pltpu.SMEM)] * smem + [
        pl.BlockSpec(memory_space=pltpu.VMEM)
    ] * (len(args) - smem)
    return pl.pallas_call(
        kernel,
        out_shape=outs,
        in_specs=specs,
        out_specs=jax.tree.map(lambda _: pl.BlockSpec(memory_space=pltpu.VMEM), outs),
        scratch_shapes=scratch,
        compiler_params=pltpu.CompilerParams(vmem_limit_bytes=24 << 20),
        cost_estimate=pl.CostEstimate(flops=flops, transcendentals=0, bytes_accessed=10**6),
    )(*args)


def onehot(mask):
    return jnp.where(mask, 1.0, 0.0).astype(bf16)


def iota(shape, axis):
    return lax.broadcasted_iota(i32, shape, axis)


def pick_kernel(chunks):
    def kernel(
        rank_ref, owner_ref, position_ref, features_ref, factor_ref,
        slots_x_ref, slots_h_ref, kept_ref, high_ref, low_ref,
        owner_in, position_in, factor_in, slots_sum, small_sems, factor_sems,
    ):
        slots = slots_x_ref.shape[0]
        pivots = owner_ref.shape[1]
        rows, _ = features_ref.shape
        size = rows // chunks
        small = [
            pltpu.make_async_copy(source, target, small_sems.at[k])
            for k, (source, target) in enumerate(
                ((owner_ref, owner_in), (position_ref, position_in), (features_ref, kept_ref))
            )
        ]
        large = [
            pltpu.make_async_copy(
                factor_ref.at[pl.ds(k * size, size), :],
                factor_in.at[pl.ds(k * size, size), :],
                factor_sems.at[k],
            )
            for k in range(chunks)
        ]
        for copy in small + large:
            copy.start()
        ahead = onehot(iota((pivots, pivots), 0) < iota((pivots, pivots), 1))
        small[0].wait()
        mine = owner_in[...] == rank_ref[0]
        mine_rows = jnp.broadcast_to(jnp.where(mine, 1.0, 0.0), (8, pivots)).astype(bf16)
        order = nn(mine_rows, ahead)[0:1, :].astype(i32)
        chosen = onehot((iota((slots, pivots), 0) == order) & mine)
        small[1].wait()
        located = onehot(iota((rows, pivots), 0) == position_in[...])
        take = nt(chosen, located).astype(bf16)
        small[2].wait()
        slots_x_ref[...] = nn(take, kept_ref[...]).astype(bf16)
        for k in range(chunks):
            large[k].wait()
            part = slice(k * size, (k + 1) * size)
            exact = factor_in[part, :]
            high, low = split(exact)
            high_ref[part, :] = high
            low_ref[part, :] = low
            rest = (exact - high.astype(f32) - low.astype(f32)).astype(bf16)
            chosen_rows = take[:, part]
            got = nn(chosen_rows, high) + (nn(chosen_rows, low) + nn(chosen_rows, rest))
            if k:
                got = slots_sum[...] + got
            if k < chunks - 1:
                slots_sum[...] = got
            else:
                slots_h_ref[...] = jnp.round(got * STEPS).astype(i32).astype(jnp.int16)

    return kernel


def prepare_kernel(core, side, col_low, others, slots, devices):
    def kernel(rank_ref, owner_ref, features_ref, source_ref, norm_ref):
        pivots = owner_ref.shape[1]
        owner = owner_ref[...]
        ahead = onehot(iota((pivots, pivots), 0) < iota((pivots, pivots), 1))
        owned = iota((devices, pivots), 0) == owner
        counts = nn(onehot(owned), ahead)
        slot_rank = jnp.sum(jnp.where(owned, counts, 0.0), axis=0, keepdims=True).astype(i32)
        apart = owner ^ rank_ref[0]
        bit = lambda mask: (apart >> (mask.bit_length() - 1)) & 1
        place = jnp.zeros_like(apart)
        for k, mask in enumerate(others):
            place = place + (bit(mask) << k)
        at = len(others)
        low_core = (owner & core) == 0
        lead = jnp.where(low_core, bit(side), bit(col_low))
        trail = jnp.where(low_core, bit(col_low), bit(side))
        place = place + (lead << at) + (trail << (at + 1)) + (bit(core) << (at + 2))
        source_ref[...] = place * slots + slot_rank
        wide = features_ref[...].astype(f32)
        norm_ref[...] = nt(jnp.ones((8, wide.shape[1]), f32), wide * wide, HIGHEST)[0:1, :]

    return kernel


def mixed(cross, left, right, width):
    base = jnp.exp((left + right - 2.0 * cross) * (-0.25 / width))
    square = base * base
    return 0.5 * base + 0.3 * square + 0.2 * (square * square)


def join_kernel(*refs):
    out_ref = refs[-1]
    at = 0
    for ref in refs[:-1]:
        out_ref[at : at + ref.shape[0]] = ref[...]
        at += ref.shape[0]


def spots(rank, core, side, col_low):
    bit = lambda mask: (rank >> (mask.bit_length() - 1)) & 1
    lead = jnp.where(bit(core) == 0, bit(side), bit(col_low))
    trail = jnp.where(bit(core) == 0, bit(col_low), bit(side))
    return bit(core), lead * 2 + trail, trail * 2 + lead


def gram_half(residual_ref, half, weights, high, low, order, out_ref):
    count, piece, _ = out_ref.shape
    size = count * piece
    depth = high.shape[1]
    rows = residual_ref[pl.ds(pl.multiple_of(half * size, size), size), :]
    weighted = rows * weights
    weighted_hi, weighted_lo = split(weighted)
    left = nn(weighted_hi, high) + (nn(weighted_lo, high) + nn(weighted_hi, low))
    right = nt(weighted, residual_ref[...], HIGHEST)
    for p in range(count):
        spot = (order & (count - 1)) ^ p
        out_ref[spot, :, 0:depth] = left[p * piece : (p + 1) * piece, :]
        out_ref[spot, :, depth:] = right[p * piece : (p + 1) * piece, :]


def chosen_rows(source, start, held):
    return onehot(iota((held, source.shape[1]), 0) == source - start)


def ordered_h(source, start, h_ref):
    chosen = chosen_rows(source, start, h_ref.shape[0])
    q = h_ref[...].astype(i32)
    coarse = (q + 128) >> 8
    fine = q - (coarse << 8)
    coarse = (coarse.astype(f32) * (256 / STEPS)).astype(bf16)
    fine = (fine.astype(f32) * (1 / STEPS)).astype(bf16)
    return tn(chosen, coarse), tn(chosen, fine)


def ordered_x(source, start, x_ref):
    return tn(chosen_rows(source, start, x_ref.shape[0]), x_ref[...])


def order_kernel(source_ref, a_x_ref, a_h_ref, c_x_ref, c_h_ref, x_ref, coarse_ref, fine_ref):
    held = a_x_ref.shape[0]
    source = source_ref[...]
    x_ref[...] = (
        ordered_x(source, 0, a_x_ref) + ordered_x(source, 2 * held, c_x_ref)
    ).astype(bf16)
    one, two = ordered_h(source, 0, a_h_ref), ordered_h(source, 2 * held, c_h_ref)
    coarse_ref[...] = (one[0] + two[0]).astype(bf16)
    fine_ref[...] = (one[1] + two[1]).astype(bf16)


def across_kernel(source_ref, h_ref, coarse_in, fine_in, coarse_ref, fine_ref):
    coarse, fine = ordered_h(source_ref[...], h_ref.shape[0], h_ref)
    coarse_ref[...] = (coarse_in[...].astype(f32) + coarse).astype(bf16)
    fine_ref[...] = (fine_in[...].astype(f32) + fine).astype(bf16)


def product_kernel(
    source_ref, h_ref, coarse_in, fine_in, high_ref, low_ref, coarse_ref, fine_ref, product_ref
):
    coarse, fine = ordered_h(source_ref[...], 3 * h_ref.shape[0], h_ref)
    coarse = (coarse_in[...].astype(f32) + coarse).astype(bf16)
    fine = (fine_in[...].astype(f32) + fine).astype(bf16)
    coarse_ref[...] = coarse
    fine_ref[...] = fine
    high = high_ref[...]
    product_ref[...] = nt(coarse, high) + (nt(fine, high) + nt(coarse, low_ref[...]))


def residual_kernel(
    masks, samples, rank_ref, source_ref, x_ref, b_x_ref, d_x_ref, product_ref,
    features_ref, high_ref, low_ref, norm_ref, weights_ref, pivot_ref, residual_ref, send_ref,
):
    held, width = b_x_ref.shape
    source = source_ref[...]
    new = ordered_x(source, held, b_x_ref) + ordered_x(source, 3 * held, d_x_ref)
    pivot_x = (new + x_ref[...].astype(f32)).astype(bf16)
    pivot_ref[...] = pivot_x
    high, low = high_ref[...], low_ref[...]
    pivot_wide = pivot_x.astype(f32)
    pivot_norm = jnp.sum(pivot_wide * pivot_wide, axis=1, keepdims=True)
    residual_ref[...] = (
        mixed(nt(pivot_x, features_ref[...]), pivot_norm, norm_ref[...], width) - product_ref[...]
    )
    core, _, order = spots(rank_ref[0], *masks)
    weights = weights_ref[...] / samples
    gram_half(residual_ref, 1 - core, weights, high, low, order, send_ref)


def keep_kernel(masks, samples, rank_ref, residual_ref, high_ref, low_ref, weights_ref, keep_ref):
    core, order, _ = spots(rank_ref[0], *masks)
    weights = weights_ref[...] / samples
    gram_half(residual_ref, core, weights, high_ref[...], low_ref[...], order, keep_ref)


def eliminate(work_ref, k):
    n = work_ref.shape[0]
    size = PANEL
    lane = iota((size, n), 1)
    row_wide = iota((size, n), 0)
    row = iota((size, 128), 0)
    first = pl.multiple_of(k * size, size)
    rows = work_ref[pl.ds(first, size), :]
    slab = rows[:, 0:128]
    for g in range(1, n // 128):
        slab = jnp.where(first >= g * 128, rows[:, g * 128 : (g + 1) * 128], slab)
    slab = pltpu.roll(slab, (128 - first % 128) % 128, 1)
    columns = [jnp.broadcast_to(slab[:, j : j + 1], (size, 128)) for j in range(size)]
    scale = jnp.zeros((size, 128), f32)
    for j in range(size):
        pivot = columns[j][j : j + 1, :]
        scale = jnp.where(row == j, lax.rsqrt(pivot), scale)
        factor = jnp.where(row > j, columns[j] * (1.0 / pivot), 0.0)
        for l in range(j + 1, size):
            columns[l] = columns[l] - factor * columns[l][j : j + 1, :]
        rows = jnp.where(lane == first + j, jnp.where(row_wide == j, 1.0, 0.0), rows)
        rows = rows - jnp.concatenate([factor] * (n // 128), axis=1) * rows[j : j + 1, :]
    rows = rows * jnp.concatenate([scale] * (n // 128), axis=1)
    upper = jnp.where(lane >= first + size, rows, 0.0)
    update = tn(upper, rows, HIGHEST)
    full_lane, full_row = iota((n, n), 1), iota((n, n), 0)
    stale = (full_row >= first + size) & (full_lane >= first) & (full_lane < first + size)
    work_ref[...] = jnp.where(stale, 0.0, work_ref[...]) - update
    work_ref[pl.ds(first, size), :] = rows


def inverse_kernel(start, stop):
    def kernel(*refs):
        work_ref = refs[-1]
        n = work_ref.shape[0]
        if start == 0:
            pivot_x, pivot_hi, pivot_lo = [ref[...] for ref in refs[:3]]
            width = pivot_x.shape[1]
            wide = pivot_x.astype(f32)
            square = wide * wide
            left = jnp.sum(square, axis=1, keepdims=True)
            right = nt(jnp.ones((8, width), f32), square, HIGHEST)[0:1, :]
            product = nt(pivot_hi, pivot_hi) + (nt(pivot_lo, pivot_hi) + nt(pivot_hi, pivot_lo))
            work_ref[...] = mixed(nt(pivot_x, pivot_x), left, right, width) - product
        else:
            work_ref[...] = refs[0][...]

        def panel(k, carry):
            eliminate(work_ref, k)
            return carry

        lax.fori_loop(start, stop, panel, 0)
        if stop == n // PANEL:
            work_ref[...] = jnp.where(iota((n, n), 1) <= iota((n, n), 0), work_ref[...], 0.0)

    return kernel


def columns_kernel(residual_ref, inverse_ref, out_ref):
    out_ref[...] = dot(residual_ref[...], inverse_ref[...], 0, 1, HIGHEST)


def rows_kernel(masks, rank_ref, *refs):
    inverse_ref, out_ref, work_ref, done_ref, sems = refs[-5:]
    parts = refs[:-5]
    count = len(parts) // 2
    piece = parts[0].shape[1]
    n = inverse_ref.shape[0]
    total = done_ref.shape[1]
    depth = total - n
    core, near_order, far_order = spots(rank_ref[0], *masks)
    for k, part in enumerate(parts):
        mine = k < count
        half = core if mine else 1 - core
        at = half * count + ((near_order if mine else far_order) ^ (k % count))
        work_ref[pl.ds(pl.multiple_of(at * piece, piece), piece), :] = part[0]
    inverse = inverse_ref[...]
    copies = []
    for k, at in enumerate([depth] + list(range(0, depth, depth // 2))):
        here = slice(at, total if at == depth else at + depth // 2)
        done = nn(inverse, work_ref[:, here], HIGHEST)
        if at == depth:
            done = nt(done, inverse, HIGHEST)
        done_ref[:, here] = done
        copies.append(pltpu.make_async_copy(done_ref.at[:, here], out_ref.at[:, here], sems.at[k]))
        copies[-1].start()
    for copy in copies:
        copy.wait()


def body(features, factor, ip_weights, pivot_owner, pivot_position):
    axes = ("row", "col")
    n_row, n_col = lax.axis_size("row"), lax.axis_size("col")
    devices = n_row * n_col
    row_bits, col_bits = n_row.bit_length() - 1, n_col.bit_length() - 1
    assert n_row == 1 << row_bits and n_col == 1 << col_bits and row_bits >= 2 and col_bits >= 1
    col_low = 1
    core = n_col
    side = 2 * n_col
    masks = (core, side, col_low)
    others = [n_col << k for k in range(2, row_bits)] + [1 << k for k in range(1, col_bits)]
    others = others[::-1]
    rank = (lax.axis_index("row") * n_col + lax.axis_index("col")).astype(i32)[None]
    pivots = pivot_owner.shape[0]
    slots = 2 * pivots // devices + 2
    rows, width = features.shape
    depth = factor.shape[1]
    samples = rows * devices
    total = depth + pivots

    def pair(mask):
        return [(i, i ^ mask) for i in range(devices)]

    def staggered(mask_zero, mask_one):
        return [(i, i ^ (mask_one if i & core else mask_zero)) for i in range(devices)]

    first_pair = staggered(side, col_low)
    second_pair = staggered(col_low, side)
    both_pair = pair(side | col_low)
    core_pair = pair(core)

    def move(value, perm):
        return lax.ppermute(value, axes, perm)

    def tie(*values):
        return lax.optimization_barrier(values)

    owner_row = pivot_owner[None, :]
    chunks = 4
    far = lambda x: pltpu.with_memory_space_constraint(x, pltpu.HBM)
    held_x, held_h, kept, high, low = pl.pallas_call(
        pick_kernel(chunks),
        out_shape=(
            pltpu.VMEM((slots, width), bf16),
            pltpu.VMEM((slots, depth), jnp.int16),
            pltpu.VMEM((rows, width), bf16),
            pltpu.VMEM((rows, depth), bf16),
            pltpu.VMEM((rows, depth), bf16),
        ),
        in_specs=[pl.BlockSpec(memory_space=pltpu.SMEM)] + [pl.BlockSpec(memory_space=pltpu.HBM)] * 4,
        out_specs=tuple(pl.BlockSpec(memory_space=pltpu.VMEM) for _ in range(5)),
        scratch_shapes=[
            pltpu.VMEM((1, pivots), i32),
            pltpu.VMEM((1, pivots), i32),
            pltpu.VMEM((rows, depth), f32),
            pltpu.VMEM((slots, depth), f32),
            pltpu.SemaphoreType.DMA((3,)),
            pltpu.SemaphoreType.DMA((chunks,)),
        ],
        compiler_params=pltpu.CompilerParams(vmem_limit_bytes=24 << 20),
    )(rank, far(owner_row), far(pivot_position[None, :]), far(features), far(factor))

    def joined(one, two):
        shape = (2 * one.shape[0], one.shape[1])
        return call(join_kernel, pltpu.VMEM(shape, one.dtype), one, two)

    prepared = False
    perms = [pair(mask) for mask in others] + [first_pair]
    for perm in perms:
        got_h = near(move(held_h, perm))
        got_x = near(move(held_x, perm))
        if not prepared:
            source, norm = call(
                prepare_kernel(core, side, col_low, others, slots, devices),
                (pltpu.VMEM((1, pivots), i32), pltpu.VMEM((1, rows), f32)),
                rank, owner_row, kept, smem=1,
            )
            got_h, got_x, source, norm = tie(got_h, got_x, source, norm)
            prepared = True
        held_h = joined(held_h, got_h)
        held_x = joined(held_x, got_x)
    across_h = near(move(held_h, second_pair))
    across_x = near(move(held_x, second_pair))
    far_h, far_x = near(move(held_h, core_pair)), near(move(held_x, core_pair))
    plane = pltpu.VMEM((pivots, depth), bf16)
    pivot_x, coarse, fine = call(
        order_kernel,
        (pltpu.VMEM((pivots, width), bf16), plane, plane),
        source, held_x, held_h, far_x, far_h,
    )
    across_h, coarse, fine = tie(across_h, coarse, fine)
    beyond_h = near(move(across_h, core_pair))
    coarse, fine = call(across_kernel, (plane, plane), source, across_h, coarse, fine)
    across_x, coarse, fine = tie(across_x, coarse, fine)
    beyond_x = near(move(across_x, core_pair))
    coarse, fine, product = call(
        product_kernel,
        (plane, plane, pltpu.VMEM((pivots, rows), f32)),
        source, beyond_h, coarse, fine, high, low,
    )
    beyond_x, product = tie(beyond_x, product)

    weights = ip_weights[None, :]
    half = pltpu.VMEM((4, pivots // 8, total), f32)
    pivot_x, residual, send = call(
        partial(residual_kernel, masks, samples),
        (pltpu.VMEM((pivots, width), bf16), pltpu.VMEM((pivots, rows), f32), half),
        rank, source, pivot_x, across_x, beyond_x, product, kept, high, low, norm, weights,
        smem=1,
    )
    received = move(send, core_pair)
    keep = call(partial(keep_kernel, masks, samples), half, rank, residual, high, low, weights, smem=1)
    keep = keep + received

    panels = pivots // PANEL
    cuts = [0, panels // 4, panels * 5 // 8, panels]

    def eliminate_step(step, *given):
        return call(
            inverse_kernel(cuts[step], cuts[step + 1]), pltpu.VMEM((pivots, pivots), f32), *given
        )

    keep, pivot_x, coarse, fine = tie(keep, pivot_x, coarse, fine)
    from_both = move(keep[3:4], both_pair)
    from_second = move(keep[1:2], second_pair)
    from_first = move(keep[2:3], first_pair)
    work = eliminate_step(0, pivot_x, coarse, fine)
    from_both, from_second, from_first, work = tie(from_both, from_second, from_first, work)
    keep = (keep[0:1] + from_both) + (from_second + from_first)
    step = 1
    for mask in others:
        got = move(keep, pair(mask))
        if step < len(cuts) - 1:
            work = eliminate_step(step, work)
            got, work = tie(got, work)
            step += 1
        keep = keep + got
    inverse = work
    keep, inverse = tie(keep, inverse)
    pieces = [near(keep)] + [near(move(keep, perm)) for perm in (second_pair, first_pair, both_pair)]
    new_columns = call(columns_kernel, jax.ShapeDtypeStruct((rows, pivots), f32), residual, inverse)
    pieces[3], new_columns = tie(pieces[3], new_columns)
    pieces += [near(move(piece, core_pair)) for piece in pieces]
    gram_rows = pl.pallas_call(
        partial(rows_kernel, masks),
        out_shape=jax.ShapeDtypeStruct((pivots, total), f32),
        in_specs=[pl.BlockSpec(memory_space=pltpu.SMEM)] + [pl.BlockSpec(memory_space=pltpu.VMEM)] * 9,
        out_specs=pl.BlockSpec(memory_space=pltpu.HBM),
        scratch_shapes=[
            pltpu.VMEM((pivots, total), f32),
            pltpu.VMEM((pivots, total), f32),
            pltpu.SemaphoreType.DMA((3,)),
        ],
        compiler_params=pltpu.CompilerParams(vmem_limit_bytes=24 << 20),
    )(rank, *pieces, inverse)
    return (new_columns, gram_rows)


def solution(mesh):
    placed = (P(("row", "col"), None), P(("row", "col"), None), P(("row", "col")), P(), P())

    return jax.shard_map(
        body, mesh=mesh, in_specs=placed, out_specs=(P(("row", "col"), None), P()), check_vma=False
    )
```

profile of v0, /device:TPU:0, one launch (start us, length us, event | category | flops | bytes accessed | tf_op | source)
XLA Modules:
  0.0 83.0 jit_solution(7528485225806096668)
XLA Ops:
  0.6 3.1 %shard_map.68 = (bf16[18,512]{1,0:T(8,128)(2,1)S(1)}, s16[18,1024]{1,0:T(8,128)(2,1)S(1)}, bf16[512,512]{1,0:T(8,128)(2,1)S(1)}, bf16[512,1024]{1,0:T(8,128)(2,1)S(1)}, bf16[512,1024]{1,0:T(8,128)(2,1)S(1)}) custom-call(s32[1]{0:T(128)} %bitcast.rank_ref, s32[1,256]{1,0:T(1,128)} %bitcast.6, s32[1,256]{1,0:T(1,128)} %bitcast.8, ...), custom_call_target="tpu_custom_call" | custom-call | tf_op jit(solution)/shard_map/pallas_call | solution.py:391
  3.8 4.1 %collective-permute-start.1 = (bf16[18,512]{1,0:T(8,128)(2,1)S(1)}, bf16[18,512]{1,0:T(8,128)(2,1)S(1)}, u32[]{:S(2)}, u32[]{:S(2)}) collective-permute-start(bf16[18,512]{1,0:T(8,128)(2,1)S(1)} %get-tuple-element.49.refs_0_), channel_id=1, source_target_pairs={{0,16},{1,17},{2,18},{3,19},{4,20},{5,21},{6,22},{7,23},{8,24},{9,... | collective-permute-start | bytes 55304 | tf_op jit(solution)/shard_map/ppermute | solution.py:383
  7.9 0.1 collective-permute-start
  8.0 0.9 %shard_map.69 = (s32[1,256]{1,0:T(1,128)S(1)}, f32[1,512]{1,0:T(1,128)S(1)}) custom-call(s32[1]{0:T(128)} %bitcast.rank_ref, s32[1,256]{1,0:T(1,128)S(1)} %bitcast.7, bf16[512,512]{1,0:T(8,128)(2,1)S(1)} %get-tuple-element.50.features_ref), custom_call_target="tpu_custom_call" | custom-call | flops 1000000000 | bytes 1000000 | tf_op jit(solution)/shard_map/pallas_call | solution.py:51
  8.9 0.8 collective-permute-done.1.refs_1_
  9.7 3.3 %collective-permute-done.refs_1_ = s16[18,1024]{1,0:T(8,128)(2,1)S(1)} collective-permute-done((s16[18,1024]{1,0:T(8,128)(2,1)S(1)}, s16[18,1024]{1,0:T(8,128)(2,1)S(1)}, u32[]{:S(2)}, u32[]{:S(2)}) %collective-permute-start) | collective-permute-done | bytes 36896 | tf_op jit(solution)/shard_map/ppermute | solution.py:383
  13.0 1.5 %collective-permute-start.4 = (s16[36,1024]{1,0:T(8,128)(2,1)S(1)}, s16[36,1024]{1,0:T(8,128)(2,1)S(1)}, u32[]{:S(2)}, u32[]{:S(2)}) collective-permute-start(s16[36,1024]{1,0:T(8,128)(2,1)S(1)} %shard_map.73.refs_0_), channel_id=1, source_target_pairs={{0,8},{1,9},{2,10},{3,11},{4,12},{5,13},{6,14},{7,15},{8,0},{9,1},... | collective-permute-start | bytes 221192 | tf_op jit(solution)/shard_map/ppermute | solution.py:383
  14.5 3.0 %collective-permute-done.4.refs_1_ = s16[36,1024]{1,0:T(8,128)(2,1)S(1)} collective-permute-done((s16[36,1024]{1,0:T(8,128)(2,1)S(1)}, s16[36,1024]{1,0:T(8,128)(2,1)S(1)}, u32[]{:S(2)}, u32[]{:S(2)}) %collective-permute-start.4) | collective-permute-done | bytes 73760 | tf_op jit(solution)/shard_map/ppermute | solution.py:383
  17.6 1.6 %collective-permute-start.5 = (s16[72,1024]{1,0:T(8,128)(2,1)S(1)}, s16[72,1024]{1,0:T(8,128)(2,1)S(1)}, u32[]{:S(2)}, u32[]{:S(2)}) collective-permute-start(s16[72,1024]{1,0:T(8,128)(2,1)S(1)} %shard_map.74.refs_0_), channel_id=1, source_target_pairs={{0,4},{1,5},{2,3},{3,2},{4,0},{5,1},{6,7},{7,6},{8,12},{9,13},{10,... | collective-permute-start | bytes 442376 | tf_op jit(solution)/shard_map/ppermute | solution.py:383
  19.1 1.5 %collective-permute-start.2 = (bf16[36,512]{1,0:T(8,128)(2,1)S(1)}, bf16[36,512]{1,0:T(8,128)(2,1)S(1)}, u32[]{:S(2)}, u32[]{:S(2)}) collective-permute-start(bf16[36,512]{1,0:T(8,128)(2,1)S(1)} %shard_map.70.refs_0_), channel_id=1, source_target_pairs={{0,8},{1,9},{2,10},{3,11},{4,12},{5,13},{6,14},{7,15},{8,0},{9,1},... | collective-permute-start | bytes 110600 | tf_op jit(solution)/shard_map/ppermute | solution.py:383
  20.6 2.5 %collective-permute-done.2.refs_1_ = bf16[36,512]{1,0:T(8,128)(2,1)S(1)} collective-permute-done((bf16[36,512]{1,0:T(8,128)(2,1)S(1)}, bf16[36,512]{1,0:T(8,128)(2,1)S(1)}, u32[]{:S(2)}, u32[]{:S(2)}) %collective-permute-start.2) | collective-permute-done | bytes 36896 | tf_op jit(solution)/shard_map/ppermute | solution.py:383
  23.2 0.6 collective-permute-start.3
  23.8 0.1 collective-permute-start.7
  23.9 1.6 %collective-permute-start.9 = (s16[144,1024]{1,0:T(8,128)(2,1)S(1)}, s16[144,1024]{1,0:T(8,128)(2,1)S(1)}, u32[]{:S(2)}, u32[]{:S(2)}) collective-permute-start(s16[144,1024]{1,0:T(8,128)(2,1)S(1)} %shard_map.75.a_h_ref), channel_id=1, source_target_pairs={{0,1},{1,0},{2,6},{3,7},{4,5},{5,4},{6,2},{7,3},{8,9},{9,8},{10,14... | collective-permute-start | bytes 884744 | tf_op jit(solution)/shard_map/ppermute | solution.py:383
  25.5 2.7 %collective-permute-done.3.refs_1_ = bf16[72,512]{1,0:T(8,128)(2,1)S(1)} collective-permute-done((bf16[72,512]{1,0:T(8,128)(2,1)S(1)}, bf16[72,512]{1,0:T(8,128)(2,1)S(1)}, u32[]{:S(2)}, u32[]{:S(2)}) %collective-permute-start.3) | collective-permute-done | bytes 73760 | tf_op jit(solution)/shard_map/ppermute | solution.py:383
  28.3 1.4 %collective-permute-done.6.c_x_ref = bf16[144,512]{1,0:T(8,128)(2,1)S(1)} collective-permute-done((bf16[144,512]{1,0:T(8,128)(2,1)S(1)}, bf16[144,512]{1,0:T(8,128)(2,1)S(1)}, u32[]{:S(2)}, u32[]{:S(2)}) %collective-permute-start.6) | collective-permute-done | bytes 147488 | tf_op jit(solution)/shard_map/ppermute | solution.py:383
  29.7 1.0 %shard_map.76 = (bf16[256,512]{1,0:T(8,128)(2,1)S(1)}, bf16[256,1024]{1,0:T(8,128)(2,1)S(1)}, bf16[256,1024]{1,0:T(8,128)(2,1)S(1)}) custom-call(s32[1,256]{1,0:T(1,128)S(1)} %get-tuple-element.53.source_ref, bf16[144,512]{1,0:T(8,128)(2,1)S(1)} %shard_map.72.a_x_ref, s16[144,1024]{1,0:T(8,128)(2,1)S(1)} %shard_map.75.a_h_ref, ...), custom_call_target="tpu_custom_call" | custom-call | flops 1000000000 | bytes 1000000 | tf_op jit(solution)/shard_map/pallas_call | solution.py:51
  30.7 0.2 collective-permute-start.11
  30.9 1.5 %collective-permute-start.8 = (bf16[144,512]{1,0:T(8,128)(2,1)S(1)}, bf16[144,512]{1,0:T(8,128)(2,1)S(1)}, u32[]{:S(2)}, u32[]{:S(2)}) collective-permute-start(bf16[144,512]{1,0:T(8,128)(2,1)S(1)} %shard_map.72.a_x_ref), channel_id=1, source_target_pairs={{0,1},{1,0},{2,6},{3,7},{4,5},{5,4},{6,2},{7,3},{8,9},{9,8},{10,14... | collective-permute-start | bytes 442376 | tf_op jit(solution)/shard_map/ppermute | solution.py:383
  32.4 0.5 shard_map.77
  33.0 3.1 %collective-permute-done.8.b_x_ref = bf16[144,512]{1,0:T(8,128)(2,1)S(1)} collective-permute-done((bf16[144,512]{1,0:T(8,128)(2,1)S(1)}, bf16[144,512]{1,0:T(8,128)(2,1)S(1)}, u32[]{:S(2)}, u32[]{:S(2)}) %collective-permute-start.8) | collective-permute-done | bytes 147488 | tf_op jit(solution)/shard_map/ppermute | solution.py:383
  36.1 1.4 %shard_map.78 = (bf16[256,1024]{1,0:T(8,128)(2,1)S(1)}, bf16[256,1024]{1,0:T(8,128)(2,1)S(1)}, f32[256,512]{1,0:T(8,128)S(1)}) custom-call(s32[1,256]{1,0:T(1,128)S(1)} %get-tuple-element.53.source_ref, s16[144,1024]{1,0:T(8,128)(2,1)S(1)} %collective-permute-done.11.h_ref, bf16[256,1024]{1,0:T(8,128)(2,1)S(1)} %get-tuple-element.65.coarse_in, ...), custom_call_target="tpu_custom_call" | custom-call | flops 1000000000 | bytes 1000000 | tf_op jit(solution)/shard_map/pallas_call | solution.py:51
  37.5 2.0 %shard_map.79 = (bf16[256,512]{1,0:T(8,128)(2,1)S(1)}, f32[256,512]{1,0:T(8,128)S(1)}, f32[4,32,1280]{2,1,0:T(8,128)S(1)}) custom-call(s32[1]{0:T(128)} %bitcast.rank_ref, s32[1,256]{1,0:T(1,128)S(1)} %get-tuple-element.53.source_ref, bf16[256,512]{1,0:T(8,128)(2,1)S(1)} %get-tuple-element.56.x_ref, bf16[144,512]{1,0:T(8,128)(2,1)S(1)} %collective-permute-done.8.b_x_ref, ...), custom_call_target="tpu_custom_call" | custom-call | flops 1000000000 | bytes 1000000 | tf_op jit(solution)/shard_map/pallas_call | solution.py:51
  39.5 0.6 collective-permute-start.12
  40.0 1.1 %shard_map.80 = f32[4,32,1280]{2,1,0:T(8,128)S(1)} custom-call(s32[1]{0:T(128)} %bitcast.rank_ref, f32[256,512]{1,0:T(8,128)S(1)} %get-tuple-element.73.residual_ref, bf16[512,1024]{1,0:T(8,128)(2,1)S(1)} %get-tuple-element.67.high_ref, bf16[512,1024]{1,0:T(8,128)(2,1)S(1)} %get-tuple-element.68.low_ref, f32[1,512]{1,0:T(1,128)S(1)} %bitcast.5), custom_call_target="tpu_custom_call" | custom-call | flops 1000000000 | bytes 1000000 | tf_op jit(solution)/shard_map/pallas_call | solution.py:51
  41.2 0.6 collective-permute-done.12
  41.8 0.1 add.22
  41.9 1.3 %collective-permute-start.15 = (f32[1,32,1280]{2,1,0:T(8,128)S(1)}, f32[1,32,1280]{2,1,0:T(8,128)S(1)}, u32[]{:S(2)}, u32[]{:S(2)}) collective-permute-start(f32[1,32,1280]{2,1,0:T(8,128)S(1)} %get-tuple-element.94), channel_id=1, source_target_pairs={{0,4},{1,5},{2,3},{3,2},{4,0},{5,1},{6,7},{7,6},{8,12},{9,13},{10,... | collective-permute-start | bytes 491528 | tf_op jit(solution)/shard_map/ppermute | solution.py:383
  43.2 1.5 %collective-permute-start.14 = (f32[1,32,1280]{2,1,0:T(8,128)S(1)}, f32[1,32,1280]{2,1,0:T(8,128)S(1)}, u32[]{:S(2)}, u32[]{:S(2)}) collective-permute-start(f32[1,32,1280]{2,1,0:T(8,128)S(1)} %get-tuple-element.95), channel_id=1, source_target_pairs={{0,1},{1,0},{2,6},{3,7},{4,5},{5,4},{6,2},{7,3},{8,9},{9,8},{10,14... | collective-permute-start | bytes 491528 | tf_op jit(solution)/shard_map/ppermute | solution.py:383
  44.8 0.7 collective-permute-start.13
  45.5 4.1 %shard_map.81.refs_0_ = f32[256,256]{1,0:T(8,128)S(1)} custom-call(bf16[256,512]{1,0:T(8,128)(2,1)S(1)} %get-tuple-element.79.refs_0_, bf16[256,1024]{1,0:T(8,128)(2,1)S(1)} %get-tuple-element.80.refs_1_, bf16[256,1024]{1,0:T(8,128)(2,1)S(1)} %get-tuple-element.81.refs_2_), custom_call_target="tpu_custom_call" | custom-call | flops 1000000000 | bytes 1000000 | tf_op jit(solution)/shard_map/pallas_call | solution.py:51
  49.5 3.6 %collective-permute-done.13 = f32[1,32,1280]{2,1,0:T(8,128)S(1)} collective-permute-done((f32[1,32,1280]{2,1,0:T(8,128)S(1)}, f32[1,32,1280]{2,1,0:T(8,128)S(1)}, u32[]{:S(2)}, u32[]{:S(2)}) %collective-permute-start.13) | collective-permute-done | bytes 163872 | tf_op jit(solution)/shard_map/ppermute | solution.py:383
  53.2 0.8 %collective-permute-start.16 = (f32[1,32,1280]{2,1,0:T(8,128)S(1)}, f32[1,32,1280]{2,1,0:T(8,128)S(1)}, u32[]{:S(2)}, u32[]{:S(2)}) collective-permute-start(f32[1,32,1280]{2,1,0:T(8,128)S(1)} %add_add_fusion), channel_id=1, source_target_pairs={{0,16},{1,17},{2,18},{3,19},{4,20},{5,21},{6,22},{7,23},{8,24},{9,... | collective-permute-start | bytes 491528 | tf_op jit(solution)/shard_map/ppermute | solution.py:383
  54.0 4.2 %shard_map.82.refs_0_ = f32[256,256]{1,0:T(8,128)S(1)} custom-call(f32[256,256]{1,0:T(8,128)S(1)} %shard_map.81.refs_0_), custom_call_target="tpu_custom_call" | custom-call | flops 1000000000 | bytes 1000000 | tf_op jit(solution)/shard_map/pallas_call | solution.py:51
  58.2 5.3 %collective-permute-done.16 = f32[1,32,1280]{2,1,0:T(8,128)S(1)} collective-permute-done((f32[1,32,1280]{2,1,0:T(8,128)S(1)}, f32[1,32,1280]{2,1,0:T(8,128)S(1)}, u32[]{:S(2)}, u32[]{:S(2)}) %collective-permute-start.16) | collective-permute-done | bytes 163872 | tf_op jit(solution)/shard_map/ppermute | solution.py:383
  63.6 4.2 %shard_map.83.inverse_ref.refs_8_ = f32[256,256]{1,0:T(8,128)S(1)} custom-call(f32[256,256]{1,0:T(8,128)S(1)} %shard_map.82.refs_0_), custom_call_target="tpu_custom_call" | custom-call | flops 1000000000 | bytes 1000000 | tf_op jit(solution)/shard_map/pallas_call | solution.py:51
  67.8 1.1 %collective-permute-done.17 = f32[1,32,1280]{2,1,0:T(8,128)S(1)} collective-permute-done((f32[1,32,1280]{2,1,0:T(8,128)S(1)}, f32[1,32,1280]{2,1,0:T(8,128)S(1)}, u32[]{:S(2)}, u32[]{:S(2)}) %collective-permute-start.17) | collective-permute-done | bytes 163872 | tf_op jit(solution)/shard_map/ppermute | solution.py:383
  68.9 2.1 %collective-permute-start.18 = (f32[1,32,1280]{2,1,0:T(8,128)S(1)}, f32[1,32,1280]{2,1,0:T(8,128)S(1)}, u32[]{:S(2)}, u32[]{:S(2)}) collective-permute-start(f32[1,32,1280]{2,1,0:T(8,128)S(1)} %add.27.refs_0_), channel_id=1, source_target_pairs={{0,5},{1,4},{2,7},{3,6},{4,1},{5,0},{6,3},{7,2},{8,13},{9,12},{10,... | collective-permute-start | bytes 491528 | tf_op jit(solution)/shard_map/ppermute | solution.py:383
  71.1 0.8 collective-permute-start.20
  71.8 0.7 collective-permute-start.19
  72.5 1.4 %shard_map.84 = f32[512,256]{1,0:T(8,128)} custom-call(f32[256,512]{1,0:T(8,128)S(1)} %get-tuple-element.73.residual_ref, f32[256,256]{1,0:T(8,128)S(1)} %shard_map.83.inverse_ref.refs_8_), custom_call_target="tpu_custom_call" | custom-call | flops 1000000000 | bytes 1000000 | tf_op jit(solution)/shard_map/pallas_call | solution.py:51
  73.9 3.0 %collective-permute-done.18.refs_3_ = f32[1,32,1280]{2,1,0:T(8,128)S(1)} collective-permute-done((f32[1,32,1280]{2,1,0:T(8,128)S(1)}, f32[1,32,1280]{2,1,0:T(8,128)S(1)}, u32[]{:S(2)}, u32[]{:S(2)}) %collective-permute-start.18) | collective-permute-done | bytes 163872 | tf_op jit(solution)/shard_map/ppermute | solution.py:383
  76.9 1.3 %collective-permute-done.20.refs_2_ = f32[1,32,1280]{2,1,0:T(8,128)S(1)} collective-permute-done((f32[1,32,1280]{2,1,0:T(8,128)S(1)}, f32[1,32,1280]{2,1,0:T(8,128)S(1)}, u32[]{:S(2)}, u32[]{:S(2)}) %collective-permute-start.20) | collective-permute-done | bytes 163872 | tf_op jit(solution)/shard_map/ppermute | solution.py:383
  78.2 0.5 collective-permute-start.22
  78.7 0.9 %collective-permute-done.23.refs_6_ = f32[1,32,1280]{2,1,0:T(8,128)S(1)} collective-permute-done((f32[1,32,1280]{2,1,0:T(8,128)S(1)}, f32[1,32,1280]{2,1,0:T(8,128)S(1)}, u32[]{:S(2)}, u32[]{:S(2)}) %collective-permute-start.23) | collective-permute-done | bytes 163872 | tf_op jit(solution)/shard_map/ppermute | solution.py:383
  79.6 0.2 collective-permute-done.22.refs_5_
  79.8 0.3 collective-permute-done.24.refs_7_
  80.1 2.8 %shard_map.85 = f32[256,1280]{1,0:T(8,128)} custom-call(s32[1]{0:T(128)} %bitcast.rank_ref, f32[1,32,1280]{2,1,0:T(8,128)S(1)} %add.27.refs_0_, f32[1,32,1280]{2,1,0:T(8,128)S(1)} %collective-permute-done.19.refs_1_, f32[1,32,1280]{2,1,0:T(8,128)S(1)} %collective-permute-done.20.refs_2_, f32[1,32,1280]{2,1,0:T(8,128)S(1)} %collective-permute-done.18.refs_3_, ...), custom_call_target="tpu_custom_call" | custom-call | tf_op jit(solution)/shard_map/pallas_call | solution.py:494
  (29 shorter events, 0.4 us)
Async XLA Ops:
  0.6 7.4 %copy-start.1 = (s32[256]{0:T(256)S(1)}, s32[256]{0:T(256)}, u32[]{:S(2)}) copy-start(s32[256]{0:T(256)} %param.8) | copy-start | bytes 3076
  3.8 5.9 %collective-permute-start.1 = (bf16[18,512]{1,0:T(8,128)(2,1)S(1)}, bf16[18,512]{1,0:T(8,128)(2,1)S(1)}, u32[]{:S(2)}, u32[]{:S(2)}) collective-permute-start(bf16[18,512]{1,0:T(8,128)(2,1)S(1)} %get-tuple-element.49.refs_0_), channel_id=1, source_target_pairs={{0,16},{1,17},{2,18},{3,19},{4,20},{5,21},{6,22},{7,23},{8,24},{9,... | collective-permute-start | bytes 55304 | tf_op jit(solution)/shard_map/ppermute | solution.py:383
  7.9 5.1 %collective-permute-start = (s16[18,1024]{1,0:T(8,128)(2,1)S(1)}, s16[18,1024]{1,0:T(8,128)(2,1)S(1)}, u32[]{:S(2)}, u32[]{:S(2)}) collective-permute-start(s16[18,1024]{1,0:T(8,128)(2,1)S(1)} %get-tuple-element.48.refs_0_), channel_id=1, source_target_pairs={{0,16},{1,17},{2,18},{3,19},{4,20},{5,21},{6,22},{7,23},{8,24},{9,... | collective-permute-start | bytes 110600 | tf_op jit(solution)/shard_map/ppermute | solution.py:383
  13.0 4.5 %collective-permute-start.4 = (s16[36,1024]{1,0:T(8,128)(2,1)S(1)}, s16[36,1024]{1,0:T(8,128)(2,1)S(1)}, u32[]{:S(2)}, u32[]{:S(2)}) collective-permute-start(s16[36,1024]{1,0:T(8,128)(2,1)S(1)} %shard_map.73.refs_0_), channel_id=1, source_target_pairs={{0,8},{1,9},{2,10},{3,11},{4,12},{5,13},{6,14},{7,15},{8,0},{9,1},... | collective-permute-start | bytes 221192 | tf_op jit(solution)/shard_map/ppermute | solution.py:383
  17.6 6.2 %collective-permute-start.5 = (s16[72,1024]{1,0:T(8,128)(2,1)S(1)}, s16[72,1024]{1,0:T(8,128)(2,1)S(1)}, u32[]{:S(2)}, u32[]{:S(2)}) collective-permute-start(s16[72,1024]{1,0:T(8,128)(2,1)S(1)} %shard_map.74.refs_0_), channel_id=1, source_target_pairs={{0,4},{1,5},{2,3},{3,2},{4,0},{5,1},{6,7},{7,6},{8,12},{9,13},{10,... | collective-permute-start | bytes 442376 | tf_op jit(solution)/shard_map/ppermute | solution.py:383
  19.1 4.1 %collective-permute-start.2 = (bf16[36,512]{1,0:T(8,128)(2,1)S(1)}, bf16[36,512]{1,0:T(8,128)(2,1)S(1)}, u32[]{:S(2)}, u32[]{:S(2)}) collective-permute-start(bf16[36,512]{1,0:T(8,128)(2,1)S(1)} %shard_map.70.refs_0_), channel_id=1, source_target_pairs={{0,8},{1,9},{2,10},{3,11},{4,12},{5,13},{6,14},{7,15},{8,0},{9,1},... | collective-permute-start | bytes 110600 | tf_op jit(solution)/shard_map/ppermute | solution.py:383
  23.2 5.0 %collective-permute-start.3 = (bf16[72,512]{1,0:T(8,128)(2,1)S(1)}, bf16[72,512]{1,0:T(8,128)(2,1)S(1)}, u32[]{:S(2)}, u32[]{:S(2)}) collective-permute-start(bf16[72,512]{1,0:T(8,128)(2,1)S(1)} %shard_map.71.refs_0_), channel_id=1, source_target_pairs={{0,4},{1,5},{2,3},{3,2},{4,0},{5,1},{6,7},{7,6},{8,12},{9,13},{10,... | collective-permute-start | bytes 221192 | tf_op jit(solution)/shard_map/ppermute | solution.py:383
  23.8 5.9 %collective-permute-start.7 = (s16[144,1024]{1,0:T(8,128)(2,1)S(1)}, s16[144,1024]{1,0:T(8,128)(2,1)S(1)}, u32[]{:S(2)}, u32[]{:S(2)}) collective-permute-start(s16[144,1024]{1,0:T(8,128)(2,1)S(1)} %shard_map.75.a_h_ref), channel_id=1, source_target_pairs={{0,2},{1,3},{2,0},{3,1},{4,6},{5,7},{6,4},{7,5},{8,10},{9,11},{10,... | collective-permute-start | bytes 884744 | tf_op jit(solution)/shard_map/ppermute | solution.py:383
  23.9 6.8 %collective-permute-start.9 = (s16[144,1024]{1,0:T(8,128)(2,1)S(1)}, s16[144,1024]{1,0:T(8,128)(2,1)S(1)}, u32[]{:S(2)}, u32[]{:S(2)}) collective-permute-start(s16[144,1024]{1,0:T(8,128)(2,1)S(1)} %shard_map.75.a_h_ref), channel_id=1, source_target_pairs={{0,1},{1,0},{2,6},{3,7},{4,5},{5,4},{6,2},{7,3},{8,9},{9,8},{10,14... | collective-permute-start | bytes 884744 | tf_op jit(solution)/shard_map/ppermute | solution.py:383
  28.3 1.4 %collective-permute-start.6 = (bf16[144,512]{1,0:T(8,128)(2,1)S(1)}, bf16[144,512]{1,0:T(8,128)(2,1)S(1)}, u32[]{:S(2)}, u32[]{:S(2)}) collective-permute-start(bf16[144,512]{1,0:T(8,128)(2,1)S(1)} %shard_map.72.a_x_ref), channel_id=1, source_target_pairs={{0,2},{1,3},{2,0},{3,1},{4,6},{5,7},{6,4},{7,5},{8,10},{9,11},{10,... | collective-permute-start | bytes 442376 | tf_op jit(solution)/shard_map/ppermute | solution.py:383
  30.7 5.3 %collective-permute-start.11 = (s16[144,1024]{1,0:T(8,128)(2,1)S(1)}, s16[144,1024]{1,0:T(8,128)(2,1)S(1)}, u32[]{:S(2)}, u32[]{:S(2)}) collective-permute-start(s16[144,1024]{1,0:T(8,128)(2,1)S(1)} %collective-permute-done.9.h_ref), channel_id=1, source_target_pairs={{0,2},{1,3},{2,0},{3,1},{4,6},{5,7},{6,4},{7,5},{8,10},{9,11},{10,... | collective-permute-start | bytes 884744 | tf_op jit(solution)/shard_map/ppermute | solution.py:383
  30.9 5.1 %collective-permute-start.8 = (bf16[144,512]{1,0:T(8,128)(2,1)S(1)}, bf16[144,512]{1,0:T(8,128)(2,1)S(1)}, u32[]{:S(2)}, u32[]{:S(2)}) collective-permute-start(bf16[144,512]{1,0:T(8,128)(2,1)S(1)} %shard_map.72.a_x_ref), channel_id=1, source_target_pairs={{0,1},{1,0},{2,6},{3,7},{4,5},{5,4},{6,2},{7,3},{8,9},{9,8},{10,14... | collective-permute-start | bytes 442376 | tf_op jit(solution)/shard_map/ppermute | solution.py:383
  33.0 4.5 %copy-start = (f32[512]{0:T(512)S(1)}, f32[512]{0:T(512)}, u32[]{:S(2)}) copy-start(f32[512]{0:T(512)} %param.7) | copy-start | bytes 6148
  36.1 1.4 %collective-permute-start.10 = (bf16[144,512]{1,0:T(8,128)(2,1)S(1)}, bf16[144,512]{1,0:T(8,128)(2,1)S(1)}, u32[]{:S(2)}, u32[]{:S(2)}) collective-permute-start(bf16[144,512]{1,0:T(8,128)(2,1)S(1)} %collective-permute-done.8.b_x_ref), channel_id=1, source_target_pairs={{0,2},{1,3},{2,0},{3,1},{4,6},{5,7},{6,4},{7,5},{8,10},{9,11},{10,... | collective-permute-start | bytes 442376 | tf_op jit(solution)/shard_map/ppermute | solution.py:383
  39.5 2.3 %collective-permute-start.12 = (f32[4,32,1280]{2,1,0:T(8,128)S(1)}, f32[4,32,1280]{2,1,0:T(8,128)S(1)}, u32[]{:S(2)}, u32[]{:S(2)}) collective-permute-start(f32[4,32,1280]{2,1,0:T(8,128)S(1)} %get-tuple-element.74), channel_id=1, source_target_pairs={{0,2},{1,3},{2,0},{3,1},{4,6},{5,7},{6,4},{7,5},{8,10},{9,11},{10,... | collective-permute-start | bytes 1966088 | tf_op jit(solution)/shard_map/ppermute | solution.py:383
  41.9 7.6 %collective-permute-start.15 = (f32[1,32,1280]{2,1,0:T(8,128)S(1)}, f32[1,32,1280]{2,1,0:T(8,128)S(1)}, u32[]{:S(2)}, u32[]{:S(2)}) collective-permute-start(f32[1,32,1280]{2,1,0:T(8,128)S(1)} %get-tuple-element.94), channel_id=1, source_target_pairs={{0,4},{1,5},{2,3},{3,2},{4,0},{5,1},{6,7},{7,6},{8,12},{9,13},{10,... | collective-permute-start | bytes 491528 | tf_op jit(solution)/shard_map/ppermute | solution.py:383
  43.2 6.3 %collective-permute-start.14 = (f32[1,32,1280]{2,1,0:T(8,128)S(1)}, f32[1,32,1280]{2,1,0:T(8,128)S(1)}, u32[]{:S(2)}, u32[]{:S(2)}) collective-permute-start(f32[1,32,1280]{2,1,0:T(8,128)S(1)} %get-tuple-element.95), channel_id=1, source_target_pairs={{0,1},{1,0},{2,6},{3,7},{4,5},{5,4},{6,2},{7,3},{8,9},{9,8},{10,14... | collective-permute-start | bytes 491528 | tf_op jit(solution)/shard_map/ppermute | solution.py:383
  44.8 8.4 %collective-permute-start.13 = (f32[1,32,1280]{2,1,0:T(8,128)S(1)}, f32[1,32,1280]{2,1,0:T(8,128)S(1)}, u32[]{:S(2)}, u32[]{:S(2)}) collective-permute-start(f32[1,32,1280]{2,1,0:T(8,128)S(1)} %get-tuple-element.96), channel_id=1, source_target_pairs={{0,5},{1,4},{2,7},{3,6},{4,1},{5,0},{6,3},{7,2},{8,13},{9,12},{10,... | collective-permute-start | bytes 491528 | tf_op jit(solution)/shard_map/ppermute | solution.py:383
  53.2 10.3 %collective-permute-start.16 = (f32[1,32,1280]{2,1,0:T(8,128)S(1)}, f32[1,32,1280]{2,1,0:T(8,128)S(1)}, u32[]{:S(2)}, u32[]{:S(2)}) collective-permute-start(f32[1,32,1280]{2,1,0:T(8,128)S(1)} %add_add_fusion), channel_id=1, source_target_pairs={{0,16},{1,17},{2,18},{3,19},{4,20},{5,21},{6,22},{7,23},{8,24},{9,... | collective-permute-start | bytes 491528 | tf_op jit(solution)/shard_map/ppermute | solution.py:383
  63.5 5.4 %collective-permute-start.17 = (f32[1,32,1280]{2,1,0:T(8,128)S(1)}, f32[1,32,1280]{2,1,0:T(8,128)S(1)}, u32[]{:S(2)}, u32[]{:S(2)}) collective-permute-start(f32[1,32,1280]{2,1,0:T(8,128)S(1)} %add.26), channel_id=1, source_target_pairs={{0,8},{1,9},{2,10},{3,11},{4,12},{5,13},{6,14},{7,15},{8,0},{9,1},... | collective-permute-start | bytes 491528 | tf_op jit(solution)/shard_map/ppermute | solution.py:383
  68.9 8.0 %collective-permute-start.18 = (f32[1,32,1280]{2,1,0:T(8,128)S(1)}, f32[1,32,1280]{2,1,0:T(8,128)S(1)}, u32[]{:S(2)}, u32[]{:S(2)}) collective-permute-start(f32[1,32,1280]{2,1,0:T(8,128)S(1)} %add.27.refs_0_), channel_id=1, source_target_pairs={{0,5},{1,4},{2,7},{3,6},{4,1},{5,0},{6,3},{7,2},{8,13},{9,12},{10,... | collective-permute-start | bytes 491528 | tf_op jit(solution)/shard_map/ppermute | solution.py:383
  71.1 7.1 %collective-permute-start.20 = (f32[1,32,1280]{2,1,0:T(8,128)S(1)}, f32[1,32,1280]{2,1,0:T(8,128)S(1)}, u32[]{:S(2)}, u32[]{:S(2)}) collective-permute-start(f32[1,32,1280]{2,1,0:T(8,128)S(1)} %add.27.refs_0_), channel_id=1, source_target_pairs={{0,4},{1,5},{2,3},{3,2},{4,0},{5,1},{6,7},{7,6},{8,12},{9,13},{10,... | collective-permute-start | bytes 491528 | tf_op jit(solution)/shard_map/ppermute | solution.py:383
  71.8 6.4 %collective-permute-start.19 = (f32[1,32,1280]{2,1,0:T(8,128)S(1)}, f32[1,32,1280]{2,1,0:T(8,128)S(1)}, u32[]{:S(2)}, u32[]{:S(2)}) collective-permute-start(f32[1,32,1280]{2,1,0:T(8,128)S(1)} %add.27.refs_0_), channel_id=1, source_target_pairs={{0,1},{1,0},{2,6},{3,7},{4,5},{5,4},{6,2},{7,3},{8,9},{9,8},{10,14... | collective-permute-start | bytes 491528 | tf_op jit(solution)/shard_map/ppermute | solution.py:383
  72.5 6.2 %collective-permute-start.21 = (f32[1,32,1280]{2,1,0:T(8,128)S(1)}, f32[1,32,1280]{2,1,0:T(8,128)S(1)}, u32[]{:S(2)}, u32[]{:S(2)}) collective-permute-start(f32[1,32,1280]{2,1,0:T(8,128)S(1)} %add.27.refs_0_), channel_id=1, source_target_pairs={{0,2},{1,3},{2,0},{3,1},{4,6},{5,7},{6,4},{7,5},{8,10},{9,11},{10,... | collective-permute-start | bytes 491528 | tf_op jit(solution)/shard_map/ppermute | solution.py:383
  78.2 1.4 %collective-permute-start.23 = (f32[1,32,1280]{2,1,0:T(8,128)S(1)}, f32[1,32,1280]{2,1,0:T(8,128)S(1)}, u32[]{:S(2)}, u32[]{:S(2)}) collective-permute-start(f32[1,32,1280]{2,1,0:T(8,128)S(1)} %collective-permute-done.20.refs_2_), channel_id=1, source_target_pairs={{0,2},{1,3},{2,0},{3,1},{4,6},{5,7},{6,4},{7,5},{8,10},{9,11},{10,... | collective-permute-start | bytes 491528 | tf_op jit(solution)/shard_map/ppermute | solution.py:383
  78.2 1.6 %collective-permute-start.22 = (f32[1,32,1280]{2,1,0:T(8,128)S(1)}, f32[1,32,1280]{2,1,0:T(8,128)S(1)}, u32[]{:S(2)}, u32[]{:S(2)}) collective-permute-start(f32[1,32,1280]{2,1,0:T(8,128)S(1)} %collective-permute-done.19.refs_1_), channel_id=1, source_target_pairs={{0,2},{1,3},{2,0},{3,1},{4,6},{5,7},{6,4},{7,5},{8,10},{9,11},{10,... | collective-permute-start | bytes 491528 | tf_op jit(solution)/shard_map/ppermute | solution.py:383
  78.7 1.4 %collective-permute-start.24 = (f32[1,32,1280]{2,1,0:T(8,128)S(1)}, f32[1,32,1280]{2,1,0:T(8,128)S(1)}, u32[]{:S(2)}, u32[]{:S(2)}) collective-permute-start(f32[1,32,1280]{2,1,0:T(8,128)S(1)} %collective-permute-done.18.refs_3_), channel_id=1, source_target_pairs={{0,2},{1,3},{2,0},{3,1},{4,6},{5,7},{6,4},{7,5},{8,10},{9,11},{10,... | collective-permute-start | bytes 491528 | tf_op jit(solution)/shard_map/ppermute | solution.py:383
where the time goes:
time: 83.2 us; the launch traced here: 83 us
  waiting for transfers between devices  33.1 us (40%)
  Pallas kernels  26.7 us (32%)
  starting transfers between devices  22 us (26%)
  between operations  1.01 us (1%)
    ppermute x25, waiting for transfers between devices, move(): return lax.ppermute(value, axes, perm)  33.1 us
    ppermute x25, starting transfers between devices, move(): return lax.ppermute(value, axes, perm)  22 us
    pallas_call x16, Pallas kernels, call(): pl.pallas_call(kernel, out_shape=outs, in_specs=specs, out_specs=jax.tree...  20.8 us
    pallas_call x1, Pallas kernels, body(): pl.pallas_call(pick_kernel(chunks), out_shape=(pltpu.VMEM((slots, width),...  3.12 us
    pallas_call x1, Pallas kernels, body(): pl.pallas_call(partial(rows_kernel, masks), out_shape=jax.ShapeDtypeStruc...  2.77 us
  transfers between devices with their start and end apart: 25, of which 16 were waited for; matrix products, arithmetic and copies ran while one was open for 0% of the time, Pallas kernels for 23%

commit v1 on v0

--- a/solution.py
+++ b/solution.py
@@ -67,65 +67,65 @@
     return lax.broadcasted_iota(i32, shape, axis)
 
 
-def pick_kernel(chunks):
+def pick_kernel(
+    rank_ref, owner_ref, position_ref, features_ref, factor_ref,
+    slots_x_ref, slots_h_ref, kept_ref, factor_in,
+    owner_in, position_in, owner_list, position_list, found, rows_in, sems,
+):
+    slots = slots_x_ref.shape[0]
+    pivots = owner_ref.shape[1]
+    rows = features_ref.shape[0]
+    half = rows // 2
+    pairs = [
+        (owner_ref, owner_list),
+        (position_ref, position_list),
+        (owner_ref, owner_in),
+        (position_ref, position_in),
+        (features_ref, kept_ref),
+        (factor_ref.at[pl.ds(0, half), :], factor_in.at[pl.ds(0, half), :]),
+        (factor_ref.at[pl.ds(half, half), :], factor_in.at[pl.ds(half, half), :]),
+    ]
+    copies = [
+        pltpu.make_async_copy(source, target, sems.at[k]) for k, (source, target) in enumerate(pairs)
+    ]
+    for copy in copies:
+        copy.start()
+    rank = rank_ref[0]
+    for k in range(slots + 1):
+        found[k] = 0
+    copies[0].wait()
+    copies[1].wait()
+
+    def collect(k, count):
+        for p in range(8):
+            at = k * 8 + p
+            found[count] = position_list[0, at]
+            count = jnp.minimum(count + (owner_list[0, at] == rank).astype(i32), slots)
+        return count
+
+    lax.fori_loop(0, pivots // 8, collect, jnp.int32(0))
+    ahead = onehot(iota((pivots, pivots), 0) < iota((pivots, pivots), 1))
+    copies[2].wait()
+    mine = owner_in[...] == rank
+    mine_rows = jnp.broadcast_to(jnp.where(mine, 1.0, 0.0), (8, pivots)).astype(bf16)
+    order = nn(mine_rows, ahead)[0:1, :].astype(i32)
+    chosen = onehot((iota((slots, pivots), 0) == order) & mine)
+    copies[3].wait()
+    located = onehot(iota((rows, pivots), 0) == position_in[...])
+    take = nt(chosen, located).astype(bf16)
+    copies[4].wait()
+    slots_x_ref[...] = nn(take, kept_ref[...]).astype(bf16)
+    copies[5].wait()
+    copies[6].wait()
+    for k in range(slots):
+        rows_in[k : k + 1, :] = factor_in[pl.ds(found[k], 1), :]
+    slots_h_ref[...] = jnp.round(rows_in[...] * STEPS).astype(i32).astype(jnp.int16)
+
+
+def prepare_kernel(core, side, col_low, others, slots, devices):
     def kernel(
-        rank_ref, owner_ref, position_ref, features_ref, factor_ref,
-        slots_x_ref, slots_h_ref, kept_ref, high_ref, low_ref,
-        owner_in, position_in, factor_in, slots_sum, small_sems, factor_sems,
+        rank_ref, owner_ref, features_ref, factor_ref, source_ref, norm_ref, high_ref, low_ref
     ):
-        slots = slots_x_ref.shape[0]
-        pivots = owner_ref.shape[1]
-        rows, _ = features_ref.shape
-        size = rows // chunks
-        small = [
-            pltpu.make_async_copy(source, target, small_sems.at[k])
-            for k, (source, target) in enumerate(
-                ((owner_ref, owner_in), (position_ref, position_in), (features_ref, kept_ref))
-            )
-        ]
-        large = [
-            pltpu.make_async_copy(
-                factor_ref.at[pl.ds(k * size, size), :],
-                factor_in.at[pl.ds(k * size, size), :],
-                factor_sems.at[k],
-            )
-            for k in range(chunks)
-        ]
-        for copy in small + large:
-            copy.start()
-        ahead = onehot(iota((pivots, pivots), 0) < iota((pivots, pivots), 1))
-        small[0].wait()
-        mine = owner_in[...] == rank_ref[0]
-        mine_rows = jnp.broadcast_to(jnp.where(mine, 1.0, 0.0), (8, pivots)).astype(bf16)
-        order = nn(mine_rows, ahead)[0:1, :].astype(i32)
-        chosen = onehot((iota((slots, pivots), 0) == order) & mine)
-        small[1].wait()
-        located = onehot(iota((rows, pivots), 0) == position_in[...])
-        take = nt(chosen, located).astype(bf16)
-        small[2].wait()
-        slots_x_ref[...] = nn(take, kept_ref[...]).astype(bf16)
-        for k in range(chunks):
-            large[k].wait()
-            part = slice(k * size, (k + 1) * size)
-            exact = factor_in[part, :]
-            high, low = split(exact)
-            high_ref[part, :] = high
-            low_ref[part, :] = low
-            rest = (exact - high.astype(f32) - low.astype(f32)).astype(bf16)
-            chosen_rows = take[:, part]
-            got = nn(chosen_rows, high) + (nn(chosen_rows, low) + nn(chosen_rows, rest))
-            if k:
-                got = slots_sum[...] + got
-            if k < chunks - 1:
-                slots_sum[...] = got
-            else:
-                slots_h_ref[...] = jnp.round(got * STEPS).astype(i32).astype(jnp.int16)
-
-    return kernel
-
-
-def prepare_kernel(core, side, col_low, others, slots, devices):
-    def kernel(rank_ref, owner_ref, features_ref, source_ref, norm_ref):
         pivots = owner_ref.shape[1]
         owner = owner_ref[...]
         ahead = onehot(iota((pivots, pivots), 0) < iota((pivots, pivots), 1))
@@ -143,6 +143,9 @@
         trail = jnp.where(low_core, bit(col_low), bit(side))
         place = place + (lead << at) + (trail << (at + 1)) + (bit(core) << (at + 2))
         source_ref[...] = place * slots + slot_rank
+        high, low = split(factor_ref[...])
+        high_ref[...] = high
+        low_ref[...] = low
         wide = features_ref[...].astype(f32)
         norm_ref[...] = nt(jnp.ones((8, wide.shape[1]), f32), wide * wide, HIGHEST)[0:1, :]
 
@@ -174,15 +177,22 @@
     count, piece, _ = out_ref.shape
     size = count * piece
     depth = high.shape[1]
-    rows = residual_ref[pl.ds(pl.multiple_of(half * size, size), size), :]
-    weighted = rows * weights
+    n = residual_ref.shape[0]
+    upper = residual_ref[pl.ds(pl.multiple_of(half * size, size), size), :]
+    lower = residual_ref[pl.ds(pl.multiple_of(n // 2 + half * size, size), size), :]
+    weighted = jnp.concatenate([upper, lower], axis=0) * weights
     weighted_hi, weighted_lo = split(weighted)
     left = nn(weighted_hi, high) + (nn(weighted_lo, high) + nn(weighted_hi, low))
-    right = nt(weighted, residual_ref[...], HIGHEST)
+    residual = residual_ref[...]
+    top = nt(weighted[0:size], residual, HIGHEST)
+    bottom = nt(weighted[size:], residual[n // 2 :], HIGHEST)
     for p in range(count):
         spot = (order & (count - 1)) ^ p
-        out_ref[spot, :, 0:depth] = left[p * piece : (p + 1) * piece, :]
-        out_ref[spot, :, depth:] = right[p * piece : (p + 1) * piece, :]
+        rows = slice(p * piece, (p + 1) * piece)
+        out_ref[spot, :, 0:depth] = left[rows]
+        out_ref[spot, :, depth : 2 * depth] = left[size + p * piece : size + (p + 1) * piece]
+        out_ref[spot, :, 2 * depth : 2 * depth + n] = top[rows]
+        out_ref[spot, :, 2 * depth + n :] = bottom[rows]
 
 
 def chosen_rows(source, start, held):
@@ -214,22 +224,15 @@
     fine_ref[...] = (one[1] + two[1]).astype(bf16)
 
 
-def across_kernel(source_ref, h_ref, coarse_in, fine_in, coarse_ref, fine_ref):
-    coarse, fine = ordered_h(source_ref[...], h_ref.shape[0], h_ref)
+def across_kernel(place, source_ref, h_ref, coarse_in, fine_in, coarse_ref, fine_ref):
+    coarse, fine = ordered_h(source_ref[...], place * h_ref.shape[0], h_ref)
     coarse_ref[...] = (coarse_in[...].astype(f32) + coarse).astype(bf16)
     fine_ref[...] = (fine_in[...].astype(f32) + fine).astype(bf16)
 
 
-def product_kernel(
-    source_ref, h_ref, coarse_in, fine_in, high_ref, low_ref, coarse_ref, fine_ref, product_ref
-):
-    coarse, fine = ordered_h(source_ref[...], 3 * h_ref.shape[0], h_ref)
-    coarse = (coarse_in[...].astype(f32) + coarse).astype(bf16)
-    fine = (fine_in[...].astype(f32) + fine).astype(bf16)
-    coarse_ref[...] = coarse
-    fine_ref[...] = fine
-    high = high_ref[...]
-    product_ref[...] = nt(coarse, high) + (nt(fine, high) + nt(coarse, low_ref[...]))
+def product_kernel(coarse_ref, fine_ref, high_ref, low_ref, product_ref):
+    coarse, high = coarse_ref[...], high_ref[...]
+    product_ref[...] = nt(coarse, high) + (nt(fine_ref[...], high) + nt(coarse, low_ref[...]))
 
 
 def residual_kernel(
@@ -328,22 +331,39 @@
     n = inverse_ref.shape[0]
     total = done_ref.shape[1]
     depth = total - n
+    middle = n // 2
     core, near_order, far_order = spots(rank_ref[0], *masks)
     for k, part in enumerate(parts):
         mine = k < count
         half = core if mine else 1 - core
         at = half * count + ((near_order if mine else far_order) ^ (k % count))
-        work_ref[pl.ds(pl.multiple_of(at * piece, piece), piece), :] = part[0]
+        upper = pl.ds(pl.multiple_of(at * piece, piece), piece)
+        lower = pl.ds(pl.multiple_of(middle + at * piece, piece), piece)
+        work_ref[upper, 0:depth] = part[0, :, 0:depth]
+        work_ref[lower, 0:depth] = part[0, :, depth : 2 * depth]
+        work_ref[upper, depth:] = part[0, :, 2 * depth : 2 * depth + n]
+        work_ref[lower, depth + middle :] = part[0, :, 2 * depth + n :]
     inverse = inverse_ref[...]
+    corner = work_ref[0:middle, depth + middle :]
+    first = nn(inverse[:, 0:middle], work_ref[0:middle, depth : depth + middle], HIGHEST) + nt(
+        inverse[:, middle:], corner, HIGHEST
+    )
+    second = nn(inverse, work_ref[:, depth + middle :], HIGHEST)
+    done_ref[:, depth:] = nt(jnp.concatenate([first, second], axis=1), inverse, HIGHEST)
     copies = []
-    for k, at in enumerate([depth] + list(range(0, depth, depth // 2))):
-        here = slice(at, total if at == depth else at + depth // 2)
-        done = nn(inverse, work_ref[:, here], HIGHEST)
-        if at == depth:
-            done = nt(done, inverse, HIGHEST)
-        done_ref[:, here] = done
-        copies.append(pltpu.make_async_copy(done_ref.at[:, here], out_ref.at[:, here], sems.at[k]))
-        copies[-1].start()
+
+    def send(here):
+        copy = pltpu.make_async_copy(
+            done_ref.at[:, here], out_ref.at[:, here], sems.at[len(copies)]
+        )
+        copies.append(copy)
+        copy.start()
+
+    send(slice(depth, total))
+    for at in range(0, depth, depth // 4):
+        here = slice(at, at + depth // 4)
+        done_ref[:, here] = nn(inverse, work_ref[:, here], HIGHEST)
+        send(here)
     for copy in copies:
         copy.wait()
 
@@ -386,26 +406,26 @@
         return lax.optimization_barrier(values)
 
     owner_row = pivot_owner[None, :]
-    chunks = 4
     far = lambda x: pltpu.with_memory_space_constraint(x, pltpu.HBM)
-    held_x, held_h, kept, high, low = pl.pallas_call(
-        pick_kernel(chunks),
+    listed = (1, pivots)
+    held_x, held_h, kept, factor_near = pl.pallas_call(
+        pick_kernel,
         out_shape=(
             pltpu.VMEM((slots, width), bf16),
             pltpu.VMEM((slots, depth), jnp.int16),
             pltpu.VMEM((rows, width), bf16),
-            pltpu.VMEM((rows, depth), bf16),
-            pltpu.VMEM((rows, depth), bf16),
+            pltpu.VMEM((rows, depth), f32),
         ),
         in_specs=[pl.BlockSpec(memory_space=pltpu.SMEM)] + [pl.BlockSpec(memory_space=pltpu.HBM)] * 4,
-        out_specs=tuple(pl.BlockSpec(memory_space=pltpu.VMEM) for _ in range(5)),
+        out_specs=tuple(pl.BlockSpec(memory_space=pltpu.VMEM) for _ in range(4)),
         scratch_shapes=[
-            pltpu.VMEM((1, pivots), i32),
-            pltpu.VMEM((1, pivots), i32),
-            pltpu.VMEM((rows, depth), f32),
+            pltpu.VMEM(listed, i32),
+            pltpu.VMEM(listed, i32),
+            pltpu.SMEM(listed, i32),
+            pltpu.SMEM(listed, i32),
+            pltpu.SMEM((slots + 1,), i32),
             pltpu.VMEM((slots, depth), f32),
-            pltpu.SemaphoreType.DMA((3,)),
-            pltpu.SemaphoreType.DMA((chunks,)),
+            pltpu.SemaphoreType.DMA((7,)),
         ],
         compiler_params=pltpu.CompilerParams(vmem_limit_bytes=24 << 20),
     )(rank, far(owner_row), far(pivot_position[None, :]), far(features), far(factor))
@@ -420,12 +440,17 @@
         got_h = near(move(held_h, perm))
         got_x = near(move(held_x, perm))
         if not prepared:
-            source, norm = call(
+            source, norm, high, low = call(
                 prepare_kernel(core, side, col_low, others, slots, devices),
-                (pltpu.VMEM((1, pivots), i32), pltpu.VMEM((1, rows), f32)),
-                rank, owner_row, kept, smem=1,
+                (
+                    pltpu.VMEM((1, pivots), i32),
+                    pltpu.VMEM((1, rows), f32),
+                    pltpu.VMEM((rows, depth), bf16),
+                    pltpu.VMEM((rows, depth), bf16),
+                ),
+                rank, owner_row, kept, factor_near, smem=1,
             )
-            got_h, got_x, source, norm = tie(got_h, got_x, source, norm)
+            got_h, got_x, source, norm, high, low = tie(got_h, got_x, source, norm, high, low)
             prepared = True
         held_h = joined(held_h, got_h)
         held_x = joined(held_x, got_x)
@@ -440,18 +465,15 @@
     )
     across_h, coarse, fine = tie(across_h, coarse, fine)
     beyond_h = near(move(across_h, core_pair))
-    coarse, fine = call(across_kernel, (plane, plane), source, across_h, coarse, fine)
+    coarse, fine = call(partial(across_kernel, 1), (plane, plane), source, across_h, coarse, fine)
+    coarse, fine = call(partial(across_kernel, 3), (plane, plane), source, beyond_h, coarse, fine)
     across_x, coarse, fine = tie(across_x, coarse, fine)
     beyond_x = near(move(across_x, core_pair))
-    coarse, fine, product = call(
-        product_kernel,
-        (plane, plane, pltpu.VMEM((pivots, rows), f32)),
-        source, beyond_h, coarse, fine, high, low,
-    )
+    product = call(product_kernel, pltpu.VMEM((pivots, rows), f32), coarse, fine, high, low)
     beyond_x, product = tie(beyond_x, product)
 
     weights = ip_weights[None, :]
-    half = pltpu.VMEM((4, pivots // 8, total), f32)
+    half = pltpu.VMEM((4, pivots // 16, 2 * depth + pivots + pivots // 2), f32)
     pivot_x, residual, send = call(
         partial(residual_kernel, masks, samples),
         (pltpu.VMEM((pivots, width), bf16), pltpu.VMEM((pivots, rows), f32), half),
@@ -499,7 +521,7 @@
         scratch_shapes=[
             pltpu.VMEM((pivots, total), f32),
             pltpu.VMEM((pivots, total), f32),
-            pltpu.SemaphoreType.DMA((3,)),
+            pltpu.SemaphoreType.DMA((5,)),
         ],
         compiler_params=pltpu.CompilerParams(vmem_limit_bytes=24 << 20),
     )(rank, *pieces, inverse)

time: 83.2 us -> 80.5 us (0.968)
  waiting for transfers between devices: 33.1 us -> 30.6 us
    ppermute x25, waiting for transfers between devices: 33.1 us -> 30.6 us  [move(): return lax.ppermute(value, axes, perm)]
    pallas_call x16 -> x17, Pallas kernels: 20.8 us -> 22.1 us  [call(): pl.pallas_call(kernel, out_shape=outs, in_specs=specs, out_specs=jax.tree...]
  transfers between devices with their start and end apart: 25 -> 25, of which waited for: 16 -> 18; matrix products, arithmetic and copies ran while one was open for 0% -> 0% of each run, Pallas kernels for 23% -> 25%
where the time goes in v1:
time: 80.5 us; the launch traced here: 80.4 us
  waiting for transfers between devices  30.6 us (38%)
  Pallas kernels  27 us (34%)
  starting transfers between devices  21.6 us (27%)
  between operations  1.01 us (1%)
    ppermute x25, waiting for transfers between devices, move(): return lax.ppermute(value, axes, perm)  30.6 us
    pallas_call x17, Pallas kernels, call(): pl.pallas_call(kernel, out_shape=outs, in_specs=specs, out_specs=jax.tree...  22.1 us
    ppermute x25, starting transfers between devices, move(): return lax.ppermute(value, axes, perm)  21.6 us
    pallas_call x1, Pallas kernels, body(): pl.pallas_call(partial(rows_kernel, masks), out_shape=jax.ShapeDtypeStruc...  2.63 us
    pallas_call x1, Pallas kernels, body(): pl.pallas_call(pick_kernel, out_shape=(pltpu.VMEM((slots, width), bf16),...  2.29 us
  transfers between devices with their start and end apart: 25, of which 18 were waited for; matrix products, arithmetic and copies ran while one was open for 0% of the time, Pallas kernels for 25%

profile of v1, /device:TPU:0, one launch (start us, length us, event | category | flops | bytes accessed | tf_op | source)
XLA Modules:
  0.0 80.4 jit_solution(15557839471698157830)
XLA Ops:
  0.6 2.3 %shard_map.68 = (bf16[18,512]{1,0:T(8,128)(2,1)S(1)}, s16[18,1024]{1,0:T(8,128)(2,1)S(1)}, bf16[512,512]{1,0:T(8,128)(2,1)S(1)}, f32[512,1024]{1,0:T(8,128)S(1)}) custom-call(s32[1]{0:T(128)} %bitcast.rank_ref, s32[1,256]{1,0:T(1,128)} %bitcast.6, s32[1,256]{1,0:T(1,128)} %bitcast.8, bf16[512,512]{1,0:T(8,128)(2,1)} %features_ref.1, f32[512,1024]{1,0:T(8,128)} %factor_ref.1), custom_call_target="tpu_custom_call" | custom-call | tf_op jit(solution)/shard_map/pallas_call | solution.py:411
  2.9 4.1 %collective-permute-start.1 = (bf16[18,512]{1,0:T(8,128)(2,1)S(1)}, bf16[18,512]{1,0:T(8,128)(2,1)S(1)}, u32[]{:S(2)}, u32[]{:S(2)}) collective-permute-start(bf16[18,512]{1,0:T(8,128)(2,1)S(1)} %get-tuple-element.51.refs_0_), channel_id=1, source_target_pairs={{0,16},{1,17},{2,18},{3,19},{4,20},{5,21},{6,22},{7,23},{8,24},{9,... | collective-permute-start | bytes 55304 | tf_op jit(solution)/shard_map/ppermute | solution.py:403
  7.2 1.6 %shard_map.69 = (s32[1,256]{1,0:T(1,128)S(1)}, f32[1,512]{1,0:T(1,128)S(1)}, bf16[512,1024]{1,0:T(8,128)(2,1)S(1)}, bf16[512,1024]{1,0:T(8,128)(2,1)S(1)}) custom-call(s32[1]{0:T(128)} %bitcast.rank_ref, s32[1,256]{1,0:T(1,128)S(1)} %bitcast.7, bf16[512,512]{1,0:T(8,128)(2,1)S(1)} %get-tuple-element.52.features_ref, f32[512,1024]{1,0:T(8,128)S(1)} %get-tuple-element.53.factor_ref), custom_call_target="tpu_custom_call" | custom-call | flops 1000000000 | bytes 1000000 | tf_op jit(solution)/shard_map/pallas_call | solution.py:51
  8.8 0.1 collective-permute-done.1.refs_1_
  8.9 3.3 %collective-permute-done.refs_1_ = s16[18,1024]{1,0:T(8,128)(2,1)S(1)} collective-permute-done((s16[18,1024]{1,0:T(8,128)(2,1)S(1)}, s16[18,1024]{1,0:T(8,128)(2,1)S(1)}, u32[]{:S(2)}, u32[]{:S(2)}) %collective-permute-start) | collective-permute-done | bytes 36896 | tf_op jit(solution)/shard_map/ppermute | solution.py:403
  12.2 1.5 %collective-permute-start.4 = (s16[36,1024]{1,0:T(8,128)(2,1)S(1)}, s16[36,1024]{1,0:T(8,128)(2,1)S(1)}, u32[]{:S(2)}, u32[]{:S(2)}) collective-permute-start(s16[36,1024]{1,0:T(8,128)(2,1)S(1)} %shard_map.73.refs_0_), channel_id=1, source_target_pairs={{0,8},{1,9},{2,10},{3,11},{4,12},{5,13},{6,14},{7,15},{8,0},{9,1},... | collective-permute-start | bytes 221192 | tf_op jit(solution)/shard_map/ppermute | solution.py:403
  13.7 3.0 %collective-permute-done.4.refs_1_ = s16[36,1024]{1,0:T(8,128)(2,1)S(1)} collective-permute-done((s16[36,1024]{1,0:T(8,128)(2,1)S(1)}, s16[36,1024]{1,0:T(8,128)(2,1)S(1)}, u32[]{:S(2)}, u32[]{:S(2)}) %collective-permute-start.4) | collective-permute-done | bytes 73760 | tf_op jit(solution)/shard_map/ppermute | solution.py:403
  16.7 1.6 %collective-permute-start.5 = (s16[72,1024]{1,0:T(8,128)(2,1)S(1)}, s16[72,1024]{1,0:T(8,128)(2,1)S(1)}, u32[]{:S(2)}, u32[]{:S(2)}) collective-permute-start(s16[72,1024]{1,0:T(8,128)(2,1)S(1)} %shard_map.74.refs_0_), channel_id=1, source_target_pairs={{0,4},{1,5},{2,3},{3,2},{4,0},{5,1},{6,7},{7,6},{8,12},{9,13},{10,... | collective-permute-start | bytes 442376 | tf_op jit(solution)/shard_map/ppermute | solution.py:403
  18.3 1.5 %collective-permute-start.2 = (bf16[36,512]{1,0:T(8,128)(2,1)S(1)}, bf16[36,512]{1,0:T(8,128)(2,1)S(1)}, u32[]{:S(2)}, u32[]{:S(2)}) collective-permute-start(bf16[36,512]{1,0:T(8,128)(2,1)S(1)} %shard_map.70.refs_0_), channel_id=1, source_target_pairs={{0,8},{1,9},{2,10},{3,11},{4,12},{5,13},{6,14},{7,15},{8,0},{9,1},... | collective-permute-start | bytes 110600 | tf_op jit(solution)/shard_map/ppermute | solution.py:403
  19.8 2.5 %collective-permute-done.2.refs_1_ = bf16[36,512]{1,0:T(8,128)(2,1)S(1)} collective-permute-done((bf16[36,512]{1,0:T(8,128)(2,1)S(1)}, bf16[36,512]{1,0:T(8,128)(2,1)S(1)}, u32[]{:S(2)}, u32[]{:S(2)}) %collective-permute-start.2) | collective-permute-done | bytes 36896 | tf_op jit(solution)/shard_map/ppermute | solution.py:403
  22.4 0.6 collective-permute-start.3
  23.1 1.6 %collective-permute-start.9 = (s16[144,1024]{1,0:T(8,128)(2,1)S(1)}, s16[144,1024]{1,0:T(8,128)(2,1)S(1)}, u32[]{:S(2)}, u32[]{:S(2)}) collective-permute-start(s16[144,1024]{1,0:T(8,128)(2,1)S(1)} %shard_map.75.a_h_ref), channel_id=1, source_target_pairs={{0,1},{1,0},{2,6},{3,7},{4,5},{5,4},{6,2},{7,3},{8,9},{9,8},{10,14... | collective-permute-start | bytes 884744 | tf_op jit(solution)/shard_map/ppermute | solution.py:403
  24.7 2.7 %collective-permute-done.3.refs_1_ = bf16[72,512]{1,0:T(8,128)(2,1)S(1)} collective-permute-done((bf16[72,512]{1,0:T(8,128)(2,1)S(1)}, bf16[72,512]{1,0:T(8,128)(2,1)S(1)}, u32[]{:S(2)}, u32[]{:S(2)}) %collective-permute-start.3) | collective-permute-done | bytes 73760 | tf_op jit(solution)/shard_map/ppermute | solution.py:403
  27.5 1.4 %collective-permute-done.6.c_x_ref = bf16[144,512]{1,0:T(8,128)(2,1)S(1)} collective-permute-done((bf16[144,512]{1,0:T(8,128)(2,1)S(1)}, bf16[144,512]{1,0:T(8,128)(2,1)S(1)}, u32[]{:S(2)}, u32[]{:S(2)}) %collective-permute-start.6) | collective-permute-done | bytes 147488 | tf_op jit(solution)/shard_map/ppermute | solution.py:403
  28.9 1.0 %shard_map.76 = (bf16[256,512]{1,0:T(8,128)(2,1)S(1)}, bf16[256,1024]{1,0:T(8,128)(2,1)S(1)}, bf16[256,1024]{1,0:T(8,128)(2,1)S(1)}) custom-call(s32[1,256]{1,0:T(1,128)S(1)} %get-tuple-element.58.source_ref, bf16[144,512]{1,0:T(8,128)(2,1)S(1)} %shard_map.72.a_x_ref, s16[144,1024]{1,0:T(8,128)(2,1)S(1)} %shard_map.75.a_h_ref, ...), custom_call_target="tpu_custom_call" | custom-call | flops 1000000000 | bytes 1000000 | tf_op jit(solution)/shard_map/pallas_call | solution.py:51
  29.9 0.2 collective-permute-start.10
  30.1 1.5 %collective-permute-start.8 = (bf16[144,512]{1,0:T(8,128)(2,1)S(1)}, bf16[144,512]{1,0:T(8,128)(2,1)S(1)}, u32[]{:S(2)}, u32[]{:S(2)}) collective-permute-start(bf16[144,512]{1,0:T(8,128)(2,1)S(1)} %shard_map.72.a_x_ref), channel_id=1, source_target_pairs={{0,1},{1,0},{2,6},{3,7},{4,5},{5,4},{6,2},{7,3},{8,9},{9,8},{10,14... | collective-permute-start | bytes 442376 | tf_op jit(solution)/shard_map/ppermute | solution.py:403
  31.6 0.5 shard_map.77
  32.1 0.5 shard_map.78
  32.7 2.5 %collective-permute-done.8.b_x_ref = bf16[144,512]{1,0:T(8,128)(2,1)S(1)} collective-permute-done((bf16[144,512]{1,0:T(8,128)(2,1)S(1)}, bf16[144,512]{1,0:T(8,128)(2,1)S(1)}, u32[]{:S(2)}, u32[]{:S(2)}) %collective-permute-start.8) | collective-permute-done | bytes 147488 | tf_op jit(solution)/shard_map/ppermute | solution.py:403
  35.2 1.0 %shard_map.79.product_ref = f32[256,512]{1,0:T(8,128)S(1)} custom-call(bf16[256,1024]{1,0:T(8,128)(2,1)S(1)} %get-tuple-element.84.coarse_ref.refs_1_, bf16[256,1024]{1,0:T(8,128)(2,1)S(1)} %get-tuple-element.85.fine_ref.refs_2_, bf16[512,1024]{1,0:T(8,128)(2,1)S(1)} %get-tuple-element.74.high_ref, bf16[512,1024]{1,0:T(8,128)(2,1)S(1)} %get-tuple-element.75.low_ref), custom_call_target="tpu_custom_call" | custom-call | flops 1000000000 | bytes 1000000 | tf_op jit(solution)/shard_map/pallas_call | solution.py:51
  36.3 0.4 collective-permute-done.11.d_x_ref
  36.6 2.2 %shard_map.80 = (bf16[256,512]{1,0:T(8,128)(2,1)S(1)}, f32[256,512]{1,0:T(8,128)S(1)}, f32[4,16,2432]{2,1,0:T(8,128)S(1)}) custom-call(s32[1]{0:T(128)} %bitcast.rank_ref, s32[1,256]{1,0:T(1,128)S(1)} %get-tuple-element.58.source_ref, bf16[256,512]{1,0:T(8,128)(2,1)S(1)} %get-tuple-element.61.x_ref, bf16[144,512]{1,0:T(8,128)(2,1)S(1)} %collective-permute-done.8.b_x_ref, ...), custom_call_target="tpu_custom_call" | custom-call | flops 1000000000 | bytes 1000000 | tf_op jit(solution)/shard_map/pallas_call | solution.py:51
  38.9 0.2 collective-permute-start.12
  39.1 1.3 %shard_map.81 = f32[4,16,2432]{2,1,0:T(8,128)S(1)} custom-call(s32[1]{0:T(128)} %bitcast.rank_ref, f32[256,512]{1,0:T(8,128)S(1)} %get-tuple-element.79.residual_ref, bf16[512,1024]{1,0:T(8,128)(2,1)S(1)} %get-tuple-element.74.high_ref, bf16[512,1024]{1,0:T(8,128)(2,1)S(1)} %get-tuple-element.75.low_ref, f32[1,512]{1,0:T(1,128)S(1)} %bitcast.5), custom_call_target="tpu_custom_call" | custom-call | flops 1000000000 | bytes 1000000 | tf_op jit(solution)/shard_map/pallas_call | solution.py:51
  40.4 0.6 collective-permute-done.12
  41.1 1.3 %collective-permute-start.15 = (f32[1,16,2432]{2,1,0:T(8,128)S(1)}, f32[1,16,2432]{2,1,0:T(8,128)S(1)}, u32[]{:S(2)}, u32[]{:S(2)}) collective-permute-start(f32[1,16,2432]{2,1,0:T(8,128)S(1)} %get-tuple-element.98), channel_id=1, source_target_pairs={{0,4},{1,5},{2,3},{3,2},{4,0},{5,1},{6,7},{7,6},{8,12},{9,13},{10,... | collective-permute-start | bytes 466952 | tf_op jit(solution)/shard_map/ppermute | solution.py:403
  42.4 1.5 %collective-permute-start.14 = (f32[1,16,2432]{2,1,0:T(8,128)S(1)}, f32[1,16,2432]{2,1,0:T(8,128)S(1)}, u32[]{:S(2)}, u32[]{:S(2)}) collective-permute-start(f32[1,16,2432]{2,1,0:T(8,128)S(1)} %get-tuple-element.99), channel_id=1, source_target_pairs={{0,1},{1,0},{2,6},{3,7},{4,5},{5,4},{6,2},{7,3},{8,9},{9,8},{10,14... | collective-permute-start | bytes 466952 | tf_op jit(solution)/shard_map/ppermute | solution.py:403
  43.9 0.7 collective-permute-start.13
  44.7 3.9 %shard_map.82.refs_0_ = f32[256,256]{1,0:T(8,128)S(1)} custom-call(bf16[256,512]{1,0:T(8,128)(2,1)S(1)} %get-tuple-element.83.refs_0_, bf16[256,1024]{1,0:T(8,128)(2,1)S(1)} %get-tuple-element.84.coarse_ref.refs_1_, bf16[256,1024]{1,0:T(8,128)(2,1)S(1)} %get-tuple-element.85.fine_ref.refs_2_), custom_call_target="tpu_custom_call" | custom-call | flops 1000000000 | bytes 1000000 | tf_op jit(solution)/shard_map/pallas_call | solution.py:51
  48.6 3.2 %collective-permute-done.13 = f32[1,16,2432]{2,1,0:T(8,128)S(1)} collective-permute-done((f32[1,16,2432]{2,1,0:T(8,128)S(1)}, f32[1,16,2432]{2,1,0:T(8,128)S(1)}, u32[]{:S(2)}, u32[]{:S(2)}) %collective-permute-start.13) | collective-permute-done | bytes 155680 | tf_op jit(solution)/shard_map/ppermute | solution.py:403
  51.8 0.9 %collective-permute-start.16 = (f32[1,16,2432]{2,1,0:T(8,128)S(1)}, f32[1,16,2432]{2,1,0:T(8,128)S(1)}, u32[]{:S(2)}, u32[]{:S(2)}) collective-permute-start(f32[1,16,2432]{2,1,0:T(8,128)S(1)} %add_add_fusion), channel_id=1, source_target_pairs={{0,16},{1,17},{2,18},{3,19},{4,20},{5,21},{6,22},{7,23},{8,24},{9,... | collective-permute-start | bytes 466952 | tf_op jit(solution)/shard_map/ppermute | solution.py:403
  52.7 4.2 %shard_map.83.refs_0_ = f32[256,256]{1,0:T(8,128)S(1)} custom-call(f32[256,256]{1,0:T(8,128)S(1)} %shard_map.82.refs_0_), custom_call_target="tpu_custom_call" | custom-call | flops 1000000000 | bytes 1000000 | tf_op jit(solution)/shard_map/pallas_call | solution.py:51
  56.8 4.7 %collective-permute-done.16 = f32[1,16,2432]{2,1,0:T(8,128)S(1)} collective-permute-done((f32[1,16,2432]{2,1,0:T(8,128)S(1)}, f32[1,16,2432]{2,1,0:T(8,128)S(1)}, u32[]{:S(2)}, u32[]{:S(2)}) %collective-permute-start.16) | collective-permute-done | bytes 155680 | tf_op jit(solution)/shard_map/ppermute | solution.py:403
  61.7 4.4 %shard_map.84.inverse_ref.refs_8_ = f32[256,256]{1,0:T(8,128)S(1)} custom-call(f32[256,256]{1,0:T(8,128)S(1)} %shard_map.83.refs_0_), custom_call_target="tpu_custom_call" | custom-call | flops 1000000000 | bytes 1000000 | tf_op jit(solution)/shard_map/pallas_call | solution.py:51
  66.1 0.9 %collective-permute-done.17 = f32[1,16,2432]{2,1,0:T(8,128)S(1)} collective-permute-done((f32[1,16,2432]{2,1,0:T(8,128)S(1)}, f32[1,16,2432]{2,1,0:T(8,128)S(1)}, u32[]{:S(2)}, u32[]{:S(2)}) %collective-permute-start.17) | collective-permute-done | bytes 155680 | tf_op jit(solution)/shard_map/ppermute | solution.py:403
  66.9 2.2 %collective-permute-start.18 = (f32[1,16,2432]{2,1,0:T(8,128)S(1)}, f32[1,16,2432]{2,1,0:T(8,128)S(1)}, u32[]{:S(2)}, u32[]{:S(2)}) collective-permute-start(f32[1,16,2432]{2,1,0:T(8,128)S(1)} %add.27.refs_0_), channel_id=1, source_target_pairs={{0,5},{1,4},{2,7},{3,6},{4,1},{5,0},{6,3},{7,2},{8,13},{9,12},{10,... | collective-permute-start | bytes 466952 | tf_op jit(solution)/shard_map/ppermute | solution.py:403
  69.2 0.7 collective-permute-start.20
  69.9 0.6 collective-permute-start.19
  70.5 1.4 %shard_map.85 = f32[512,256]{1,0:T(8,128)} custom-call(f32[256,512]{1,0:T(8,128)S(1)} %get-tuple-element.79.residual_ref, f32[256,256]{1,0:T(8,128)S(1)} %shard_map.84.inverse_ref.refs_8_), custom_call_target="tpu_custom_call" | custom-call | flops 1000000000 | bytes 1000000 | tf_op jit(solution)/shard_map/pallas_call | solution.py:51
  71.9 2.7 %collective-permute-done.18.refs_3_ = f32[1,16,2432]{2,1,0:T(8,128)S(1)} collective-permute-done((f32[1,16,2432]{2,1,0:T(8,128)S(1)}, f32[1,16,2432]{2,1,0:T(8,128)S(1)}, u32[]{:S(2)}, u32[]{:S(2)}) %collective-permute-start.18) | collective-permute-done | bytes 155680 | tf_op jit(solution)/shard_map/ppermute | solution.py:403
  74.6 1.1 %collective-permute-done.20.refs_2_ = f32[1,16,2432]{2,1,0:T(8,128)S(1)} collective-permute-done((f32[1,16,2432]{2,1,0:T(8,128)S(1)}, f32[1,16,2432]{2,1,0:T(8,128)S(1)}, u32[]{:S(2)}, u32[]{:S(2)}) %collective-permute-start.20) | collective-permute-done | bytes 155680 | tf_op jit(solution)/shard_map/ppermute | solution.py:403
  75.7 0.1 collective-permute-done.19.refs_1_
  75.8 0.4 collective-permute-start.22
  76.3 0.8 collective-permute-done.23.refs_6_
  77.1 0.2 collective-permute-done.22.refs_5_
  77.3 0.3 collective-permute-done.24.refs_7_
  77.6 2.6 %shard_map.86 = f32[256,1280]{1,0:T(8,128)} custom-call(s32[1]{0:T(128)} %bitcast.rank_ref, f32[1,16,2432]{2,1,0:T(8,128)S(1)} %add.27.refs_0_, f32[1,16,2432]{2,1,0:T(8,128)S(1)} %collective-permute-done.19.refs_1_, f32[1,16,2432]{2,1,0:T(8,128)S(1)} %collective-permute-done.20.refs_2_, f32[1,16,2432]{2,1,0:T(8,128)S(1)} %collective-permute-done.18.refs_3_, ...), custom_call_target="tpu_custom_call" | custom-call | tf_op jit(solution)/shard_map/pallas_call | solution.py:516
  (30 shorter events, 0.7 us)
Async XLA Ops:
  0.6 6.5 %copy-start.1 = (s32[256]{0:T(256)S(1)}, s32[256]{0:T(256)}, u32[]{:S(2)}) copy-start(s32[256]{0:T(256)} %param.8) | copy-start | bytes 3076
  2.9 5.9 %collective-permute-start.1 = (bf16[18,512]{1,0:T(8,128)(2,1)S(1)}, bf16[18,512]{1,0:T(8,128)(2,1)S(1)}, u32[]{:S(2)}, u32[]{:S(2)}) collective-permute-start(bf16[18,512]{1,0:T(8,128)(2,1)S(1)} %get-tuple-element.51.refs_0_), channel_id=1, source_target_pairs={{0,16},{1,17},{2,18},{3,19},{4,20},{5,21},{6,22},{7,23},{8,24},{9,... | collective-permute-start | bytes 55304 | tf_op jit(solution)/shard_map/ppermute | solution.py:403
  7.1 5.1 %collective-permute-start = (s16[18,1024]{1,0:T(8,128)(2,1)S(1)}, s16[18,1024]{1,0:T(8,128)(2,1)S(1)}, u32[]{:S(2)}, u32[]{:S(2)}) collective-permute-start(s16[18,1024]{1,0:T(8,128)(2,1)S(1)} %get-tuple-element.50.refs_0_), channel_id=1, source_target_pairs={{0,16},{1,17},{2,18},{3,19},{4,20},{5,21},{6,22},{7,23},{8,24},{9,... | collective-permute-start | bytes 110600 | tf_op jit(solution)/shard_map/ppermute | solution.py:403
  12.2 4.5 %collective-permute-start.4 = (s16[36,1024]{1,0:T(8,128)(2,1)S(1)}, s16[36,1024]{1,0:T(8,128)(2,1)S(1)}, u32[]{:S(2)}, u32[]{:S(2)}) collective-permute-start(s16[36,1024]{1,0:T(8,128)(2,1)S(1)} %shard_map.73.refs_0_), channel_id=1, source_target_pairs={{0,8},{1,9},{2,10},{3,11},{4,12},{5,13},{6,14},{7,15},{8,0},{9,1},... | collective-permute-start | bytes 221192 | tf_op jit(solution)/shard_map/ppermute | solution.py:403
  16.7 6.2 %collective-permute-start.5 = (s16[72,1024]{1,0:T(8,128)(2,1)S(1)}, s16[72,1024]{1,0:T(8,128)(2,1)S(1)}, u32[]{:S(2)}, u32[]{:S(2)}) collective-permute-start(s16[72,1024]{1,0:T(8,128)(2,1)S(1)} %shard_map.74.refs_0_), channel_id=1, source_target_pairs={{0,4},{1,5},{2,3},{3,2},{4,0},{5,1},{6,7},{7,6},{8,12},{9,13},{10,... | collective-permute-start | bytes 442376 | tf_op jit(solution)/shard_map/ppermute | solution.py:403
  18.3 4.1 %collective-permute-start.2 = (bf16[36,512]{1,0:T(8,128)(2,1)S(1)}, bf16[36,512]{1,0:T(8,128)(2,1)S(1)}, u32[]{:S(2)}, u32[]{:S(2)}) collective-permute-start(bf16[36,512]{1,0:T(8,128)(2,1)S(1)} %shard_map.70.refs_0_), channel_id=1, source_target_pairs={{0,8},{1,9},{2,10},{3,11},{4,12},{5,13},{6,14},{7,15},{8,0},{9,1},... | collective-permute-start | bytes 110600 | tf_op jit(solution)/shard_map/ppermute | solution.py:403
  22.4 5.0 %collective-permute-start.3 = (bf16[72,512]{1,0:T(8,128)(2,1)S(1)}, bf16[72,512]{1,0:T(8,128)(2,1)S(1)}, u32[]{:S(2)}, u32[]{:S(2)}) collective-permute-start(bf16[72,512]{1,0:T(8,128)(2,1)S(1)} %shard_map.71.refs_0_), channel_id=1, source_target_pairs={{0,4},{1,5},{2,3},{3,2},{4,0},{5,1},{6,7},{7,6},{8,12},{9,13},{10,... | collective-permute-start | bytes 221192 | tf_op jit(solution)/shard_map/ppermute | solution.py:403
  23.0 5.9 %collective-permute-start.7 = (s16[144,1024]{1,0:T(8,128)(2,1)S(1)}, s16[144,1024]{1,0:T(8,128)(2,1)S(1)}, u32[]{:S(2)}, u32[]{:S(2)}) collective-permute-start(s16[144,1024]{1,0:T(8,128)(2,1)S(1)} %shard_map.75.a_h_ref), channel_id=1, source_target_pairs={{0,2},{1,3},{2,0},{3,1},{4,6},{5,7},{6,4},{7,5},{8,10},{9,11},{10,... | collective-permute-start | bytes 884744 | tf_op jit(solution)/shard_map/ppermute | solution.py:403
  23.1 6.8 %collective-permute-start.9 = (s16[144,1024]{1,0:T(8,128)(2,1)S(1)}, s16[144,1024]{1,0:T(8,128)(2,1)S(1)}, u32[]{:S(2)}, u32[]{:S(2)}) collective-permute-start(s16[144,1024]{1,0:T(8,128)(2,1)S(1)} %shard_map.75.a_h_ref), channel_id=1, source_target_pairs={{0,1},{1,0},{2,6},{3,7},{4,5},{5,4},{6,2},{7,3},{8,9},{9,8},{10,14... | collective-permute-start | bytes 884744 | tf_op jit(solution)/shard_map/ppermute | solution.py:403
  27.4 1.4 %collective-permute-start.6 = (bf16[144,512]{1,0:T(8,128)(2,1)S(1)}, bf16[144,512]{1,0:T(8,128)(2,1)S(1)}, u32[]{:S(2)}, u32[]{:S(2)}) collective-permute-start(bf16[144,512]{1,0:T(8,128)(2,1)S(1)} %shard_map.72.a_x_ref), channel_id=1, source_target_pairs={{0,2},{1,3},{2,0},{3,1},{4,6},{5,7},{6,4},{7,5},{8,10},{9,11},{10,... | collective-permute-start | bytes 442376 | tf_op jit(solution)/shard_map/ppermute | solution.py:403
  29.9 2.3 %collective-permute-start.10 = (s16[144,1024]{1,0:T(8,128)(2,1)S(1)}, s16[144,1024]{1,0:T(8,128)(2,1)S(1)}, u32[]{:S(2)}, u32[]{:S(2)}) collective-permute-start(s16[144,1024]{1,0:T(8,128)(2,1)S(1)} %collective-permute-done.9.h_ref), channel_id=1, source_target_pairs={{0,2},{1,3},{2,0},{3,1},{4,6},{5,7},{6,4},{7,5},{8,10},{9,11},{10,... | collective-permute-start | bytes 884744 | tf_op jit(solution)/shard_map/ppermute | solution.py:403
  30.1 5.1 %collective-permute-start.8 = (bf16[144,512]{1,0:T(8,128)(2,1)S(1)}, bf16[144,512]{1,0:T(8,128)(2,1)S(1)}, u32[]{:S(2)}, u32[]{:S(2)}) collective-permute-start(bf16[144,512]{1,0:T(8,128)(2,1)S(1)} %shard_map.72.a_x_ref), channel_id=1, source_target_pairs={{0,1},{1,0},{2,6},{3,7},{4,5},{5,4},{6,2},{7,3},{8,9},{9,8},{10,14... | collective-permute-start | bytes 442376 | tf_op jit(solution)/shard_map/ppermute | solution.py:403
  32.7 3.9 %copy-start = (f32[512]{0:T(512)S(1)}, f32[512]{0:T(512)}, u32[]{:S(2)}) copy-start(f32[512]{0:T(512)} %param.7) | copy-start | bytes 6148
  35.2 1.4 %collective-permute-start.11 = (bf16[144,512]{1,0:T(8,128)(2,1)S(1)}, bf16[144,512]{1,0:T(8,128)(2,1)S(1)}, u32[]{:S(2)}, u32[]{:S(2)}) collective-permute-start(bf16[144,512]{1,0:T(8,128)(2,1)S(1)} %collective-permute-done.8.b_x_ref), channel_id=1, source_target_pairs={{0,2},{1,3},{2,0},{3,1},{4,6},{5,7},{6,4},{7,5},{8,10},{9,11},{10,... | collective-permute-start | bytes 442376 | tf_op jit(solution)/shard_map/ppermute | solution.py:403
  38.9 2.1 %collective-permute-start.12 = (f32[4,16,2432]{2,1,0:T(8,128)S(1)}, f32[4,16,2432]{2,1,0:T(8,128)S(1)}, u32[]{:S(2)}, u32[]{:S(2)}) collective-permute-start(f32[4,16,2432]{2,1,0:T(8,128)S(1)} %get-tuple-element.80), channel_id=1, source_target_pairs={{0,2},{1,3},{2,0},{3,1},{4,6},{5,7},{6,4},{7,5},{8,10},{9,11},{10,... | collective-permute-start | bytes 1867784 | tf_op jit(solution)/shard_map/ppermute | solution.py:403
  41.1 7.5 %collective-permute-start.15 = (f32[1,16,2432]{2,1,0:T(8,128)S(1)}, f32[1,16,2432]{2,1,0:T(8,128)S(1)}, u32[]{:S(2)}, u32[]{:S(2)}) collective-permute-start(f32[1,16,2432]{2,1,0:T(8,128)S(1)} %get-tuple-element.98), channel_id=1, source_target_pairs={{0,4},{1,5},{2,3},{3,2},{4,0},{5,1},{6,7},{7,6},{8,12},{9,13},{10,... | collective-permute-start | bytes 466952 | tf_op jit(solution)/shard_map/ppermute | solution.py:403
  42.4 6.1 %collective-permute-start.14 = (f32[1,16,2432]{2,1,0:T(8,128)S(1)}, f32[1,16,2432]{2,1,0:T(8,128)S(1)}, u32[]{:S(2)}, u32[]{:S(2)}) collective-permute-start(f32[1,16,2432]{2,1,0:T(8,128)S(1)} %get-tuple-element.99), channel_id=1, source_target_pairs={{0,1},{1,0},{2,6},{3,7},{4,5},{5,4},{6,2},{7,3},{8,9},{9,8},{10,14... | collective-permute-start | bytes 466952 | tf_op jit(solution)/shard_map/ppermute | solution.py:403
  43.9 7.8 %collective-permute-start.13 = (f32[1,16,2432]{2,1,0:T(8,128)S(1)}, f32[1,16,2432]{2,1,0:T(8,128)S(1)}, u32[]{:S(2)}, u32[]{:S(2)}) collective-permute-start(f32[1,16,2432]{2,1,0:T(8,128)S(1)} %get-tuple-element.100), channel_id=1, source_target_pairs={{0,5},{1,4},{2,7},{3,6},{4,1},{5,0},{6,3},{7,2},{8,13},{9,12},{10,... | collective-permute-start | bytes 466952 | tf_op jit(solution)/shard_map/ppermute | solution.py:403
  51.8 9.8 %collective-permute-start.16 = (f32[1,16,2432]{2,1,0:T(8,128)S(1)}, f32[1,16,2432]{2,1,0:T(8,128)S(1)}, u32[]{:S(2)}, u32[]{:S(2)}) collective-permute-start(f32[1,16,2432]{2,1,0:T(8,128)S(1)} %add_add_fusion), channel_id=1, source_target_pairs={{0,16},{1,17},{2,18},{3,19},{4,20},{5,21},{6,22},{7,23},{8,24},{9,... | collective-permute-start | bytes 466952 | tf_op jit(solution)/shard_map/ppermute | solution.py:403
  61.6 5.3 %collective-permute-start.17 = (f32[1,16,2432]{2,1,0:T(8,128)S(1)}, f32[1,16,2432]{2,1,0:T(8,128)S(1)}, u32[]{:S(2)}, u32[]{:S(2)}) collective-permute-start(f32[1,16,2432]{2,1,0:T(8,128)S(1)} %add.26), channel_id=1, source_target_pairs={{0,8},{1,9},{2,10},{3,11},{4,12},{5,13},{6,14},{7,15},{8,0},{9,1},... | collective-permute-start | bytes 466952 | tf_op jit(solution)/shard_map/ppermute | solution.py:403
  66.9 7.7 %collective-permute-start.18 = (f32[1,16,2432]{2,1,0:T(8,128)S(1)}, f32[1,16,2432]{2,1,0:T(8,128)S(1)}, u32[]{:S(2)}, u32[]{:S(2)}) collective-permute-start(f32[1,16,2432]{2,1,0:T(8,128)S(1)} %add.27.refs_0_), channel_id=1, source_target_pairs={{0,5},{1,4},{2,7},{3,6},{4,1},{5,0},{6,3},{7,2},{8,13},{9,12},{10,... | collective-permute-start | bytes 466952 | tf_op jit(solution)/shard_map/ppermute | solution.py:403
  69.2 6.5 %collective-permute-start.20 = (f32[1,16,2432]{2,1,0:T(8,128)S(1)}, f32[1,16,2432]{2,1,0:T(8,128)S(1)}, u32[]{:S(2)}, u32[]{:S(2)}) collective-permute-start(f32[1,16,2432]{2,1,0:T(8,128)S(1)} %add.27.refs_0_), channel_id=1, source_target_pairs={{0,4},{1,5},{2,3},{3,2},{4,0},{5,1},{6,7},{7,6},{8,12},{9,13},{10,... | collective-permute-start | bytes 466952 | tf_op jit(solution)/shard_map/ppermute | solution.py:403
  69.9 5.9 %collective-permute-start.19 = (f32[1,16,2432]{2,1,0:T(8,128)S(1)}, f32[1,16,2432]{2,1,0:T(8,128)S(1)}, u32[]{:S(2)}, u32[]{:S(2)}) collective-permute-start(f32[1,16,2432]{2,1,0:T(8,128)S(1)} %add.27.refs_0_), channel_id=1, source_target_pairs={{0,1},{1,0},{2,6},{3,7},{4,5},{5,4},{6,2},{7,3},{8,9},{9,8},{10,14... | collective-permute-start | bytes 466952 | tf_op jit(solution)/shard_map/ppermute | solution.py:403
  70.5 5.8 %collective-permute-start.21 = (f32[1,16,2432]{2,1,0:T(8,128)S(1)}, f32[1,16,2432]{2,1,0:T(8,128)S(1)}, u32[]{:S(2)}, u32[]{:S(2)}) collective-permute-start(f32[1,16,2432]{2,1,0:T(8,128)S(1)} %add.27.refs_0_), channel_id=1, source_target_pairs={{0,2},{1,3},{2,0},{3,1},{4,6},{5,7},{6,4},{7,5},{8,10},{9,11},{10,... | collective-permute-start | bytes 466952 | tf_op jit(solution)/shard_map/ppermute | solution.py:403
  75.7 1.4 %collective-permute-start.23 = (f32[1,16,2432]{2,1,0:T(8,128)S(1)}, f32[1,16,2432]{2,1,0:T(8,128)S(1)}, u32[]{:S(2)}, u32[]{:S(2)}) collective-permute-start(f32[1,16,2432]{2,1,0:T(8,128)S(1)} %collective-permute-done.20.refs_2_), channel_id=1, source_target_pairs={{0,2},{1,3},{2,0},{3,1},{4,6},{5,7},{6,4},{7,5},{8,10},{9,11},{10,... | collective-permute-start | bytes 466952 | tf_op jit(solution)/shard_map/ppermute | solution.py:403
  75.8 1.5 %collective-permute-start.22 = (f32[1,16,2432]{2,1,0:T(8,128)S(1)}, f32[1,16,2432]{2,1,0:T(8,128)S(1)}, u32[]{:S(2)}, u32[]{:S(2)}) collective-permute-start(f32[1,16,2432]{2,1,0:T(8,128)S(1)} %collective-permute-done.19.refs_1_), channel_id=1, source_target_pairs={{0,2},{1,3},{2,0},{3,1},{4,6},{5,7},{6,4},{7,5},{8,10},{9,11},{10,... | collective-permute-start | bytes 466952 | tf_op jit(solution)/shard_map/ppermute | solution.py:403
  76.2 1.4 %collective-permute-start.24 = (f32[1,16,2432]{2,1,0:T(8,128)S(1)}, f32[1,16,2432]{2,1,0:T(8,128)S(1)}, u32[]{:S(2)}, u32[]{:S(2)}) collective-permute-start(f32[1,16,2432]{2,1,0:T(8,128)S(1)} %collective-permute-done.18.refs_3_), channel_id=1, source_target_pairs={{0,2},{1,3},{2,0},{3,1},{4,6},{5,7},{6,4},{7,5},{8,10},{9,11},{10,... | collective-permute-start | bytes 466952 | tf_op jit(solution)/shard_map/ppermute | solution.py:403

commit v2 on v1

--- a/solution.py
+++ b/solution.py
@@ -485,7 +485,7 @@
     keep = keep + received
 
     panels = pivots // PANEL
-    cuts = [0, panels // 4, panels * 5 // 8, panels]
+    cuts = [0, panels * 3 // 8, panels * 3 // 4, panels]
 
     def eliminate_step(step, *given):
         return call(
@@ -500,13 +500,16 @@
     from_both, from_second, from_first, work = tie(from_both, from_second, from_first, work)
     keep = (keep[0:1] + from_both) + (from_second + from_first)
     step = 1
-    for mask in others:
-        got = move(keep, pair(mask))
+    split_at = keep.shape[1] // 2
+    one, two = keep[:, :split_at], keep[:, split_at:]
+    for mask, other_mask in zip(others, others[::-1]):
+        got_one, got_two = move(one, pair(mask)), move(two, pair(other_mask))
         if step < len(cuts) - 1:
             work = eliminate_step(step, work)
-            got, work = tie(got, work)
+            got_one, got_two, work = tie(got_one, got_two, work)
             step += 1
-        keep = keep + got
+        one, two = one + got_one, two + got_two
+    keep = jnp.concatenate([one, two], axis=1)
     inverse = work
     keep, inverse = tie(keep, inverse)
     pieces = [near(keep)] + [near(move(keep, perm)) for perm in (second_pair, first_pair, both_pair)]

time: 80.5 us -> 79.3 us (0.985)
  waiting for transfers between devices: 30.6 us -> 24.7 us
  starting transfers between devices: 21.6 us -> 26.2 us
    ppermute x25 -> x27, waiting for transfers between devices: 30.6 us -> 24.7 us  [move(): return lax.ppermute(value, axes, perm)]
    ppermute x25 -> x27, starting transfers between devices: 21.6 us -> 26.2 us  [move(): return lax.ppermute(value, axes, perm)]
  transfers between devices with their start and end apart: 25 -> 27, of which waited for: 18 -> 18; matrix products, arithmetic and copies ran while one was open for 0% -> 0% of each run, Pallas kernels for 25% -> 25%
where the time goes in v2:
time: 79.3 us; the launch traced here: 79.1 us
  Pallas kernels  27 us (34%)
  starting transfers between devices  26.2 us (33%)
  waiting for transfers between devices  24.7 us (31%)
  between operations  1.03 us (1%)
    ppermute x27, starting transfers between devices, move(): return lax.ppermute(value, axes, perm)  26.2 us
    ppermute x27, waiting for transfers between devices, move(): return lax.ppermute(value, axes, perm)  24.7 us
    pallas_call x17, Pallas kernels, call(): pl.pallas_call(kernel, out_shape=outs, in_specs=specs, out_specs=jax.tree...  22.1 us
    pallas_call x1, Pallas kernels, body(): pl.pallas_call(partial(rows_kernel, masks), out_shape=jax.ShapeDtypeStruc...  2.63 us
    pallas_call x1, Pallas kernels, body(): pl.pallas_call(pick_kernel, out_shape=(pltpu.VMEM((slots, width), bf16),...  2.29 us
  transfers between devices with their start and end apart: 27, of which 18 were waited for; matrix products, arithmetic and copies ran while one was open for 0% of the time, Pallas kernels for 25%

profile of v2, /device:TPU:0, one launch (start us, length us, event | category | flops | bytes accessed | tf_op | source)
XLA Modules:
  0.0 79.1 jit_solution(6582041527266791296)
XLA Ops:
  0.6 2.3 %shard_map.68 = (bf16[18,512]{1,0:T(8,128)(2,1)S(1)}, s16[18,1024]{1,0:T(8,128)(2,1)S(1)}, bf16[512,512]{1,0:T(8,128)(2,1)S(1)}, f32[512,1024]{1,0:T(8,128)S(1)}) custom-call(s32[1]{0:T(128)} %bitcast.rank_ref, s32[1,256]{1,0:T(1,128)} %bitcast.6, s32[1,256]{1,0:T(1,128)} %bitcast.8, bf16[512,512]{1,0:T(8,128)(2,1)} %features_ref.1, f32[512,1024]{1,0:T(8,128)} %factor_ref.1), custom_call_target="tpu_custom_call" | custom-call | tf_op jit(solution)/shard_map/pallas_call | solution.py:411
  2.9 4.1 %collective-permute-start.1 = (bf16[18,512]{1,0:T(8,128)(2,1)S(1)}, bf16[18,512]{1,0:T(8,128)(2,1)S(1)}, u32[]{:S(2)}, u32[]{:S(2)}) collective-permute-start(bf16[18,512]{1,0:T(8,128)(2,1)S(1)} %get-tuple-element.53.refs_0_), channel_id=1, source_target_pairs={{0,16},{1,17},{2,18},{3,19},{4,20},{5,21},{6,22},{7,23},{8,24},{9,... | collective-permute-start | bytes 55304 | tf_op jit(solution)/shard_map/ppermute | solution.py:403
  7.2 1.6 %shard_map.69 = (s32[1,256]{1,0:T(1,128)S(1)}, f32[1,512]{1,0:T(1,128)S(1)}, bf16[512,1024]{1,0:T(8,128)(2,1)S(1)}, bf16[512,1024]{1,0:T(8,128)(2,1)S(1)}) custom-call(s32[1]{0:T(128)} %bitcast.rank_ref, s32[1,256]{1,0:T(1,128)S(1)} %bitcast.7, bf16[512,512]{1,0:T(8,128)(2,1)S(1)} %get-tuple-element.54.features_ref, f32[512,1024]{1,0:T(8,128)S(1)} %get-tuple-element.55.factor_ref), custom_call_target="tpu_custom_call" | custom-call | flops 1000000000 | bytes 1000000 | tf_op jit(solution)/shard_map/pallas_call | solution.py:51
  8.9 3.3 %collective-permute-done.refs_1_ = s16[18,1024]{1,0:T(8,128)(2,1)S(1)} collective-permute-done((s16[18,1024]{1,0:T(8,128)(2,1)S(1)}, s16[18,1024]{1,0:T(8,128)(2,1)S(1)}, u32[]{:S(2)}, u32[]{:S(2)}) %collective-permute-start) | collective-permute-done | bytes 36896 | tf_op jit(solution)/shard_map/ppermute | solution.py:403
  12.2 1.5 %collective-permute-start.4 = (s16[36,1024]{1,0:T(8,128)(2,1)S(1)}, s16[36,1024]{1,0:T(8,128)(2,1)S(1)}, u32[]{:S(2)}, u32[]{:S(2)}) collective-permute-start(s16[36,1024]{1,0:T(8,128)(2,1)S(1)} %shard_map.73.refs_0_), channel_id=1, source_target_pairs={{0,8},{1,9},{2,10},{3,11},{4,12},{5,13},{6,14},{7,15},{8,0},{9,1},... | collective-permute-start | bytes 221192 | tf_op jit(solution)/shard_map/ppermute | solution.py:403
  13.7 3.0 %collective-permute-done.4.refs_1_ = s16[36,1024]{1,0:T(8,128)(2,1)S(1)} collective-permute-done((s16[36,1024]{1,0:T(8,128)(2,1)S(1)}, s16[36,1024]{1,0:T(8,128)(2,1)S(1)}, u32[]{:S(2)}, u32[]{:S(2)}) %collective-permute-start.4) | collective-permute-done | bytes 73760 | tf_op jit(solution)/shard_map/ppermute | solution.py:403
  16.7 1.6 %collective-permute-start.5 = (s16[72,1024]{1,0:T(8,128)(2,1)S(1)}, s16[72,1024]{1,0:T(8,128)(2,1)S(1)}, u32[]{:S(2)}, u32[]{:S(2)}) collective-permute-start(s16[72,1024]{1,0:T(8,128)(2,1)S(1)} %shard_map.74.refs_0_), channel_id=1, source_target_pairs={{0,4},{1,5},{2,3},{3,2},{4,0},{5,1},{6,7},{7,6},{8,12},{9,13},{10,... | collective-permute-start | bytes 442376 | tf_op jit(solution)/shard_map/ppermute | solution.py:403
  18.3 1.5 %collective-permute-start.2 = (bf16[36,512]{1,0:T(8,128)(2,1)S(1)}, bf16[36,512]{1,0:T(8,128)(2,1)S(1)}, u32[]{:S(2)}, u32[]{:S(2)}) collective-permute-start(bf16[36,512]{1,0:T(8,128)(2,1)S(1)} %shard_map.70.refs_0_), channel_id=1, source_target_pairs={{0,8},{1,9},{2,10},{3,11},{4,12},{5,13},{6,14},{7,15},{8,0},{9,1},... | collective-permute-start | bytes 110600 | tf_op jit(solution)/shard_map/ppermute | solution.py:403
  19.8 2.5 %collective-permute-done.2.refs_1_ = bf16[36,512]{1,0:T(8,128)(2,1)S(1)} collective-permute-done((bf16[36,512]{1,0:T(8,128)(2,1)S(1)}, bf16[36,512]{1,0:T(8,128)(2,1)S(1)}, u32[]{:S(2)}, u32[]{:S(2)}) %collective-permute-start.2) | collective-permute-done | bytes 36896 | tf_op jit(solution)/shard_map/ppermute | solution.py:403
  22.4 0.6 collective-permute-start.3
  23.1 1.6 %collective-permute-start.9 = (s16[144,1024]{1,0:T(8,128)(2,1)S(1)}, s16[144,1024]{1,0:T(8,128)(2,1)S(1)}, u32[]{:S(2)}, u32[]{:S(2)}) collective-permute-start(s16[144,1024]{1,0:T(8,128)(2,1)S(1)} %shard_map.75.a_h_ref), channel_id=1, source_target_pairs={{0,1},{1,0},{2,6},{3,7},{4,5},{5,4},{6,2},{7,3},{8,9},{9,8},{10,14... | collective-permute-start | bytes 884744 | tf_op jit(solution)/shard_map/ppermute | solution.py:403
  24.7 2.7 %collective-permute-done.3.refs_1_ = bf16[72,512]{1,0:T(8,128)(2,1)S(1)} collective-permute-done((bf16[72,512]{1,0:T(8,128)(2,1)S(1)}, bf16[72,512]{1,0:T(8,128)(2,1)S(1)}, u32[]{:S(2)}, u32[]{:S(2)}) %collective-permute-start.3) | collective-permute-done | bytes 73760 | tf_op jit(solution)/shard_map/ppermute | solution.py:403
  27.5 1.4 %collective-permute-done.6.c_x_ref = bf16[144,512]{1,0:T(8,128)(2,1)S(1)} collective-permute-done((bf16[144,512]{1,0:T(8,128)(2,1)S(1)}, bf16[144,512]{1,0:T(8,128)(2,1)S(1)}, u32[]{:S(2)}, u32[]{:S(2)}) %collective-permute-start.6) | collective-permute-done | bytes 147488 | tf_op jit(solution)/shard_map/ppermute | solution.py:403
  28.9 1.0 %shard_map.76 = (bf16[256,512]{1,0:T(8,128)(2,1)S(1)}, bf16[256,1024]{1,0:T(8,128)(2,1)S(1)}, bf16[256,1024]{1,0:T(8,128)(2,1)S(1)}) custom-call(s32[1,256]{1,0:T(1,128)S(1)} %get-tuple-element.60.source_ref, bf16[144,512]{1,0:T(8,128)(2,1)S(1)} %shard_map.72.a_x_ref, s16[144,1024]{1,0:T(8,128)(2,1)S(1)} %shard_map.75.a_h_ref, ...), custom_call_target="tpu_custom_call" | custom-call | flops 1000000000 | bytes 1000000 | tf_op jit(solution)/shard_map/pallas_call | solution.py:51
  29.9 0.2 collective-permute-start.10
  30.1 1.5 %collective-permute-start.8 = (bf16[144,512]{1,0:T(8,128)(2,1)S(1)}, bf16[144,512]{1,0:T(8,128)(2,1)S(1)}, u32[]{:S(2)}, u32[]{:S(2)}) collective-permute-start(bf16[144,512]{1,0:T(8,128)(2,1)S(1)} %shard_map.72.a_x_ref), channel_id=1, source_target_pairs={{0,1},{1,0},{2,6},{3,7},{4,5},{5,4},{6,2},{7,3},{8,9},{9,8},{10,14... | collective-permute-start | bytes 442376 | tf_op jit(solution)/shard_map/ppermute | solution.py:403
  31.6 0.5 shard_map.77
  32.1 0.5 shard_map.78
  32.7 2.5 %collective-permute-done.8.b_x_ref = bf16[144,512]{1,0:T(8,128)(2,1)S(1)} collective-permute-done((bf16[144,512]{1,0:T(8,128)(2,1)S(1)}, bf16[144,512]{1,0:T(8,128)(2,1)S(1)}, u32[]{:S(2)}, u32[]{:S(2)}) %collective-permute-start.8) | collective-permute-done | bytes 147488 | tf_op jit(solution)/shard_map/ppermute | solution.py:403
  35.2 1.0 %shard_map.79.product_ref = f32[256,512]{1,0:T(8,128)S(1)} custom-call(bf16[256,1024]{1,0:T(8,128)(2,1)S(1)} %get-tuple-element.86.coarse_ref.refs_1_, bf16[256,1024]{1,0:T(8,128)(2,1)S(1)} %get-tuple-element.87.fine_ref.refs_2_, bf16[512,1024]{1,0:T(8,128)(2,1)S(1)} %get-tuple-element.76.high_ref, bf16[512,1024]{1,0:T(8,128)(2,1)S(1)} %get-tuple-element.77.low_ref), custom_call_target="tpu_custom_call" | custom-call | flops 1000000000 | bytes 1000000 | tf_op jit(solution)/shard_map/pallas_call | solution.py:51
  36.3 0.4 collective-permute-done.11.d_x_ref
  36.6 2.2 %shard_map.80 = (bf16[256,512]{1,0:T(8,128)(2,1)S(1)}, f32[256,512]{1,0:T(8,128)S(1)}, f32[4,16,2432]{2,1,0:T(8,128)S(1)}) custom-call(s32[1]{0:T(128)} %bitcast.rank_ref, s32[1,256]{1,0:T(1,128)S(1)} %get-tuple-element.60.source_ref, bf16[256,512]{1,0:T(8,128)(2,1)S(1)} %get-tuple-element.63.x_ref, bf16[144,512]{1,0:T(8,128)(2,1)S(1)} %collective-permute-done.8.b_x_ref, ...), custom_call_target="tpu_custom_call" | custom-call | flops 1000000000 | bytes 1000000 | tf_op jit(solution)/shard_map/pallas_call | solution.py:51
  38.9 0.2 collective-permute-start.12
  39.1 1.3 %shard_map.81 = f32[4,16,2432]{2,1,0:T(8,128)S(1)} custom-call(s32[1]{0:T(128)} %bitcast.rank_ref, f32[256,512]{1,0:T(8,128)S(1)} %get-tuple-element.81.residual_ref, bf16[512,1024]{1,0:T(8,128)(2,1)S(1)} %get-tuple-element.76.high_ref, bf16[512,1024]{1,0:T(8,128)(2,1)S(1)} %get-tuple-element.77.low_ref, f32[1,512]{1,0:T(1,128)S(1)} %bitcast.5), custom_call_target="tpu_custom_call" | custom-call | flops 1000000000 | bytes 1000000 | tf_op jit(solution)/shard_map/pallas_call | solution.py:51
  40.4 0.6 collective-permute-done.12
  41.1 1.3 %collective-permute-start.15 = (f32[1,16,2432]{2,1,0:T(8,128)S(1)}, f32[1,16,2432]{2,1,0:T(8,128)S(1)}, u32[]{:S(2)}, u32[]{:S(2)}) collective-permute-start(f32[1,16,2432]{2,1,0:T(8,128)S(1)} %get-tuple-element.102), channel_id=1, source_target_pairs={{0,4},{1,5},{2,3},{3,2},{4,0},{5,1},{6,7},{7,6},{8,12},{9,13},{10,... | collective-permute-start | bytes 466952 | tf_op jit(solution)/shard_map/ppermute | solution.py:403
  42.4 1.5 %collective-permute-start.14 = (f32[1,16,2432]{2,1,0:T(8,128)S(1)}, f32[1,16,2432]{2,1,0:T(8,128)S(1)}, u32[]{:S(2)}, u32[]{:S(2)}) collective-permute-start(f32[1,16,2432]{2,1,0:T(8,128)S(1)} %get-tuple-element.103), channel_id=1, source_target_pairs={{0,1},{1,0},{2,6},{3,7},{4,5},{5,4},{6,2},{7,3},{8,9},{9,8},{10,14... | collective-permute-start | bytes 466952 | tf_op jit(solution)/shard_map/ppermute | solution.py:403
  43.9 0.7 collective-permute-start.13
  44.7 5.3 %shard_map.82.refs_0_ = f32[256,256]{1,0:T(8,128)S(1)} custom-call(bf16[256,512]{1,0:T(8,128)(2,1)S(1)} %get-tuple-element.85.refs_0_, bf16[256,1024]{1,0:T(8,128)(2,1)S(1)} %get-tuple-element.86.coarse_ref.refs_1_, bf16[256,1024]{1,0:T(8,128)(2,1)S(1)} %get-tuple-element.87.fine_ref.refs_2_), custom_call_target="tpu_custom_call" | custom-call | flops 1000000000 | bytes 1000000 | tf_op jit(solution)/shard_map/pallas_call | solution.py:51
  50.0 1.8 %collective-permute-done.13 = f32[1,16,2432]{2,1,0:T(8,128)S(1)} collective-permute-done((f32[1,16,2432]{2,1,0:T(8,128)S(1)}, f32[1,16,2432]{2,1,0:T(8,128)S(1)}, u32[]{:S(2)}, u32[]{:S(2)}) %collective-permute-start.13) | collective-permute-done | bytes 155680 | tf_op jit(solution)/shard_map/ppermute | solution.py:403
  51.8 1.5 %collective-permute-start.17 = (f32[1,8,2432]{2,1,0:T(8,128)S(1)}, f32[1,8,2432]{2,1,0:T(8,128)S(1)}, u32[]{:S(2)}, u32[]{:S(2)}) collective-permute-start(f32[1,8,2432]{2,1,0:T(8,128)S(1)} %get-tuple-element.107), channel_id=1, source_target_pairs={{0,8},{1,9},{2,10},{3,11},{4,12},{5,13},{6,14},{7,15},{8,0},{9,1},... | collective-permute-start | bytes 233480 | tf_op jit(solution)/shard_map/ppermute | solution.py:403
  53.3 1.4 %collective-permute-start.16 = (f32[1,8,2432]{2,1,0:T(8,128)S(1)}, f32[1,8,2432]{2,1,0:T(8,128)S(1)}, u32[]{:S(2)}, u32[]{:S(2)}) collective-permute-start(f32[1,8,2432]{2,1,0:T(8,128)S(1)} %get-tuple-element.108), channel_id=1, source_target_pairs={{0,16},{1,17},{2,18},{3,19},{4,20},{5,21},{6,22},{7,23},{8,24},{9,... | collective-permute-start | bytes 233480 | tf_op jit(solution)/shard_map/ppermute | solution.py:403
  54.7 4.2 %shard_map.83.refs_0_ = f32[256,256]{1,0:T(8,128)S(1)} custom-call(f32[256,256]{1,0:T(8,128)S(1)} %shard_map.82.refs_0_), custom_call_target="tpu_custom_call" | custom-call | flops 1000000000 | bytes 1000000 | tf_op jit(solution)/shard_map/pallas_call | solution.py:51
  58.9 0.6 collective-permute-done.16
  59.6 1.6 %collective-permute-start.19 = (f32[1,8,2432]{2,1,0:T(8,128)S(1)}, f32[1,8,2432]{2,1,0:T(8,128)S(1)}, u32[]{:S(2)}, u32[]{:S(2)}) collective-permute-start(f32[1,8,2432]{2,1,0:T(8,128)S(1)} %get-tuple-element.106), channel_id=1, source_target_pairs={{0,16},{1,17},{2,18},{3,19},{4,20},{5,21},{6,22},{7,23},{8,24},{9,... | collective-permute-start | bytes 233480 | tf_op jit(solution)/shard_map/ppermute | solution.py:403
  61.1 3.0 %shard_map.84.inverse_ref.refs_8_ = f32[256,256]{1,0:T(8,128)S(1)} custom-call(f32[256,256]{1,0:T(8,128)S(1)} %shard_map.83.refs_0_), custom_call_target="tpu_custom_call" | custom-call | flops 1000000000 | bytes 1000000 | tf_op jit(solution)/shard_map/pallas_call | solution.py:51
  64.1 0.8 %collective-permute-done.19 = f32[1,8,2432]{2,1,0:T(8,128)S(1)} collective-permute-done((f32[1,8,2432]{2,1,0:T(8,128)S(1)}, f32[1,8,2432]{2,1,0:T(8,128)S(1)}, u32[]{:S(2)}, u32[]{:S(2)}) %collective-permute-start.19) | collective-permute-done | bytes 77856 | tf_op jit(solution)/shard_map/ppermute | solution.py:403
  65.0 3.8 %collective-permute-start.20 = (f32[1,16,2432]{2,1,0:T(8,128)S(1)}, f32[1,16,2432]{2,1,0:T(8,128)S(1)}, u32[]{:S(2)}, u32[]{:S(2)}) collective-permute-start(f32[1,16,2432]{2,1,0:T(8,128)S(1)} %pad_maximum_fusion.refs_0_), channel_id=1, source_target_pairs={{0,5},{1,4},{2,7},{3,6},{4,1},{5,0},{6,3},{7,2},{8,13},{9,12},{10,... | collective-permute-start | bytes 466952 | tf_op jit(solution)/shard_map/ppermute | solution.py:403
  68.8 0.7 collective-permute-start.22
  69.5 1.4 %shard_map.85 = f32[512,256]{1,0:T(8,128)} custom-call(f32[256,512]{1,0:T(8,128)S(1)} %get-tuple-element.81.residual_ref, f32[256,256]{1,0:T(8,128)S(1)} %shard_map.84.inverse_ref.refs_8_), custom_call_target="tpu_custom_call" | custom-call | flops 1000000000 | bytes 1000000 | tf_op jit(solution)/shard_map/pallas_call | solution.py:51
  70.9 1.8 %collective-permute-done.20.refs_3_ = f32[1,16,2432]{2,1,0:T(8,128)S(1)} collective-permute-done((f32[1,16,2432]{2,1,0:T(8,128)S(1)}, f32[1,16,2432]{2,1,0:T(8,128)S(1)}, u32[]{:S(2)}, u32[]{:S(2)}) %collective-permute-start.20) | collective-permute-done | bytes 155680 | tf_op jit(solution)/shard_map/ppermute | solution.py:403
  72.7 1.6 %collective-permute-done.22.refs_2_ = f32[1,16,2432]{2,1,0:T(8,128)S(1)} collective-permute-done((f32[1,16,2432]{2,1,0:T(8,128)S(1)}, f32[1,16,2432]{2,1,0:T(8,128)S(1)}, u32[]{:S(2)}, u32[]{:S(2)}) %collective-permute-start.22) | collective-permute-done | bytes 155680 | tf_op jit(solution)/shard_map/ppermute | solution.py:403
  74.4 0.4 collective-permute-done.21.refs_1_
  74.9 0.4 collective-permute-start.26
  75.3 0.5 collective-permute-done.25.refs_6_
  75.8 0.4 collective-permute-done.24.refs_5_
  76.1 0.2 collective-permute-done.26.refs_7_
  76.3 2.6 %shard_map.86 = f32[256,1280]{1,0:T(8,128)} custom-call(s32[1]{0:T(128)} %bitcast.rank_ref, f32[1,16,2432]{2,1,0:T(8,128)S(1)} %pad_maximum_fusion.refs_0_, f32[1,16,2432]{2,1,0:T(8,128)S(1)} %collective-permute-done.21.refs_1_, f32[1,16,2432]{2,1,0:T(8,128)S(1)} %collective-permute-done.22.refs_2_, f32[1,16,2432]{2,1,0:T(8,128)S(1)} %collective-permute-done.20.refs_3_, ...), custom_call_target="tpu_custom_call" | custom-call | tf_op jit(solution)/shard_map/pallas_call | solution.py:519
  (37 shorter events, 0.9 us)
Async XLA Ops:
  0.6 6.5 %copy-start.1 = (s32[256]{0:T(256)S(1)}, s32[256]{0:T(256)}, u32[]{:S(2)}) copy-start(s32[256]{0:T(256)} %param.8) | copy-start | bytes 3076
  2.9 5.9 %collective-permute-start.1 = (bf16[18,512]{1,0:T(8,128)(2,1)S(1)}, bf16[18,512]{1,0:T(8,128)(2,1)S(1)}, u32[]{:S(2)}, u32[]{:S(2)}) collective-permute-start(bf16[18,512]{1,0:T(8,128)(2,1)S(1)} %get-tuple-element.53.refs_0_), channel_id=1, source_target_pairs={{0,16},{1,17},{2,18},{3,19},{4,20},{5,21},{6,22},{7,23},{8,24},{9,... | collective-permute-start | bytes 55304 | tf_op jit(solution)/shard_map/ppermute | solution.py:403
  7.1 5.1 %collective-permute-start = (s16[18,1024]{1,0:T(8,128)(2,1)S(1)}, s16[18,1024]{1,0:T(8,128)(2,1)S(1)}, u32[]{:S(2)}, u32[]{:S(2)}) collective-permute-start(s16[18,1024]{1,0:T(8,128)(2,1)S(1)} %get-tuple-element.52.refs_0_), channel_id=1, source_target_pairs={{0,16},{1,17},{2,18},{3,19},{4,20},{5,21},{6,22},{7,23},{8,24},{9,... | collective-permute-start | bytes 110600 | tf_op jit(solution)/shard_map/ppermute | solution.py:403
  12.2 4.5 %collective-permute-start.4 = (s16[36,1024]{1,0:T(8,128)(2,1)S(1)}, s16[36,1024]{1,0:T(8,128)(2,1)S(1)}, u32[]{:S(2)}, u32[]{:S(2)}) collective-permute-start(s16[36,1024]{1,0:T(8,128)(2,1)S(1)} %shard_map.73.refs_0_), channel_id=1, source_target_pairs={{0,8},{1,9},{2,10},{3,11},{4,12},{5,13},{6,14},{7,15},{8,0},{9,1},... | collective-permute-start | bytes 221192 | tf_op jit(solution)/shard_map/ppermute | solution.py:403
  16.7 6.2 %collective-permute-start.5 = (s16[72,1024]{1,0:T(8,128)(2,1)S(1)}, s16[72,1024]{1,0:T(8,128)(2,1)S(1)}, u32[]{:S(2)}, u32[]{:S(2)}) collective-permute-start(s16[72,1024]{1,0:T(8,128)(2,1)S(1)} %shard_map.74.refs_0_), channel_id=1, source_target_pairs={{0,4},{1,5},{2,3},{3,2},{4,0},{5,1},{6,7},{7,6},{8,12},{9,13},{10,... | collective-permute-start | bytes 442376 | tf_op jit(solution)/shard_map/ppermute | solution.py:403
  18.3 4.1 %collective-permute-start.2 = (bf16[36,512]{1,0:T(8,128)(2,1)S(1)}, bf16[36,512]{1,0:T(8,128)(2,1)S(1)}, u32[]{:S(2)}, u32[]{:S(2)}) collective-permute-start(bf16[36,512]{1,0:T(8,128)(2,1)S(1)} %shard_map.70.refs_0_), channel_id=1, source_target_pairs={{0,8},{1,9},{2,10},{3,11},{4,12},{5,13},{6,14},{7,15},{8,0},{9,1},... | collective-permute-start | bytes 110600 | tf_op jit(solution)/shard_map/ppermute | solution.py:403
  22.4 5.0 %collective-permute-start.3 = (bf16[72,512]{1,0:T(8,128)(2,1)S(1)}, bf16[72,512]{1,0:T(8,128)(2,1)S(1)}, u32[]{:S(2)}, u32[]{:S(2)}) collective-permute-start(bf16[72,512]{1,0:T(8,128)(2,1)S(1)} %shard_map.71.refs_0_), channel_id=1, source_target_pairs={{0,4},{1,5},{2,3},{3,2},{4,0},{5,1},{6,7},{7,6},{8,12},{9,13},{10,... | collective-permute-start | bytes 221192 | tf_op jit(solution)/shard_map/ppermute | solution.py:403
  23.0 5.9 %collective-permute-start.7 = (s16[144,1024]{1,0:T(8,128)(2,1)S(1)}, s16[144,1024]{1,0:T(8,128)(2,1)S(1)}, u32[]{:S(2)}, u32[]{:S(2)}) collective-permute-start(s16[144,1024]{1,0:T(8,128)(2,1)S(1)} %shard_map.75.a_h_ref), channel_id=1, source_target_pairs={{0,2},{1,3},{2,0},{3,1},{4,6},{5,7},{6,4},{7,5},{8,10},{9,11},{10,... | collective-permute-start | bytes 884744 | tf_op jit(solution)/shard_map/ppermute | solution.py:403
  23.1 6.8 %collective-permute-start.9 = (s16[144,1024]{1,0:T(8,128)(2,1)S(1)}, s16[144,1024]{1,0:T(8,128)(2,1)S(1)}, u32[]{:S(2)}, u32[]{:S(2)}) collective-permute-start(s16[144,1024]{1,0:T(8,128)(2,1)S(1)} %shard_map.75.a_h_ref), channel_id=1, source_target_pairs={{0,1},{1,0},{2,6},{3,7},{4,5},{5,4},{6,2},{7,3},{8,9},{9,8},{10,14... | collective-permute-start | bytes 884744 | tf_op jit(solution)/shard_map/ppermute | solution.py:403
  27.4 1.4 %collective-permute-start.6 = (bf16[144,512]{1,0:T(8,128)(2,1)S(1)}, bf16[144,512]{1,0:T(8,128)(2,1)S(1)}, u32[]{:S(2)}, u32[]{:S(2)}) collective-permute-start(bf16[144,512]{1,0:T(8,128)(2,1)S(1)} %shard_map.72.a_x_ref), channel_id=1, source_target_pairs={{0,2},{1,3},{2,0},{3,1},{4,6},{5,7},{6,4},{7,5},{8,10},{9,11},{10,... | collective-permute-start | bytes 442376 | tf_op jit(solution)/shard_map/ppermute | solution.py:403
  29.9 2.3 %collective-permute-start.10 = (s16[144,1024]{1,0:T(8,128)(2,1)S(1)}, s16[144,1024]{1,0:T(8,128)(2,1)S(1)}, u32[]{:S(2)}, u32[]{:S(2)}) collective-permute-start(s16[144,1024]{1,0:T(8,128)(2,1)S(1)} %collective-permute-done.9.h_ref), channel_id=1, source_target_pairs={{0,2},{1,3},{2,0},{3,1},{4,6},{5,7},{6,4},{7,5},{8,10},{9,11},{10,... | collective-permute-start | bytes 884744 | tf_op jit(solution)/shard_map/ppermute | solution.py:403
  30.1 5.1 %collective-permute-start.8 = (bf16[144,512]{1,0:T(8,128)(2,1)S(1)}, bf16[144,512]{1,0:T(8,128)(2,1)S(1)}, u32[]{:S(2)}, u32[]{:S(2)}) collective-permute-start(bf16[144,512]{1,0:T(8,128)(2,1)S(1)} %shard_map.72.a_x_ref), channel_id=1, source_target_pairs={{0,1},{1,0},{2,6},{3,7},{4,5},{5,4},{6,2},{7,3},{8,9},{9,8},{10,14... | collective-permute-start | bytes 442376 | tf_op jit(solution)/shard_map/ppermute | solution.py:403
  32.7 3.9 %copy-start = (f32[512]{0:T(512)S(1)}, f32[512]{0:T(512)}, u32[]{:S(2)}) copy-start(f32[512]{0:T(512)} %param.7) | copy-start | bytes 6148
  35.2 1.4 %collective-permute-start.11 = (bf16[144,512]{1,0:T(8,128)(2,1)S(1)}, bf16[144,512]{1,0:T(8,128)(2,1)S(1)}, u32[]{:S(2)}, u32[]{:S(2)}) collective-permute-start(bf16[144,512]{1,0:T(8,128)(2,1)S(1)} %collective-permute-done.8.b_x_ref), channel_id=1, source_target_pairs={{0,2},{1,3},{2,0},{3,1},{4,6},{5,7},{6,4},{7,5},{8,10},{9,11},{10,... | collective-permute-start | bytes 442376 | tf_op jit(solution)/shard_map/ppermute | solution.py:403
  38.9 2.1 %collective-permute-start.12 = (f32[4,16,2432]{2,1,0:T(8,128)S(1)}, f32[4,16,2432]{2,1,0:T(8,128)S(1)}, u32[]{:S(2)}, u32[]{:S(2)}) collective-permute-start(f32[4,16,2432]{2,1,0:T(8,128)S(1)} %get-tuple-element.82), channel_id=1, source_target_pairs={{0,2},{1,3},{2,0},{3,1},{4,6},{5,7},{6,4},{7,5},{8,10},{9,11},{10,... | collective-permute-start | bytes 1867784 | tf_op jit(solution)/shard_map/ppermute | solution.py:403
  41.1 8.8 %collective-permute-start.15 = (f32[1,16,2432]{2,1,0:T(8,128)S(1)}, f32[1,16,2432]{2,1,0:T(8,128)S(1)}, u32[]{:S(2)}, u32[]{:S(2)}) collective-permute-start(f32[1,16,2432]{2,1,0:T(8,128)S(1)} %get-tuple-element.102), channel_id=1, source_target_pairs={{0,4},{1,5},{2,3},{3,2},{4,0},{5,1},{6,7},{7,6},{8,12},{9,13},{10,... | collective-permute-start | bytes 466952 | tf_op jit(solution)/shard_map/ppermute | solution.py:403
  42.4 7.5 %collective-permute-start.14 = (f32[1,16,2432]{2,1,0:T(8,128)S(1)}, f32[1,16,2432]{2,1,0:T(8,128)S(1)}, u32[]{:S(2)}, u32[]{:S(2)}) collective-permute-start(f32[1,16,2432]{2,1,0:T(8,128)S(1)} %get-tuple-element.103), channel_id=1, source_target_pairs={{0,1},{1,0},{2,6},{3,7},{4,5},{5,4},{6,2},{7,3},{8,9},{9,8},{10,14... | collective-permute-start | bytes 466952 | tf_op jit(solution)/shard_map/ppermute | solution.py:403
  43.9 7.8 %collective-permute-start.13 = (f32[1,16,2432]{2,1,0:T(8,128)S(1)}, f32[1,16,2432]{2,1,0:T(8,128)S(1)}, u32[]{:S(2)}, u32[]{:S(2)}) collective-permute-start(f32[1,16,2432]{2,1,0:T(8,128)S(1)} %get-tuple-element.104), channel_id=1, source_target_pairs={{0,5},{1,4},{2,7},{3,6},{4,1},{5,0},{6,3},{7,2},{8,13},{9,12},{10,... | collective-permute-start | bytes 466952 | tf_op jit(solution)/shard_map/ppermute | solution.py:403
  51.8 7.0 %collective-permute-start.17 = (f32[1,8,2432]{2,1,0:T(8,128)S(1)}, f32[1,8,2432]{2,1,0:T(8,128)S(1)}, u32[]{:S(2)}, u32[]{:S(2)}) collective-permute-start(f32[1,8,2432]{2,1,0:T(8,128)S(1)} %get-tuple-element.107), channel_id=1, source_target_pairs={{0,8},{1,9},{2,10},{3,11},{4,12},{5,13},{6,14},{7,15},{8,0},{9,1},... | collective-permute-start | bytes 233480 | tf_op jit(solution)/shard_map/ppermute | solution.py:403
  53.3 6.1 %collective-permute-start.16 = (f32[1,8,2432]{2,1,0:T(8,128)S(1)}, f32[1,8,2432]{2,1,0:T(8,128)S(1)}, u32[]{:S(2)}, u32[]{:S(2)}) collective-permute-start(f32[1,8,2432]{2,1,0:T(8,128)S(1)} %get-tuple-element.108), channel_id=1, source_target_pairs={{0,16},{1,17},{2,18},{3,19},{4,20},{5,21},{6,22},{7,23},{8,24},{9,... | collective-permute-start | bytes 233480 | tf_op jit(solution)/shard_map/ppermute | solution.py:403
  59.5 4.6 %collective-permute-start.18 = (f32[1,8,2432]{2,1,0:T(8,128)S(1)}, f32[1,8,2432]{2,1,0:T(8,128)S(1)}, u32[]{:S(2)}, u32[]{:S(2)}) collective-permute-start(f32[1,8,2432]{2,1,0:T(8,128)S(1)} %get-tuple-element.105), channel_id=1, source_target_pairs={{0,8},{1,9},{2,10},{3,11},{4,12},{5,13},{6,14},{7,15},{8,0},{9,1},... | collective-permute-start | bytes 233480 | tf_op jit(solution)/shard_map/ppermute | solution.py:403
  59.6 5.4 %collective-permute-start.19 = (f32[1,8,2432]{2,1,0:T(8,128)S(1)}, f32[1,8,2432]{2,1,0:T(8,128)S(1)}, u32[]{:S(2)}, u32[]{:S(2)}) collective-permute-start(f32[1,8,2432]{2,1,0:T(8,128)S(1)} %get-tuple-element.106), channel_id=1, source_target_pairs={{0,16},{1,17},{2,18},{3,19},{4,20},{5,21},{6,22},{7,23},{8,24},{9,... | collective-permute-start | bytes 233480 | tf_op jit(solution)/shard_map/ppermute | solution.py:403
  65.0 7.8 %collective-permute-start.20 = (f32[1,16,2432]{2,1,0:T(8,128)S(1)}, f32[1,16,2432]{2,1,0:T(8,128)S(1)}, u32[]{:S(2)}, u32[]{:S(2)}) collective-permute-start(f32[1,16,2432]{2,1,0:T(8,128)S(1)} %pad_maximum_fusion.refs_0_), channel_id=1, source_target_pairs={{0,5},{1,4},{2,7},{3,6},{4,1},{5,0},{6,3},{7,2},{8,13},{9,12},{10,... | collective-permute-start | bytes 466952 | tf_op jit(solution)/shard_map/ppermute | solution.py:403
  68.8 5.6 %collective-permute-start.22 = (f32[1,16,2432]{2,1,0:T(8,128)S(1)}, f32[1,16,2432]{2,1,0:T(8,128)S(1)}, u32[]{:S(2)}, u32[]{:S(2)}) collective-permute-start(f32[1,16,2432]{2,1,0:T(8,128)S(1)} %pad_maximum_fusion.refs_0_), channel_id=1, source_target_pairs={{0,4},{1,5},{2,3},{3,2},{4,0},{5,1},{6,7},{7,6},{8,12},{9,13},{10,... | collective-permute-start | bytes 466952 | tf_op jit(solution)/shard_map/ppermute | solution.py:403
  69.5 5.2 %collective-permute-start.21 = (f32[1,16,2432]{2,1,0:T(8,128)S(1)}, f32[1,16,2432]{2,1,0:T(8,128)S(1)}, u32[]{:S(2)}, u32[]{:S(2)}) collective-permute-start(f32[1,16,2432]{2,1,0:T(8,128)S(1)} %pad_maximum_fusion.refs_0_), channel_id=1, source_target_pairs={{0,1},{1,0},{2,6},{3,7},{4,5},{5,4},{6,2},{7,3},{8,9},{9,8},{10,14... | collective-permute-start | bytes 466952 | tf_op jit(solution)/shard_map/ppermute | solution.py:403
  69.5 5.7 %collective-permute-start.23 = (f32[1,16,2432]{2,1,0:T(8,128)S(1)}, f32[1,16,2432]{2,1,0:T(8,128)S(1)}, u32[]{:S(2)}, u32[]{:S(2)}) collective-permute-start(f32[1,16,2432]{2,1,0:T(8,128)S(1)} %pad_maximum_fusion.refs_0_), channel_id=1, source_target_pairs={{0,2},{1,3},{2,0},{3,1},{4,6},{5,7},{6,4},{7,5},{8,10},{9,11},{10,... | collective-permute-start | bytes 466952 | tf_op jit(solution)/shard_map/ppermute | solution.py:403
  74.4 1.4 %collective-permute-start.25 = (f32[1,16,2432]{2,1,0:T(8,128)S(1)}, f32[1,16,2432]{2,1,0:T(8,128)S(1)}, u32[]{:S(2)}, u32[]{:S(2)}) collective-permute-start(f32[1,16,2432]{2,1,0:T(8,128)S(1)} %collective-permute-done.22.refs_2_), channel_id=1, source_target_pairs={{0,2},{1,3},{2,0},{3,1},{4,6},{5,7},{6,4},{7,5},{8,10},{9,11},{10,... | collective-permute-start | bytes 466952 | tf_op jit(solution)/shard_map/ppermute | solution.py:403
  74.7 1.4 %collective-permute-start.24 = (f32[1,16,2432]{2,1,0:T(8,128)S(1)}, f32[1,16,2432]{2,1,0:T(8,128)S(1)}, u32[]{:S(2)}, u32[]{:S(2)}) collective-permute-start(f32[1,16,2432]{2,1,0:T(8,128)S(1)} %collective-permute-done.21.refs_1_), channel_id=1, source_target_pairs={{0,2},{1,3},{2,0},{3,1},{4,6},{5,7},{6,4},{7,5},{8,10},{9,11},{10,... | collective-permute-start | bytes 466952 | tf_op jit(solution)/shard_map/ppermute | solution.py:403
  74.9 1.4 %collective-permute-start.26 = (f32[1,16,2432]{2,1,0:T(8,128)S(1)}, f32[1,16,2432]{2,1,0:T(8,128)S(1)}, u32[]{:S(2)}, u32[]{:S(2)}) collective-permute-start(f32[1,16,2432]{2,1,0:T(8,128)S(1)} %collective-permute-done.20.refs_3_), channel_id=1, source_target_pairs={{0,2},{1,3},{2,0},{3,1},{4,6},{5,7},{6,4},{7,5},{8,10},{9,11},{10,... | collective-permute-start | bytes 466952 | tf_op jit(solution)/shard_map/ppermute | solution.py:403

commit v3 on v2

--- a/solution.py
+++ b/solution.py
@@ -134,15 +134,16 @@
         slot_rank = jnp.sum(jnp.where(owned, counts, 0.0), axis=0, keepdims=True).astype(i32)
         apart = owner ^ rank_ref[0]
         bit = lambda mask: (apart >> (mask.bit_length() - 1)) & 1
-        place = jnp.zeros_like(apart)
-        for k, mask in enumerate(others):
-            place = place + (bit(mask) << k)
         at = len(others)
         low_core = (owner & core) == 0
         lead = jnp.where(low_core, bit(side), bit(col_low))
         trail = jnp.where(low_core, bit(col_low), bit(side))
-        place = place + (lead << at) + (trail << (at + 1)) + (bit(core) << (at + 2))
-        source_ref[...] = place * slots + slot_rank
+        outer = (lead << at) + (trail << (at + 1)) + (bit(core) << (at + 2))
+        for row, chain in enumerate((others, others[::-1])):
+            place = outer
+            for k, mask in enumerate(chain):
+                place = place + (bit(mask) << k)
+            source_ref[row : row + 1, :] = place * slots + slot_rank
         high, low = split(factor_ref[...])
         high_ref[...] = high
         low_ref[...] = low
@@ -199,6 +200,10 @@
     return onehot(iota((held, source.shape[1]), 0) == source - start)
 
 
+def source_of(source_ref):
+    return source_ref[0:1, :], source_ref[1:2, :]
+
+
 def ordered_h(source, start, h_ref):
     chosen = chosen_rows(source, start, h_ref.shape[0])
     q = h_ref[...].astype(i32)
@@ -215,9 +220,9 @@
 
 def order_kernel(source_ref, a_x_ref, a_h_ref, c_x_ref, c_h_ref, x_ref, coarse_ref, fine_ref):
     held = a_x_ref.shape[0]
-    source = source_ref[...]
+    source, source_x = source_of(source_ref)
     x_ref[...] = (
-        ordered_x(source, 0, a_x_ref) + ordered_x(source, 2 * held, c_x_ref)
+        ordered_x(source_x, 0, a_x_ref) + ordered_x(source_x, 2 * held, c_x_ref)
     ).astype(bf16)
     one, two = ordered_h(source, 0, a_h_ref), ordered_h(source, 2 * held, c_h_ref)
     coarse_ref[...] = (one[0] + two[0]).astype(bf16)
@@ -225,7 +230,7 @@
 
 
 def across_kernel(place, source_ref, h_ref, coarse_in, fine_in, coarse_ref, fine_ref):
-    coarse, fine = ordered_h(source_ref[...], place * h_ref.shape[0], h_ref)
+    coarse, fine = ordered_h(source_of(source_ref)[0], place * h_ref.shape[0], h_ref)
     coarse_ref[...] = (coarse_in[...].astype(f32) + coarse).astype(bf16)
     fine_ref[...] = (fine_in[...].astype(f32) + fine).astype(bf16)
 
@@ -240,7 +245,7 @@
     features_ref, high_ref, low_ref, norm_ref, weights_ref, pivot_ref, residual_ref, send_ref,
 ):
     held, width = b_x_ref.shape
-    source = source_ref[...]
+    source = source_of(source_ref)[1]
     new = ordered_x(source, held, b_x_ref) + ordered_x(source, 3 * held, d_x_ref)
     pivot_x = (new + x_ref[...].astype(f32)).astype(bf16)
     pivot_ref[...] = pivot_x
@@ -436,14 +441,15 @@
 
     prepared = False
     perms = [pair(mask) for mask in others] + [first_pair]
-    for perm in perms:
+    perms_x = [pair(mask) for mask in others[::-1]] + [first_pair]
+    for perm, perm_x in zip(perms, perms_x):
         got_h = near(move(held_h, perm))
-        got_x = near(move(held_x, perm))
+        got_x = near(move(held_x, perm_x))
         if not prepared:
             source, norm, high, low = call(
                 prepare_kernel(core, side, col_low, others, slots, devices),
                 (
-                    pltpu.VMEM((1, pivots), i32),
+                    pltpu.VMEM((2, pivots), i32),
                     pltpu.VMEM((1, rows), f32),
                     pltpu.VMEM((rows, depth), bf16),
                     pltpu.VMEM((rows, depth), bf16),

time: 79.3 us -> 80.1 us (1.010)
  starting transfers between devices: 26.2 us -> 27.8 us
    ppermute x27, starting transfers between devices: 26.2 us -> 27.8 us  [move(): return lax.ppermute(value, axes, perm)]
  transfers between devices with their start and end apart: 27 -> 27, of which waited for: 18 -> 16; matrix products, arithmetic and copies ran while one was open for 0% -> 0% of each run, Pallas kernels for 25% -> 25%
where the time goes in v3:
time: 80.1 us; the launch traced here: 80 us
  starting transfers between devices  27.8 us (35%)
  Pallas kernels  27 us (34%)
  waiting for transfers between devices  23.9 us (30%)
  between operations  1.04 us (1%)
    ppermute x27, starting transfers between devices, move(): return lax.ppermute(value, axes, perm)  27.8 us
    ppermute x27, waiting for transfers between devices, move(): return lax.ppermute(value, axes, perm)  23.9 us
    pallas_call x17, Pallas kernels, call(): pl.pallas_call(kernel, out_shape=outs, in_specs=specs, out_specs=jax.tree...  22 us
    pallas_call x1, Pallas kernels, body(): pl.pallas_call(partial(rows_kernel, masks), out_shape=jax.ShapeDtypeStruc...  2.63 us
    pallas_call x1, Pallas kernels, body(): pl.pallas_call(pick_kernel, out_shape=(pltpu.VMEM((slots, width), bf16),...  2.29 us
  transfers between devices with their start and end apart: 27, of which 16 were waited for; matrix products, arithmetic and copies ran while one was open for 0% of the time, Pallas kernels for 25%

profile of v3, /device:TPU:0, one launch (start us, length us, event | category | flops | bytes accessed | tf_op | source)
XLA Modules:
  0.0 80.0 jit_solution(16076127250426365358)
XLA Ops:
  0.6 2.3 %shard_map.68 = (bf16[18,512]{1,0:T(8,128)(2,1)S(1)}, s16[18,1024]{1,0:T(8,128)(2,1)S(1)}, bf16[512,512]{1,0:T(8,128)(2,1)S(1)}, f32[512,1024]{1,0:T(8,128)S(1)}) custom-call(s32[1]{0:T(128)} %bitcast.rank_ref, s32[1,256]{1,0:T(1,128)} %bitcast.6, s32[1,256]{1,0:T(1,128)} %bitcast.8, bf16[512,512]{1,0:T(8,128)(2,1)} %features_ref.1, f32[512,1024]{1,0:T(8,128)} %factor_ref.1), custom_call_target="tpu_custom_call" | custom-call | tf_op jit(solution)/shard_map/pallas_call | solution.py:416
  2.9 3.1 %collective-permute-start.1 = (bf16[18,512]{1,0:T(8,128)(2,1)S(1)}, bf16[18,512]{1,0:T(8,128)(2,1)S(1)}, u32[]{:S(2)}, u32[]{:S(2)}) collective-permute-start(bf16[18,512]{1,0:T(8,128)(2,1)S(1)} %get-tuple-element.53.refs_0_), channel_id=1, source_target_pairs={{0,8},{1,9},{2,10},{3,11},{4,12},{5,13},{6,14},{7,15},{8,0},{9,1},... | collective-permute-start | bytes 55304 | tf_op jit(solution)/shard_map/ppermute | solution.py:408
  6.1 2.6 %collective-permute-start = (s16[18,1024]{1,0:T(8,128)(2,1)S(1)}, s16[18,1024]{1,0:T(8,128)(2,1)S(1)}, u32[]{:S(2)}, u32[]{:S(2)}) collective-permute-start(s16[18,1024]{1,0:T(8,128)(2,1)S(1)} %get-tuple-element.52.refs_0_), channel_id=1, source_target_pairs={{0,16},{1,17},{2,18},{3,19},{4,20},{5,21},{6,22},{7,23},{8,24},{9,... | collective-permute-start | bytes 110600 | tf_op jit(solution)/shard_map/ppermute | solution.py:408
  8.7 1.6 %shard_map.69 = (s32[2,256]{1,0:T(2,128)S(1)}, f32[1,512]{1,0:T(1,128)S(1)}, bf16[512,1024]{1,0:T(8,128)(2,1)S(1)}, bf16[512,1024]{1,0:T(8,128)(2,1)S(1)}) custom-call(s32[1]{0:T(128)} %bitcast.rank_ref, s32[1,256]{1,0:T(1,128)S(1)} %bitcast.7, bf16[512,512]{1,0:T(8,128)(2,1)S(1)} %get-tuple-element.54.features_ref, f32[512,1024]{1,0:T(8,128)S(1)} %get-tuple-element.55.factor_ref), custom_call_target="tpu_custom_call" | custom-call | flops 1000000000 | bytes 1000000 | tf_op jit(solution)/shard_map/pallas_call | solution.py:51
  10.3 1.1 %collective-permute-done.refs_1_ = s16[18,1024]{1,0:T(8,128)(2,1)S(1)} collective-permute-done((s16[18,1024]{1,0:T(8,128)(2,1)S(1)}, s16[18,1024]{1,0:T(8,128)(2,1)S(1)}, u32[]{:S(2)}, u32[]{:S(2)}) %collective-permute-start) | collective-permute-done | bytes 36896 | tf_op jit(solution)/shard_map/ppermute | solution.py:408
  11.5 4.4 %collective-permute-done.4.refs_1_ = s16[36,1024]{1,0:T(8,128)(2,1)S(1)} collective-permute-done((s16[36,1024]{1,0:T(8,128)(2,1)S(1)}, s16[36,1024]{1,0:T(8,128)(2,1)S(1)}, u32[]{:S(2)}, u32[]{:S(2)}) %collective-permute-start.4) | collective-permute-done | bytes 73760 | tf_op jit(solution)/shard_map/ppermute | solution.py:408
  15.9 1.6 %collective-permute-start.5 = (s16[72,1024]{1,0:T(8,128)(2,1)S(1)}, s16[72,1024]{1,0:T(8,128)(2,1)S(1)}, u32[]{:S(2)}, u32[]{:S(2)}) collective-permute-start(s16[72,1024]{1,0:T(8,128)(2,1)S(1)} %shard_map.74.refs_0_), channel_id=1, source_target_pairs={{0,4},{1,5},{2,3},{3,2},{4,0},{5,1},{6,7},{7,6},{8,12},{9,13},{10,... | collective-permute-start | bytes 442376 | tf_op jit(solution)/shard_map/ppermute | solution.py:408
  17.6 2.2 %collective-permute-start.2 = (bf16[36,512]{1,0:T(8,128)(2,1)S(1)}, bf16[36,512]{1,0:T(8,128)(2,1)S(1)}, u32[]{:S(2)}, u32[]{:S(2)}) collective-permute-start(bf16[36,512]{1,0:T(8,128)(2,1)S(1)} %shard_map.70.refs_0_), channel_id=1, source_target_pairs={{0,16},{1,17},{2,18},{3,19},{4,20},{5,21},{6,22},{7,23},{8,24},{9,... | collective-permute-start | bytes 110600 | tf_op jit(solution)/shard_map/ppermute | solution.py:408
  19.8 2.7 %collective-permute-done.2.refs_1_ = bf16[36,512]{1,0:T(8,128)(2,1)S(1)} collective-permute-done((bf16[36,512]{1,0:T(8,128)(2,1)S(1)}, bf16[36,512]{1,0:T(8,128)(2,1)S(1)}, u32[]{:S(2)}, u32[]{:S(2)}) %collective-permute-start.2) | collective-permute-done | bytes 36896 | tf_op jit(solution)/shard_map/ppermute | solution.py:408
  22.5 0.5 collective-permute-start.3
  23.2 1.7 %collective-permute-start.9 = (s16[144,1024]{1,0:T(8,128)(2,1)S(1)}, s16[144,1024]{1,0:T(8,128)(2,1)S(1)}, u32[]{:S(2)}, u32[]{:S(2)}) collective-permute-start(s16[144,1024]{1,0:T(8,128)(2,1)S(1)} %shard_map.75.a_h_ref), channel_id=1, source_target_pairs={{0,1},{1,0},{2,6},{3,7},{4,5},{5,4},{6,2},{7,3},{8,9},{9,8},{10,14... | collective-permute-start | bytes 884744 | tf_op jit(solution)/shard_map/ppermute | solution.py:408
  24.8 2.8 %collective-permute-done.3.refs_1_ = bf16[72,512]{1,0:T(8,128)(2,1)S(1)} collective-permute-done((bf16[72,512]{1,0:T(8,128)(2,1)S(1)}, bf16[72,512]{1,0:T(8,128)(2,1)S(1)}, u32[]{:S(2)}, u32[]{:S(2)}) %collective-permute-start.3) | collective-permute-done | bytes 73760 | tf_op jit(solution)/shard_map/ppermute | solution.py:408
  27.8 1.4 %collective-permute-done.6.c_x_ref = bf16[144,512]{1,0:T(8,128)(2,1)S(1)} collective-permute-done((bf16[144,512]{1,0:T(8,128)(2,1)S(1)}, bf16[144,512]{1,0:T(8,128)(2,1)S(1)}, u32[]{:S(2)}, u32[]{:S(2)}) %collective-permute-start.6) | collective-permute-done | bytes 147488 | tf_op jit(solution)/shard_map/ppermute | solution.py:408
  29.1 1.0 %shard_map.76 = (bf16[256,512]{1,0:T(8,128)(2,1)S(1)}, bf16[256,1024]{1,0:T(8,128)(2,1)S(1)}, bf16[256,1024]{1,0:T(8,128)(2,1)S(1)}) custom-call(s32[2,256]{1,0:T(2,128)S(1)} %get-tuple-element.60.source_ref, bf16[144,512]{1,0:T(8,128)(2,1)S(1)} %shard_map.72.a_x_ref, s16[144,1024]{1,0:T(8,128)(2,1)S(1)} %shard_map.75.a_h_ref, ...), custom_call_target="tpu_custom_call" | custom-call | flops 1000000000 | bytes 1000000 | tf_op jit(solution)/shard_map/pallas_call | solution.py:51
  30.1 0.2 collective-permute-start.10
  30.4 1.5 %collective-permute-start.8 = (bf16[144,512]{1,0:T(8,128)(2,1)S(1)}, bf16[144,512]{1,0:T(8,128)(2,1)S(1)}, u32[]{:S(2)}, u32[]{:S(2)}) collective-permute-start(bf16[144,512]{1,0:T(8,128)(2,1)S(1)} %shard_map.72.a_x_ref), channel_id=1, source_target_pairs={{0,1},{1,0},{2,6},{3,7},{4,5},{5,4},{6,2},{7,3},{8,9},{9,8},{10,14... | collective-permute-start | bytes 442376 | tf_op jit(solution)/shard_map/ppermute | solution.py:408
  31.8 0.5 shard_map.77
  32.4 0.5 shard_map.78
  32.9 2.6 %collective-permute-done.8.b_x_ref = bf16[144,512]{1,0:T(8,128)(2,1)S(1)} collective-permute-done((bf16[144,512]{1,0:T(8,128)(2,1)S(1)}, bf16[144,512]{1,0:T(8,128)(2,1)S(1)}, u32[]{:S(2)}, u32[]{:S(2)}) %collective-permute-start.8) | collective-permute-done | bytes 147488 | tf_op jit(solution)/shard_map/ppermute | solution.py:408
  35.5 1.0 %shard_map.79.product_ref = f32[256,512]{1,0:T(8,128)S(1)} custom-call(bf16[256,1024]{1,0:T(8,128)(2,1)S(1)} %get-tuple-element.86.coarse_ref.refs_1_, bf16[256,1024]{1,0:T(8,128)(2,1)S(1)} %get-tuple-element.87.fine_ref.refs_2_, bf16[512,1024]{1,0:T(8,128)(2,1)S(1)} %get-tuple-element.76.high_ref, bf16[512,1024]{1,0:T(8,128)(2,1)S(1)} %get-tuple-element.77.low_ref), custom_call_target="tpu_custom_call" | custom-call | flops 1000000000 | bytes 1000000 | tf_op jit(solution)/shard_map/pallas_call | solution.py:51
  36.5 0.4 collective-permute-done.11.d_x_ref
  36.9 2.2 %shard_map.80 = (bf16[256,512]{1,0:T(8,128)(2,1)S(1)}, f32[256,512]{1,0:T(8,128)S(1)}, f32[4,16,2432]{2,1,0:T(8,128)S(1)}) custom-call(s32[1]{0:T(128)} %bitcast.rank_ref, s32[2,256]{1,0:T(2,128)S(1)} %get-tuple-element.60.source_ref, bf16[256,512]{1,0:T(8,128)(2,1)S(1)} %get-tuple-element.63.x_ref, bf16[144,512]{1,0:T(8,128)(2,1)S(1)} %collective-permute-done.8.b_x_ref, ...), custom_call_target="tpu_custom_call" | custom-call | flops 1000000000 | bytes 1000000 | tf_op jit(solution)/shard_map/pallas_call | solution.py:51
  39.1 0.2 collective-permute-start.12
  39.3 1.3 %shard_map.81 = f32[4,16,2432]{2,1,0:T(8,128)S(1)} custom-call(s32[1]{0:T(128)} %bitcast.rank_ref, f32[256,512]{1,0:T(8,128)S(1)} %get-tuple-element.81.residual_ref, bf16[512,1024]{1,0:T(8,128)(2,1)S(1)} %get-tuple-element.76.high_ref, bf16[512,1024]{1,0:T(8,128)(2,1)S(1)} %get-tuple-element.77.low_ref, f32[1,512]{1,0:T(1,128)S(1)} %bitcast.5), custom_call_target="tpu_custom_call" | custom-call | flops 1000000000 | bytes 1000000 | tf_op jit(solution)/shard_map/pallas_call | solution.py:51
  40.6 0.6 collective-permute-done.12
  41.4 1.3 %collective-permute-start.15 = (f32[1,16,2432]{2,1,0:T(8,128)S(1)}, f32[1,16,2432]{2,1,0:T(8,128)S(1)}, u32[]{:S(2)}, u32[]{:S(2)}) collective-permute-start(f32[1,16,2432]{2,1,0:T(8,128)S(1)} %get-tuple-element.102), channel_id=1, source_target_pairs={{0,4},{1,5},{2,3},{3,2},{4,0},{5,1},{6,7},{7,6},{8,12},{9,13},{10,... | collective-permute-start | bytes 466952 | tf_op jit(solution)/shard_map/ppermute | solution.py:408
  42.6 1.5 %collective-permute-start.14 = (f32[1,16,2432]{2,1,0:T(8,128)S(1)}, f32[1,16,2432]{2,1,0:T(8,128)S(1)}, u32[]{:S(2)}, u32[]{:S(2)}) collective-permute-start(f32[1,16,2432]{2,1,0:T(8,128)S(1)} %get-tuple-element.103), channel_id=1, source_target_pairs={{0,1},{1,0},{2,6},{3,7},{4,5},{5,4},{6,2},{7,3},{8,9},{9,8},{10,14... | collective-permute-start | bytes 466952 | tf_op jit(solution)/shard_map/ppermute | solution.py:408
  44.1 0.8 collective-permute-start.13
  44.9 5.3 %shard_map.82.refs_0_ = f32[256,256]{1,0:T(8,128)S(1)} custom-call(bf16[256,512]{1,0:T(8,128)(2,1)S(1)} %get-tuple-element.85.refs_0_, bf16[256,1024]{1,0:T(8,128)(2,1)S(1)} %get-tuple-element.86.coarse_ref.refs_1_, bf16[256,1024]{1,0:T(8,128)(2,1)S(1)} %get-tuple-element.87.fine_ref.refs_2_), custom_call_target="tpu_custom_call" | custom-call | flops 1000000000 | bytes 1000000 | tf_op jit(solution)/shard_map/pallas_call | solution.py:51
  50.2 1.8 %collective-permute-done.13 = f32[1,16,2432]{2,1,0:T(8,128)S(1)} collective-permute-done((f32[1,16,2432]{2,1,0:T(8,128)S(1)}, f32[1,16,2432]{2,1,0:T(8,128)S(1)}, u32[]{:S(2)}, u32[]{:S(2)}) %collective-permute-start.13) | collective-permute-done | bytes 155680 | tf_op jit(solution)/shard_map/ppermute | solution.py:408
  52.3 2.6 %collective-permute-start.16 = (f32[1,8,2432]{2,1,0:T(8,128)S(1)}, f32[1,8,2432]{2,1,0:T(8,128)S(1)}, u32[]{:S(2)}, u32[]{:S(2)}) collective-permute-start(f32[1,8,2432]{2,1,0:T(8,128)S(1)} %get-tuple-element.108), channel_id=1, source_target_pairs={{0,16},{1,17},{2,18},{3,19},{4,20},{5,21},{6,22},{7,23},{8,24},{9,... | collective-permute-start | bytes 233480 | tf_op jit(solution)/shard_map/ppermute | solution.py:408
  54.8 4.2 %shard_map.83.refs_0_ = f32[256,256]{1,0:T(8,128)S(1)} custom-call(f32[256,256]{1,0:T(8,128)S(1)} %shard_map.82.refs_0_), custom_call_target="tpu_custom_call" | custom-call | flops 1000000000 | bytes 1000000 | tf_op jit(solution)/shard_map/pallas_call | solution.py:51
  59.0 1.8 %collective-permute-start.18 = (f32[1,8,2432]{2,1,0:T(8,128)S(1)}, f32[1,8,2432]{2,1,0:T(8,128)S(1)}, u32[]{:S(2)}, u32[]{:S(2)}) collective-permute-start(f32[1,8,2432]{2,1,0:T(8,128)S(1)} %get-tuple-element.105), channel_id=1, source_target_pairs={{0,8},{1,9},{2,10},{3,11},{4,12},{5,13},{6,14},{7,15},{8,0},{9,1},... | collective-permute-start | bytes 233480 | tf_op jit(solution)/shard_map/ppermute | solution.py:408
  60.9 1.7 %collective-permute-start.19 = (f32[1,8,2432]{2,1,0:T(8,128)S(1)}, f32[1,8,2432]{2,1,0:T(8,128)S(1)}, u32[]{:S(2)}, u32[]{:S(2)}) collective-permute-start(f32[1,8,2432]{2,1,0:T(8,128)S(1)} %get-tuple-element.106), channel_id=1, source_target_pairs={{0,16},{1,17},{2,18},{3,19},{4,20},{5,21},{6,22},{7,23},{8,24},{9,... | collective-permute-start | bytes 233480 | tf_op jit(solution)/shard_map/ppermute | solution.py:408
  62.5 3.0 %shard_map.84.inverse_ref.refs_8_ = f32[256,256]{1,0:T(8,128)S(1)} custom-call(f32[256,256]{1,0:T(8,128)S(1)} %shard_map.83.refs_0_), custom_call_target="tpu_custom_call" | custom-call | flops 1000000000 | bytes 1000000 | tf_op jit(solution)/shard_map/pallas_call | solution.py:51
  65.5 1.2 %collective-permute-done.19 = f32[1,8,2432]{2,1,0:T(8,128)S(1)} collective-permute-done((f32[1,8,2432]{2,1,0:T(8,128)S(1)}, f32[1,8,2432]{2,1,0:T(8,128)S(1)}, u32[]{:S(2)}, u32[]{:S(2)}) %collective-permute-start.19) | collective-permute-done | bytes 77856 | tf_op jit(solution)/shard_map/ppermute | solution.py:408
  66.8 2.0 %collective-permute-start.20 = (f32[1,16,2432]{2,1,0:T(8,128)S(1)}, f32[1,16,2432]{2,1,0:T(8,128)S(1)}, u32[]{:S(2)}, u32[]{:S(2)}) collective-permute-start(f32[1,16,2432]{2,1,0:T(8,128)S(1)} %pad_maximum_fusion.refs_0_), channel_id=1, source_target_pairs={{0,5},{1,4},{2,7},{3,6},{4,1},{5,0},{6,3},{7,2},{8,13},{9,12},{10,... | collective-permute-start | bytes 466952 | tf_op jit(solution)/shard_map/ppermute | solution.py:408
  68.7 1.0 %collective-permute-start.22 = (f32[1,16,2432]{2,1,0:T(8,128)S(1)}, f32[1,16,2432]{2,1,0:T(8,128)S(1)}, u32[]{:S(2)}, u32[]{:S(2)}) collective-permute-start(f32[1,16,2432]{2,1,0:T(8,128)S(1)} %pad_maximum_fusion.refs_0_), channel_id=1, source_target_pairs={{0,4},{1,5},{2,3},{3,2},{4,0},{5,1},{6,7},{7,6},{8,12},{9,13},{10,... | collective-permute-start | bytes 466952 | tf_op jit(solution)/shard_map/ppermute | solution.py:408
  69.7 0.6 collective-permute-start.21
  70.3 1.4 %shard_map.85 = f32[512,256]{1,0:T(8,128)} custom-call(f32[256,512]{1,0:T(8,128)S(1)} %get-tuple-element.81.residual_ref, f32[256,256]{1,0:T(8,128)S(1)} %shard_map.84.inverse_ref.refs_8_), custom_call_target="tpu_custom_call" | custom-call | flops 1000000000 | bytes 1000000 | tf_op jit(solution)/shard_map/pallas_call | solution.py:51
  71.7 2.3 %collective-permute-done.20.refs_3_ = f32[1,16,2432]{2,1,0:T(8,128)S(1)} collective-permute-done((f32[1,16,2432]{2,1,0:T(8,128)S(1)}, f32[1,16,2432]{2,1,0:T(8,128)S(1)}, u32[]{:S(2)}, u32[]{:S(2)}) %collective-permute-start.20) | collective-permute-done | bytes 155680 | tf_op jit(solution)/shard_map/ppermute | solution.py:408
  74.0 1.0 %collective-permute-done.22.refs_2_ = f32[1,16,2432]{2,1,0:T(8,128)S(1)} collective-permute-done((f32[1,16,2432]{2,1,0:T(8,128)S(1)}, f32[1,16,2432]{2,1,0:T(8,128)S(1)}, u32[]{:S(2)}, u32[]{:S(2)}) %collective-permute-start.22) | collective-permute-done | bytes 155680 | tf_op jit(solution)/shard_map/ppermute | solution.py:408
  75.1 0.5 collective-permute-done.21.refs_1_
  75.6 0.5 collective-permute-start.26
  76.1 0.4 collective-permute-done.25.refs_6_
  76.5 0.5 collective-permute-done.24.refs_5_
  77.0 0.2 collective-permute-done.26.refs_7_
  77.2 2.6 %shard_map.86 = f32[256,1280]{1,0:T(8,128)} custom-call(s32[1]{0:T(128)} %bitcast.rank_ref, f32[1,16,2432]{2,1,0:T(8,128)S(1)} %pad_maximum_fusion.refs_0_, f32[1,16,2432]{2,1,0:T(8,128)S(1)} %collective-permute-done.21.refs_1_, f32[1,16,2432]{2,1,0:T(8,128)S(1)} %collective-permute-done.22.refs_2_, f32[1,16,2432]{2,1,0:T(8,128)S(1)} %collective-permute-done.20.refs_3_, ...), custom_call_target="tpu_custom_call" | custom-call | tf_op jit(solution)/shard_map/pallas_call | solution.py:525
  (37 shorter events, 0.8 us)
Async XLA Ops:
  0.6 8.0 %copy-start.1 = (s32[256]{0:T(256)S(1)}, s32[256]{0:T(256)}, u32[]{:S(2)}) copy-start(s32[256]{0:T(256)} %param.8) | copy-start | bytes 3076
  2.9 7.3 %collective-permute-start.1 = (bf16[18,512]{1,0:T(8,128)(2,1)S(1)}, bf16[18,512]{1,0:T(8,128)(2,1)S(1)}, u32[]{:S(2)}, u32[]{:S(2)}) collective-permute-start(bf16[18,512]{1,0:T(8,128)(2,1)S(1)} %get-tuple-element.53.refs_0_), channel_id=1, source_target_pairs={{0,8},{1,9},{2,10},{3,11},{4,12},{5,13},{6,14},{7,15},{8,0},{9,1},... | collective-permute-start | bytes 55304 | tf_op jit(solution)/shard_map/ppermute | solution.py:408
  6.1 5.3 %collective-permute-start = (s16[18,1024]{1,0:T(8,128)(2,1)S(1)}, s16[18,1024]{1,0:T(8,128)(2,1)S(1)}, u32[]{:S(2)}, u32[]{:S(2)}) collective-permute-start(s16[18,1024]{1,0:T(8,128)(2,1)S(1)} %get-tuple-element.52.refs_0_), channel_id=1, source_target_pairs={{0,16},{1,17},{2,18},{3,19},{4,20},{5,21},{6,22},{7,23},{8,24},{9,... | collective-permute-start | bytes 110600 | tf_op jit(solution)/shard_map/ppermute | solution.py:408
  11.4 4.5 %collective-permute-start.4 = (s16[36,1024]{1,0:T(8,128)(2,1)S(1)}, s16[36,1024]{1,0:T(8,128)(2,1)S(1)}, u32[]{:S(2)}, u32[]{:S(2)}) collective-permute-start(s16[36,1024]{1,0:T(8,128)(2,1)S(1)} %shard_map.73.refs_0_), channel_id=1, source_target_pairs={{0,8},{1,9},{2,10},{3,11},{4,12},{5,13},{6,14},{7,15},{8,0},{9,1},... | collective-permute-start | bytes 221192 | tf_op jit(solution)/shard_map/ppermute | solution.py:408
  15.9 7.1 %collective-permute-start.5 = (s16[72,1024]{1,0:T(8,128)(2,1)S(1)}, s16[72,1024]{1,0:T(8,128)(2,1)S(1)}, u32[]{:S(2)}, u32[]{:S(2)}) collective-permute-start(s16[72,1024]{1,0:T(8,128)(2,1)S(1)} %shard_map.74.refs_0_), channel_id=1, source_target_pairs={{0,4},{1,5},{2,3},{3,2},{4,0},{5,1},{6,7},{7,6},{8,12},{9,13},{10,... | collective-permute-start | bytes 442376 | tf_op jit(solution)/shard_map/ppermute | solution.py:408
  17.6 5.0 %collective-permute-start.2 = (bf16[36,512]{1,0:T(8,128)(2,1)S(1)}, bf16[36,512]{1,0:T(8,128)(2,1)S(1)}, u32[]{:S(2)}, u32[]{:S(2)}) collective-permute-start(bf16[36,512]{1,0:T(8,128)(2,1)S(1)} %shard_map.70.refs_0_), channel_id=1, source_target_pairs={{0,16},{1,17},{2,18},{3,19},{4,20},{5,21},{6,22},{7,23},{8,24},{9,... | collective-permute-start | bytes 110600 | tf_op jit(solution)/shard_map/ppermute | solution.py:408
  22.5 5.1 %collective-permute-start.3 = (bf16[72,512]{1,0:T(8,128)(2,1)S(1)}, bf16[72,512]{1,0:T(8,128)(2,1)S(1)}, u32[]{:S(2)}, u32[]{:S(2)}) collective-permute-start(bf16[72,512]{1,0:T(8,128)(2,1)S(1)} %shard_map.71.refs_0_), channel_id=1, source_target_pairs={{0,4},{1,5},{2,3},{3,2},{4,0},{5,1},{6,7},{7,6},{8,12},{9,13},{10,... | collective-permute-start | bytes 221192 | tf_op jit(solution)/shard_map/ppermute | solution.py:408
  23.1 6.0 %collective-permute-start.7 = (s16[144,1024]{1,0:T(8,128)(2,1)S(1)}, s16[144,1024]{1,0:T(8,128)(2,1)S(1)}, u32[]{:S(2)}, u32[]{:S(2)}) collective-permute-start(s16[144,1024]{1,0:T(8,128)(2,1)S(1)} %shard_map.75.a_h_ref), channel_id=1, source_target_pairs={{0,2},{1,3},{2,0},{3,1},{4,6},{5,7},{6,4},{7,5},{8,10},{9,11},{10,... | collective-permute-start | bytes 884744 | tf_op jit(solution)/shard_map/ppermute | solution.py:408
  23.2 6.9 %collective-permute-start.9 = (s16[144,1024]{1,0:T(8,128)(2,1)S(1)}, s16[144,1024]{1,0:T(8,128)(2,1)S(1)}, u32[]{:S(2)}, u32[]{:S(2)}) collective-permute-start(s16[144,1024]{1,0:T(8,128)(2,1)S(1)} %shard_map.75.a_h_ref), channel_id=1, source_target_pairs={{0,1},{1,0},{2,6},{3,7},{4,5},{5,4},{6,2},{7,3},{8,9},{9,8},{10,14... | collective-permute-start | bytes 884744 | tf_op jit(solution)/shard_map/ppermute | solution.py:408
  27.7 1.4 %collective-permute-start.6 = (bf16[144,512]{1,0:T(8,128)(2,1)S(1)}, bf16[144,512]{1,0:T(8,128)(2,1)S(1)}, u32[]{:S(2)}, u32[]{:S(2)}) collective-permute-start(bf16[144,512]{1,0:T(8,128)(2,1)S(1)} %shard_map.72.a_x_ref), channel_id=1, source_target_pairs={{0,2},{1,3},{2,0},{3,1},{4,6},{5,7},{6,4},{7,5},{8,10},{9,11},{10,... | collective-permute-start | bytes 442376 | tf_op jit(solution)/shard_map/ppermute | solution.py:408
  30.1 2.2 %collective-permute-start.10 = (s16[144,1024]{1,0:T(8,128)(2,1)S(1)}, s16[144,1024]{1,0:T(8,128)(2,1)S(1)}, u32[]{:S(2)}, u32[]{:S(2)}) collective-permute-start(s16[144,1024]{1,0:T(8,128)(2,1)S(1)} %collective-permute-done.9.h_ref), channel_id=1, source_target_pairs={{0,2},{1,3},{2,0},{3,1},{4,6},{5,7},{6,4},{7,5},{8,10},{9,11},{10,... | collective-permute-start | bytes 884744 | tf_op jit(solution)/shard_map/ppermute | solution.py:408
  30.4 5.1 %collective-permute-start.8 = (bf16[144,512]{1,0:T(8,128)(2,1)S(1)}, bf16[144,512]{1,0:T(8,128)(2,1)S(1)}, u32[]{:S(2)}, u32[]{:S(2)}) collective-permute-start(bf16[144,512]{1,0:T(8,128)(2,1)S(1)} %shard_map.72.a_x_ref), channel_id=1, source_target_pairs={{0,1},{1,0},{2,6},{3,7},{4,5},{5,4},{6,2},{7,3},{8,9},{9,8},{10,14... | collective-permute-start | bytes 442376 | tf_op jit(solution)/shard_map/ppermute | solution.py:408
  32.9 4.0 %copy-start = (f32[512]{0:T(512)S(1)}, f32[512]{0:T(512)}, u32[]{:S(2)}) copy-start(f32[512]{0:T(512)} %param.7) | copy-start | bytes 6148
  35.5 1.4 %collective-permute-start.11 = (bf16[144,512]{1,0:T(8,128)(2,1)S(1)}, bf16[144,512]{1,0:T(8,128)(2,1)S(1)}, u32[]{:S(2)}, u32[]{:S(2)}) collective-permute-start(bf16[144,512]{1,0:T(8,128)(2,1)S(1)} %collective-permute-done.8.b_x_ref), channel_id=1, source_target_pairs={{0,2},{1,3},{2,0},{3,1},{4,6},{5,7},{6,4},{7,5},{8,10},{9,11},{10,... | collective-permute-start | bytes 442376 | tf_op jit(solution)/shard_map/ppermute | solution.py:408
  39.1 2.1 %collective-permute-start.12 = (f32[4,16,2432]{2,1,0:T(8,128)S(1)}, f32[4,16,2432]{2,1,0:T(8,128)S(1)}, u32[]{:S(2)}, u32[]{:S(2)}) collective-permute-start(f32[4,16,2432]{2,1,0:T(8,128)S(1)} %get-tuple-element.82), channel_id=1, source_target_pairs={{0,2},{1,3},{2,0},{3,1},{4,6},{5,7},{6,4},{7,5},{8,10},{9,11},{10,... | collective-permute-start | bytes 1867784 | tf_op jit(solution)/shard_map/ppermute | solution.py:408
  41.4 8.8 %collective-permute-start.15 = (f32[1,16,2432]{2,1,0:T(8,128)S(1)}, f32[1,16,2432]{2,1,0:T(8,128)S(1)}, u32[]{:S(2)}, u32[]{:S(2)}) collective-permute-start(f32[1,16,2432]{2,1,0:T(8,128)S(1)} %get-tuple-element.102), channel_id=1, source_target_pairs={{0,4},{1,5},{2,3},{3,2},{4,0},{5,1},{6,7},{7,6},{8,12},{9,13},{10,... | collective-permute-start | bytes 466952 | tf_op jit(solution)/shard_map/ppermute | solution.py:408
  42.6 7.6 %collective-permute-start.14 = (f32[1,16,2432]{2,1,0:T(8,128)S(1)}, f32[1,16,2432]{2,1,0:T(8,128)S(1)}, u32[]{:S(2)}, u32[]{:S(2)}) collective-permute-start(f32[1,16,2432]{2,1,0:T(8,128)S(1)} %get-tuple-element.103), channel_id=1, source_target_pairs={{0,1},{1,0},{2,6},{3,7},{4,5},{5,4},{6,2},{7,3},{8,9},{9,8},{10,14... | collective-permute-start | bytes 466952 | tf_op jit(solution)/shard_map/ppermute | solution.py:408
  44.1 7.9 %collective-permute-start.13 = (f32[1,16,2432]{2,1,0:T(8,128)S(1)}, f32[1,16,2432]{2,1,0:T(8,128)S(1)}, u32[]{:S(2)}, u32[]{:S(2)}) collective-permute-start(f32[1,16,2432]{2,1,0:T(8,128)S(1)} %get-tuple-element.104), channel_id=1, source_target_pairs={{0,5},{1,4},{2,7},{3,6},{4,1},{5,0},{6,3},{7,2},{8,13},{9,12},{10,... | collective-permute-start | bytes 466952 | tf_op jit(solution)/shard_map/ppermute | solution.py:408
  52.1 6.9 %collective-permute-start.17 = (f32[1,8,2432]{2,1,0:T(8,128)S(1)}, f32[1,8,2432]{2,1,0:T(8,128)S(1)}, u32[]{:S(2)}, u32[]{:S(2)}) collective-permute-start(f32[1,8,2432]{2,1,0:T(8,128)S(1)} %get-tuple-element.107), channel_id=1, source_target_pairs={{0,8},{1,9},{2,10},{3,11},{4,12},{5,13},{6,14},{7,15},{8,0},{9,1},... | collective-permute-start | bytes 233480 | tf_op jit(solution)/shard_map/ppermute | solution.py:408
  52.3 6.7 %collective-permute-start.16 = (f32[1,8,2432]{2,1,0:T(8,128)S(1)}, f32[1,8,2432]{2,1,0:T(8,128)S(1)}, u32[]{:S(2)}, u32[]{:S(2)}) collective-permute-start(f32[1,8,2432]{2,1,0:T(8,128)S(1)} %get-tuple-element.108), channel_id=1, source_target_pairs={{0,16},{1,17},{2,18},{3,19},{4,20},{5,21},{6,22},{7,23},{8,24},{9,... | collective-permute-start | bytes 233480 | tf_op jit(solution)/shard_map/ppermute | solution.py:408
  59.0 6.4 %collective-permute-start.18 = (f32[1,8,2432]{2,1,0:T(8,128)S(1)}, f32[1,8,2432]{2,1,0:T(8,128)S(1)}, u32[]{:S(2)}, u32[]{:S(2)}) collective-permute-start(f32[1,8,2432]{2,1,0:T(8,128)S(1)} %get-tuple-element.105), channel_id=1, source_target_pairs={{0,8},{1,9},{2,10},{3,11},{4,12},{5,13},{6,14},{7,15},{8,0},{9,1},... | collective-permute-start | bytes 233480 | tf_op jit(solution)/shard_map/ppermute | solution.py:408
  60.9 5.8 %collective-permute-start.19 = (f32[1,8,2432]{2,1,0:T(8,128)S(1)}, f32[1,8,2432]{2,1,0:T(8,128)S(1)}, u32[]{:S(2)}, u32[]{:S(2)}) collective-permute-start(f32[1,8,2432]{2,1,0:T(8,128)S(1)} %get-tuple-element.106), channel_id=1, source_target_pairs={{0,16},{1,17},{2,18},{3,19},{4,20},{5,21},{6,22},{7,23},{8,24},{9,... | collective-permute-start | bytes 233480 | tf_op jit(solution)/shard_map/ppermute | solution.py:408
  66.8 7.3 %collective-permute-start.20 = (f32[1,16,2432]{2,1,0:T(8,128)S(1)}, f32[1,16,2432]{2,1,0:T(8,128)S(1)}, u32[]{:S(2)}, u32[]{:S(2)}) collective-permute-start(f32[1,16,2432]{2,1,0:T(8,128)S(1)} %pad_maximum_fusion.refs_0_), channel_id=1, source_target_pairs={{0,5},{1,4},{2,7},{3,6},{4,1},{5,0},{6,3},{7,2},{8,13},{9,12},{10,... | collective-permute-start | bytes 466952 | tf_op jit(solution)/shard_map/ppermute | solution.py:408
  68.7 6.4 %collective-permute-start.22 = (f32[1,16,2432]{2,1,0:T(8,128)S(1)}, f32[1,16,2432]{2,1,0:T(8,128)S(1)}, u32[]{:S(2)}, u32[]{:S(2)}) collective-permute-start(f32[1,16,2432]{2,1,0:T(8,128)S(1)} %pad_maximum_fusion.refs_0_), channel_id=1, source_target_pairs={{0,4},{1,5},{2,3},{3,2},{4,0},{5,1},{6,7},{7,6},{8,12},{9,13},{10,... | collective-permute-start | bytes 466952 | tf_op jit(solution)/shard_map/ppermute | solution.py:408
  69.7 5.9 %collective-permute-start.21 = (f32[1,16,2432]{2,1,0:T(8,128)S(1)}, f32[1,16,2432]{2,1,0:T(8,128)S(1)}, u32[]{:S(2)}, u32[]{:S(2)}) collective-permute-start(f32[1,16,2432]{2,1,0:T(8,128)S(1)} %pad_maximum_fusion.refs_0_), channel_id=1, source_target_pairs={{0,1},{1,0},{2,6},{3,7},{4,5},{5,4},{6,2},{7,3},{8,9},{9,8},{10,14... | collective-permute-start | bytes 466952 | tf_op jit(solution)/shard_map/ppermute | solution.py:408
  70.3 5.8 %collective-permute-start.23 = (f32[1,16,2432]{2,1,0:T(8,128)S(1)}, f32[1,16,2432]{2,1,0:T(8,128)S(1)}, u32[]{:S(2)}, u32[]{:S(2)}) collective-permute-start(f32[1,16,2432]{2,1,0:T(8,128)S(1)} %pad_maximum_fusion.refs_0_), channel_id=1, source_target_pairs={{0,2},{1,3},{2,0},{3,1},{4,6},{5,7},{6,4},{7,5},{8,10},{9,11},{10,... | collective-permute-start | bytes 466952 | tf_op jit(solution)/shard_map/ppermute | solution.py:408
  75.1 1.4 %collective-permute-start.25 = (f32[1,16,2432]{2,1,0:T(8,128)S(1)}, f32[1,16,2432]{2,1,0:T(8,128)S(1)}, u32[]{:S(2)}, u32[]{:S(2)}) collective-permute-start(f32[1,16,2432]{2,1,0:T(8,128)S(1)} %collective-permute-done.22.refs_2_), channel_id=1, source_target_pairs={{0,2},{1,3},{2,0},{3,1},{4,6},{5,7},{6,4},{7,5},{8,10},{9,11},{10,... | collective-permute-start | bytes 466952 | tf_op jit(solution)/shard_map/ppermute | solution.py:408
  75.6 1.4 %collective-permute-start.24 = (f32[1,16,2432]{2,1,0:T(8,128)S(1)}, f32[1,16,2432]{2,1,0:T(8,128)S(1)}, u32[]{:S(2)}, u32[]{:S(2)}) collective-permute-start(f32[1,16,2432]{2,1,0:T(8,128)S(1)} %collective-permute-done.21.refs_1_), channel_id=1, source_target_pairs={{0,2},{1,3},{2,0},{3,1},{4,6},{5,7},{6,4},{7,5},{8,10},{9,11},{10,... | collective-permute-start | bytes 466952 | tf_op jit(solution)/shard_map/ppermute | solution.py:408
  75.6 1.6 %collective-permute-start.26 = (f32[1,16,2432]{2,1,0:T(8,128)S(1)}, f32[1,16,2432]{2,1,0:T(8,128)S(1)}, u32[]{:S(2)}, u32[]{:S(2)}) collective-permute-start(f32[1,16,2432]{2,1,0:T(8,128)S(1)} %collective-permute-done.20.refs_3_), channel_id=1, source_target_pairs={{0,2},{1,3},{2,0},{3,1},{4,6},{5,7},{6,4},{7,5},{8,10},{9,11},{10,... | collective-permute-start | bytes 466952 | tf_op jit(solution)/shard_map/ppermute | solution.py:408

commit v4 on v3

--- a/solution.py
+++ b/solution.py
@@ -88,8 +88,8 @@
     copies = [
         pltpu.make_async_copy(source, target, sems.at[k]) for k, (source, target) in enumerate(pairs)
     ]
-    for copy in copies:
-        copy.start()
+    for k in (0, 1, 2, 3, 5, 6, 4):
+        copies[k].start()
     rank = rank_ref[0]
     for k in range(slots + 1):
         found[k] = 0
@@ -365,9 +365,13 @@
         copy.start()
 
     send(slice(depth, total))
+    inverse_hi, inverse_lo = split(inverse)
     for at in range(0, depth, depth // 4):
         here = slice(at, at + depth // 4)
-        done_ref[:, here] = nn(inverse, work_ref[:, here], HIGHEST)
+        part_hi, part_lo = split(work_ref[:, here])
+        done_ref[:, here] = nn(inverse_hi, part_hi) + (
+            nn(inverse_lo, part_hi) + nn(inverse_hi, part_lo)
+        )
         send(here)
     for copy in copies:
         copy.wait()
@@ -491,7 +495,7 @@
     keep = keep + received
 
     panels = pivots // PANEL
-    cuts = [0, panels * 3 // 8, panels * 3 // 4, panels]
+    cuts = [0, panels // 2, panels * 3 // 4, panels]
 
     def eliminate_step(step, *given):
         return call(

time: 80.1 us -> 79.1 us (0.988)
  waiting for transfers between devices: 23.9 us -> 22.7 us
    ppermute x27, waiting for transfers between devices: 23.9 us -> 22.7 us  [move(): return lax.ppermute(value, axes, perm)]
  transfers between devices with their start and end apart: 27 -> 27, of which waited for: 16 -> 17; matrix products, arithmetic and copies ran while one was open for 0% -> 0% of each run, Pallas kernels for 25% -> 25%
where the time goes in v4:
time: 79.1 us; the launch traced here: 79 us
  starting transfers between devices  28.4 us (36%)
  Pallas kernels  26.6 us (34%)
  waiting for transfers between devices  22.7 us (29%)
  between operations  1.03 us (1%)
    ppermute x27, starting transfers between devices, move(): return lax.ppermute(value, axes, perm)  28.4 us
    ppermute x27, waiting for transfers between devices, move(): return lax.ppermute(value, axes, perm)  22.7 us
    pallas_call x17, Pallas kernels, call(): pl.pallas_call(kernel, out_shape=outs, in_specs=specs, out_specs=jax.tree...  22.1 us
    pallas_call x1, Pallas kernels, body(): pl.pallas_call(pick_kernel, out_shape=(pltpu.VMEM((slots, width), bf16),...  2.29 us
    pallas_call x1, Pallas kernels, body(): pl.pallas_call(partial(rows_kernel, masks), out_shape=jax.ShapeDtypeStruc...  2.25 us
  transfers between devices with their start and end apart: 27, of which 17 were waited for; matrix products, arithmetic and copies ran while one was open for 0% of the time, Pallas kernels for 25%

profile of v4, /device:TPU:0, one launch (start us, length us, event | category | flops | bytes accessed | tf_op | source)
XLA Modules:
  0.0 79.0 jit_solution(13854891729349164659)
XLA Ops:
  0.6 2.3 %shard_map.68 = (bf16[18,512]{1,0:T(8,128)(2,1)S(1)}, s16[18,1024]{1,0:T(8,128)(2,1)S(1)}, bf16[512,512]{1,0:T(8,128)(2,1)S(1)}, f32[512,1024]{1,0:T(8,128)S(1)}) custom-call(s32[1]{0:T(128)} %bitcast.rank_ref, s32[1,256]{1,0:T(1,128)} %bitcast.6, s32[1,256]{1,0:T(1,128)} %bitcast.8, bf16[512,512]{1,0:T(8,128)(2,1)} %features_ref.1, f32[512,1024]{1,0:T(8,128)} %factor_ref.1), custom_call_target="tpu_custom_call" | custom-call | tf_op jit(solution)/shard_map/pallas_call | solution.py:420
  2.9 3.1 %collective-permute-start.1 = (bf16[18,512]{1,0:T(8,128)(2,1)S(1)}, bf16[18,512]{1,0:T(8,128)(2,1)S(1)}, u32[]{:S(2)}, u32[]{:S(2)}) collective-permute-start(bf16[18,512]{1,0:T(8,128)(2,1)S(1)} %get-tuple-element.53.refs_0_), channel_id=1, source_target_pairs={{0,8},{1,9},{2,10},{3,11},{4,12},{5,13},{6,14},{7,15},{8,0},{9,1},... | collective-permute-start | bytes 55304 | tf_op jit(solution)/shard_map/ppermute | solution.py:412
  6.1 2.6 %collective-permute-start = (s16[18,1024]{1,0:T(8,128)(2,1)S(1)}, s16[18,1024]{1,0:T(8,128)(2,1)S(1)}, u32[]{:S(2)}, u32[]{:S(2)}) collective-permute-start(s16[18,1024]{1,0:T(8,128)(2,1)S(1)} %get-tuple-element.52.refs_0_), channel_id=1, source_target_pairs={{0,16},{1,17},{2,18},{3,19},{4,20},{5,21},{6,22},{7,23},{8,24},{9,... | collective-permute-start | bytes 110600 | tf_op jit(solution)/shard_map/ppermute | solution.py:412
  8.7 1.6 %shard_map.69 = (s32[2,256]{1,0:T(2,128)S(1)}, f32[1,512]{1,0:T(1,128)S(1)}, bf16[512,1024]{1,0:T(8,128)(2,1)S(1)}, bf16[512,1024]{1,0:T(8,128)(2,1)S(1)}) custom-call(s32[1]{0:T(128)} %bitcast.rank_ref, s32[1,256]{1,0:T(1,128)S(1)} %bitcast.7, bf16[512,512]{1,0:T(8,128)(2,1)S(1)} %get-tuple-element.54.features_ref, f32[512,1024]{1,0:T(8,128)S(1)} %get-tuple-element.55.factor_ref), custom_call_target="tpu_custom_call" | custom-call | flops 1000000000 | bytes 1000000 | tf_op jit(solution)/shard_map/pallas_call | solution.py:51
  10.3 1.1 %collective-permute-done.refs_1_ = s16[18,1024]{1,0:T(8,128)(2,1)S(1)} collective-permute-done((s16[18,1024]{1,0:T(8,128)(2,1)S(1)}, s16[18,1024]{1,0:T(8,128)(2,1)S(1)}, u32[]{:S(2)}, u32[]{:S(2)}) %collective-permute-start) | collective-permute-done | bytes 36896 | tf_op jit(solution)/shard_map/ppermute | solution.py:412
  11.5 4.4 %collective-permute-done.4.refs_1_ = s16[36,1024]{1,0:T(8,128)(2,1)S(1)} collective-permute-done((s16[36,1024]{1,0:T(8,128)(2,1)S(1)}, s16[36,1024]{1,0:T(8,128)(2,1)S(1)}, u32[]{:S(2)}, u32[]{:S(2)}) %collective-permute-start.4) | collective-permute-done | bytes 73760 | tf_op jit(solution)/shard_map/ppermute | solution.py:412
  15.9 1.6 %collective-permute-start.5 = (s16[72,1024]{1,0:T(8,128)(2,1)S(1)}, s16[72,1024]{1,0:T(8,128)(2,1)S(1)}, u32[]{:S(2)}, u32[]{:S(2)}) collective-permute-start(s16[72,1024]{1,0:T(8,128)(2,1)S(1)} %shard_map.74.refs_0_), channel_id=1, source_target_pairs={{0,4},{1,5},{2,3},{3,2},{4,0},{5,1},{6,7},{7,6},{8,12},{9,13},{10,... | collective-permute-start | bytes 442376 | tf_op jit(solution)/shard_map/ppermute | solution.py:412
  17.6 2.2 %collective-permute-start.2 = (bf16[36,512]{1,0:T(8,128)(2,1)S(1)}, bf16[36,512]{1,0:T(8,128)(2,1)S(1)}, u32[]{:S(2)}, u32[]{:S(2)}) collective-permute-start(bf16[36,512]{1,0:T(8,128)(2,1)S(1)} %shard_map.70.refs_0_), channel_id=1, source_target_pairs={{0,16},{1,17},{2,18},{3,19},{4,20},{5,21},{6,22},{7,23},{8,24},{9,... | collective-permute-start | bytes 110600 | tf_op jit(solution)/shard_map/ppermute | solution.py:412
  19.8 2.7 %collective-permute-done.2.refs_1_ = bf16[36,512]{1,0:T(8,128)(2,1)S(1)} collective-permute-done((bf16[36,512]{1,0:T(8,128)(2,1)S(1)}, bf16[36,512]{1,0:T(8,128)(2,1)S(1)}, u32[]{:S(2)}, u32[]{:S(2)}) %collective-permute-start.2) | collective-permute-done | bytes 36896 | tf_op jit(solution)/shard_map/ppermute | solution.py:412
  22.5 0.5 collective-permute-start.3
  23.2 1.7 %collective-permute-start.9 = (s16[144,1024]{1,0:T(8,128)(2,1)S(1)}, s16[144,1024]{1,0:T(8,128)(2,1)S(1)}, u32[]{:S(2)}, u32[]{:S(2)}) collective-permute-start(s16[144,1024]{1,0:T(8,128)(2,1)S(1)} %shard_map.75.a_h_ref), channel_id=1, source_target_pairs={{0,1},{1,0},{2,6},{3,7},{4,5},{5,4},{6,2},{7,3},{8,9},{9,8},{10,14... | collective-permute-start | bytes 884744 | tf_op jit(solution)/shard_map/ppermute | solution.py:412
  24.8 2.8 %collective-permute-done.3.refs_1_ = bf16[72,512]{1,0:T(8,128)(2,1)S(1)} collective-permute-done((bf16[72,512]{1,0:T(8,128)(2,1)S(1)}, bf16[72,512]{1,0:T(8,128)(2,1)S(1)}, u32[]{:S(2)}, u32[]{:S(2)}) %collective-permute-start.3) | collective-permute-done | bytes 73760 | tf_op jit(solution)/shard_map/ppermute | solution.py:412
  27.8 1.4 %collective-permute-done.6.c_x_ref = bf16[144,512]{1,0:T(8,128)(2,1)S(1)} collective-permute-done((bf16[144,512]{1,0:T(8,128)(2,1)S(1)}, bf16[144,512]{1,0:T(8,128)(2,1)S(1)}, u32[]{:S(2)}, u32[]{:S(2)}) %collective-permute-start.6) | collective-permute-done | bytes 147488 | tf_op jit(solution)/shard_map/ppermute | solution.py:412
  29.1 1.0 %shard_map.76 = (bf16[256,512]{1,0:T(8,128)(2,1)S(1)}, bf16[256,1024]{1,0:T(8,128)(2,1)S(1)}, bf16[256,1024]{1,0:T(8,128)(2,1)S(1)}) custom-call(s32[2,256]{1,0:T(2,128)S(1)} %get-tuple-element.60.source_ref, bf16[144,512]{1,0:T(8,128)(2,1)S(1)} %shard_map.72.a_x_ref, s16[144,1024]{1,0:T(8,128)(2,1)S(1)} %shard_map.75.a_h_ref, ...), custom_call_target="tpu_custom_call" | custom-call | flops 1000000000 | bytes 1000000 | tf_op jit(solution)/shard_map/pallas_call | solution.py:51
  30.1 0.2 collective-permute-start.10
  30.4 1.5 %collective-permute-start.8 = (bf16[144,512]{1,0:T(8,128)(2,1)S(1)}, bf16[144,512]{1,0:T(8,128)(2,1)S(1)}, u32[]{:S(2)}, u32[]{:S(2)}) collective-permute-start(bf16[144,512]{1,0:T(8,128)(2,1)S(1)} %shard_map.72.a_x_ref), channel_id=1, source_target_pairs={{0,1},{1,0},{2,6},{3,7},{4,5},{5,4},{6,2},{7,3},{8,9},{9,8},{10,14... | collective-permute-start | bytes 442376 | tf_op jit(solution)/shard_map/ppermute | solution.py:412
  31.8 0.5 shard_map.77
  32.4 0.5 shard_map.78
  32.9 2.6 %collective-permute-done.8.b_x_ref = bf16[144,512]{1,0:T(8,128)(2,1)S(1)} collective-permute-done((bf16[144,512]{1,0:T(8,128)(2,1)S(1)}, bf16[144,512]{1,0:T(8,128)(2,1)S(1)}, u32[]{:S(2)}, u32[]{:S(2)}) %collective-permute-start.8) | collective-permute-done | bytes 147488 | tf_op jit(solution)/shard_map/ppermute | solution.py:412
  35.5 1.0 %shard_map.79.product_ref = f32[256,512]{1,0:T(8,128)S(1)} custom-call(bf16[256,1024]{1,0:T(8,128)(2,1)S(1)} %get-tuple-element.86.coarse_ref.refs_1_, bf16[256,1024]{1,0:T(8,128)(2,1)S(1)} %get-tuple-element.87.fine_ref.refs_2_, bf16[512,1024]{1,0:T(8,128)(2,1)S(1)} %get-tuple-element.76.high_ref, bf16[512,1024]{1,0:T(8,128)(2,1)S(1)} %get-tuple-element.77.low_ref), custom_call_target="tpu_custom_call" | custom-call | flops 1000000000 | bytes 1000000 | tf_op jit(solution)/shard_map/pallas_call | solution.py:51
  36.5 0.4 collective-permute-done.11.d_x_ref
  36.9 2.2 %shard_map.80 = (bf16[256,512]{1,0:T(8,128)(2,1)S(1)}, f32[256,512]{1,0:T(8,128)S(1)}, f32[4,16,2432]{2,1,0:T(8,128)S(1)}) custom-call(s32[1]{0:T(128)} %bitcast.rank_ref, s32[2,256]{1,0:T(2,128)S(1)} %get-tuple-element.60.source_ref, bf16[256,512]{1,0:T(8,128)(2,1)S(1)} %get-tuple-element.63.x_ref, bf16[144,512]{1,0:T(8,128)(2,1)S(1)} %collective-permute-done.8.b_x_ref, ...), custom_call_target="tpu_custom_call" | custom-call | flops 1000000000 | bytes 1000000 | tf_op jit(solution)/shard_map/pallas_call | solution.py:51
  39.3 1.3 %shard_map.81 = f32[4,16,2432]{2,1,0:T(8,128)S(1)} custom-call(s32[1]{0:T(128)} %bitcast.rank_ref, f32[256,512]{1,0:T(8,128)S(1)} %get-tuple-element.81.residual_ref, bf16[512,1024]{1,0:T(8,128)(2,1)S(1)} %get-tuple-element.76.high_ref, bf16[512,1024]{1,0:T(8,128)(2,1)S(1)} %get-tuple-element.77.low_ref, f32[1,512]{1,0:T(1,128)S(1)} %bitcast.5), custom_call_target="tpu_custom_call" | custom-call | flops 1000000000 | bytes 1000000 | tf_op jit(solution)/shard_map/pallas_call | solution.py:51
  40.6 0.6 collective-permute-done.12
  41.4 1.3 %collective-permute-start.15 = (f32[1,16,2432]{2,1,0:T(8,128)S(1)}, f32[1,16,2432]{2,1,0:T(8,128)S(1)}, u32[]{:S(2)}, u32[]{:S(2)}) collective-permute-start(f32[1,16,2432]{2,1,0:T(8,128)S(1)} %get-tuple-element.102), channel_id=1, source_target_pairs={{0,4},{1,5},{2,3},{3,2},{4,0},{5,1},{6,7},{7,6},{8,12},{9,13},{10,... | collective-permute-start | bytes 466952 | tf_op jit(solution)/shard_map/ppermute | solution.py:412
  42.6 1.5 %collective-permute-start.14 = (f32[1,16,2432]{2,1,0:T(8,128)S(1)}, f32[1,16,2432]{2,1,0:T(8,128)S(1)}, u32[]{:S(2)}, u32[]{:S(2)}) collective-permute-start(f32[1,16,2432]{2,1,0:T(8,128)S(1)} %get-tuple-element.103), channel_id=1, source_target_pairs={{0,1},{1,0},{2,6},{3,7},{4,5},{5,4},{6,2},{7,3},{8,9},{9,8},{10,14... | collective-permute-start | bytes 466952 | tf_op jit(solution)/shard_map/ppermute | solution.py:412
  44.1 0.8 collective-permute-start.13
  44.9 6.6 %shard_map.82.refs_0_ = f32[256,256]{1,0:T(8,128)S(1)} custom-call(bf16[256,512]{1,0:T(8,128)(2,1)S(1)} %get-tuple-element.85.refs_0_, bf16[256,1024]{1,0:T(8,128)(2,1)S(1)} %get-tuple-element.86.coarse_ref.refs_1_, bf16[256,1024]{1,0:T(8,128)(2,1)S(1)} %get-tuple-element.87.fine_ref.refs_2_), custom_call_target="tpu_custom_call" | custom-call | flops 1000000000 | bytes 1000000 | tf_op jit(solution)/shard_map/pallas_call | solution.py:51
  51.6 0.4 collective-permute-done.13
  52.3 2.6 %collective-permute-start.16 = (f32[1,8,2432]{2,1,0:T(8,128)S(1)}, f32[1,8,2432]{2,1,0:T(8,128)S(1)}, u32[]{:S(2)}, u32[]{:S(2)}) collective-permute-start(f32[1,8,2432]{2,1,0:T(8,128)S(1)} %get-tuple-element.108), channel_id=1, source_target_pairs={{0,16},{1,17},{2,18},{3,19},{4,20},{5,21},{6,22},{7,23},{8,24},{9,... | collective-permute-start | bytes 233480 | tf_op jit(solution)/shard_map/ppermute | solution.py:412
  54.8 2.8 %shard_map.83.refs_0_ = f32[256,256]{1,0:T(8,128)S(1)} custom-call(f32[256,256]{1,0:T(8,128)S(1)} %shard_map.82.refs_0_), custom_call_target="tpu_custom_call" | custom-call | flops 1000000000 | bytes 1000000 | tf_op jit(solution)/shard_map/pallas_call | solution.py:51
  57.6 0.8 collective-permute-done.16
  58.4 1.5 %collective-permute-start.18 = (f32[1,8,2432]{2,1,0:T(8,128)S(1)}, f32[1,8,2432]{2,1,0:T(8,128)S(1)}, u32[]{:S(2)}, u32[]{:S(2)}) collective-permute-start(f32[1,8,2432]{2,1,0:T(8,128)S(1)} %get-tuple-element.105), channel_id=1, source_target_pairs={{0,8},{1,9},{2,10},{3,11},{4,12},{5,13},{6,14},{7,15},{8,0},{9,1},... | collective-permute-start | bytes 233480 | tf_op jit(solution)/shard_map/ppermute | solution.py:412
  60.0 2.6 %collective-permute-start.19 = (f32[1,8,2432]{2,1,0:T(8,128)S(1)}, f32[1,8,2432]{2,1,0:T(8,128)S(1)}, u32[]{:S(2)}, u32[]{:S(2)}) collective-permute-start(f32[1,8,2432]{2,1,0:T(8,128)S(1)} %get-tuple-element.106), channel_id=1, source_target_pairs={{0,16},{1,17},{2,18},{3,19},{4,20},{5,21},{6,22},{7,23},{8,24},{9,... | collective-permute-start | bytes 233480 | tf_op jit(solution)/shard_map/ppermute | solution.py:412
  62.5 3.0 %shard_map.84.inverse_ref.refs_8_ = f32[256,256]{1,0:T(8,128)S(1)} custom-call(f32[256,256]{1,0:T(8,128)S(1)} %shard_map.83.refs_0_), custom_call_target="tpu_custom_call" | custom-call | flops 1000000000 | bytes 1000000 | tf_op jit(solution)/shard_map/pallas_call | solution.py:51
  65.5 0.6 collective-permute-done.19
  66.1 2.0 %collective-permute-start.20 = (f32[1,16,2432]{2,1,0:T(8,128)S(1)}, f32[1,16,2432]{2,1,0:T(8,128)S(1)}, u32[]{:S(2)}, u32[]{:S(2)}) collective-permute-start(f32[1,16,2432]{2,1,0:T(8,128)S(1)} %pad_maximum_fusion.refs_0_), channel_id=1, source_target_pairs={{0,5},{1,4},{2,7},{3,6},{4,1},{5,0},{6,3},{7,2},{8,13},{9,12},{10,... | collective-permute-start | bytes 466952 | tf_op jit(solution)/shard_map/ppermute | solution.py:412
  68.1 0.8 %collective-permute-start.22 = (f32[1,16,2432]{2,1,0:T(8,128)S(1)}, f32[1,16,2432]{2,1,0:T(8,128)S(1)}, u32[]{:S(2)}, u32[]{:S(2)}) collective-permute-start(f32[1,16,2432]{2,1,0:T(8,128)S(1)} %pad_maximum_fusion.refs_0_), channel_id=1, source_target_pairs={{0,4},{1,5},{2,3},{3,2},{4,0},{5,1},{6,7},{7,6},{8,12},{9,13},{10,... | collective-permute-start | bytes 466952 | tf_op jit(solution)/shard_map/ppermute | solution.py:412
  69.0 0.7 collective-permute-start.21
  69.7 1.4 %shard_map.85 = f32[512,256]{1,0:T(8,128)} custom-call(f32[256,512]{1,0:T(8,128)S(1)} %get-tuple-element.81.residual_ref, f32[256,256]{1,0:T(8,128)S(1)} %shard_map.84.inverse_ref.refs_8_), custom_call_target="tpu_custom_call" | custom-call | flops 1000000000 | bytes 1000000 | tf_op jit(solution)/shard_map/pallas_call | solution.py:51
  71.1 2.3 %collective-permute-done.20.refs_3_ = f32[1,16,2432]{2,1,0:T(8,128)S(1)} collective-permute-done((f32[1,16,2432]{2,1,0:T(8,128)S(1)}, f32[1,16,2432]{2,1,0:T(8,128)S(1)}, u32[]{:S(2)}, u32[]{:S(2)}) %collective-permute-start.20) | collective-permute-done | bytes 155680 | tf_op jit(solution)/shard_map/ppermute | solution.py:412
  73.4 1.2 %collective-permute-done.22.refs_2_ = f32[1,16,2432]{2,1,0:T(8,128)S(1)} collective-permute-done((f32[1,16,2432]{2,1,0:T(8,128)S(1)}, f32[1,16,2432]{2,1,0:T(8,128)S(1)}, u32[]{:S(2)}, u32[]{:S(2)}) %collective-permute-start.22) | collective-permute-done | bytes 155680 | tf_op jit(solution)/shard_map/ppermute | solution.py:412
  74.6 0.3 collective-permute-done.21.refs_1_
  75.1 0.3 collective-permute-start.26
  75.4 0.5 collective-permute-done.25.refs_6_
  76.0 0.3 collective-permute-done.24.refs_5_
  76.3 0.2 collective-permute-done.26.refs_7_
  76.5 2.3 %shard_map.86 = f32[256,1280]{1,0:T(8,128)} custom-call(s32[1]{0:T(128)} %bitcast.rank_ref, f32[1,16,2432]{2,1,0:T(8,128)S(1)} %pad_maximum_fusion.refs_0_, f32[1,16,2432]{2,1,0:T(8,128)S(1)} %collective-permute-done.21.refs_1_, f32[1,16,2432]{2,1,0:T(8,128)S(1)} %collective-permute-done.22.refs_2_, f32[1,16,2432]{2,1,0:T(8,128)S(1)} %collective-permute-done.20.refs_3_, ...), custom_call_target="tpu_custom_call" | custom-call | tf_op jit(solution)/shard_map/pallas_call | solution.py:529
  (37 shorter events, 1.2 us)
Async XLA Ops:
  0.6 8.0 %copy-start.1 = (s32[256]{0:T(256)S(1)}, s32[256]{0:T(256)}, u32[]{:S(2)}) copy-start(s32[256]{0:T(256)} %param.8) | copy-start | bytes 3076
  2.9 7.3 %collective-permute-start.1 = (bf16[18,512]{1,0:T(8,128)(2,1)S(1)}, bf16[18,512]{1,0:T(8,128)(2,1)S(1)}, u32[]{:S(2)}, u32[]{:S(2)}) collective-permute-start(bf16[18,512]{1,0:T(8,128)(2,1)S(1)} %get-tuple-element.53.refs_0_), channel_id=1, source_target_pairs={{0,8},{1,9},{2,10},{3,11},{4,12},{5,13},{6,14},{7,15},{8,0},{9,1},... | collective-permute-start | bytes 55304 | tf_op jit(solution)/shard_map/ppermute | solution.py:412
  6.1 5.3 %collective-permute-start = (s16[18,1024]{1,0:T(8,128)(2,1)S(1)}, s16[18,1024]{1,0:T(8,128)(2,1)S(1)}, u32[]{:S(2)}, u32[]{:S(2)}) collective-permute-start(s16[18,1024]{1,0:T(8,128)(2,1)S(1)} %get-tuple-element.52.refs_0_), channel_id=1, source_target_pairs={{0,16},{1,17},{2,18},{3,19},{4,20},{5,21},{6,22},{7,23},{8,24},{9,... | collective-permute-start | bytes 110600 | tf_op jit(solution)/shard_map/ppermute | solution.py:412
  11.4 4.5 %collective-permute-start.4 = (s16[36,1024]{1,0:T(8,128)(2,1)S(1)}, s16[36,1024]{1,0:T(8,128)(2,1)S(1)}, u32[]{:S(2)}, u32[]{:S(2)}) collective-permute-start(s16[36,1024]{1,0:T(8,128)(2,1)S(1)} %shard_map.73.refs_0_), channel_id=1, source_target_pairs={{0,8},{1,9},{2,10},{3,11},{4,12},{5,13},{6,14},{7,15},{8,0},{9,1},... | collective-permute-start | bytes 221192 | tf_op jit(solution)/shard_map/ppermute | solution.py:412
  15.9 7.1 %collective-permute-start.5 = (s16[72,1024]{1,0:T(8,128)(2,1)S(1)}, s16[72,1024]{1,0:T(8,128)(2,1)S(1)}, u32[]{:S(2)}, u32[]{:S(2)}) collective-permute-start(s16[72,1024]{1,0:T(8,128)(2,1)S(1)} %shard_map.74.refs_0_), channel_id=1, source_target_pairs={{0,4},{1,5},{2,3},{3,2},{4,0},{5,1},{6,7},{7,6},{8,12},{9,13},{10,... | collective-permute-start | bytes 442376 | tf_op jit(solution)/shard_map/ppermute | solution.py:412
  17.6 5.0 %collective-permute-start.2 = (bf16[36,512]{1,0:T(8,128)(2,1)S(1)}, bf16[36,512]{1,0:T(8,128)(2,1)S(1)}, u32[]{:S(2)}, u32[]{:S(2)}) collective-permute-start(bf16[36,512]{1,0:T(8,128)(2,1)S(1)} %shard_map.70.refs_0_), channel_id=1, source_target_pairs={{0,16},{1,17},{2,18},{3,19},{4,20},{5,21},{6,22},{7,23},{8,24},{9,... | collective-permute-start | bytes 110600 | tf_op jit(solution)/shard_map/ppermute | solution.py:412
  22.5 5.1 %collective-permute-start.3 = (bf16[72,512]{1,0:T(8,128)(2,1)S(1)}, bf16[72,512]{1,0:T(8,128)(2,1)S(1)}, u32[]{:S(2)}, u32[]{:S(2)}) collective-permute-start(bf16[72,512]{1,0:T(8,128)(2,1)S(1)} %shard_map.71.refs_0_), channel_id=1, source_target_pairs={{0,4},{1,5},{2,3},{3,2},{4,0},{5,1},{6,7},{7,6},{8,12},{9,13},{10,... | collective-permute-start | bytes 221192 | tf_op jit(solution)/shard_map/ppermute | solution.py:412
  23.1 6.0 %collective-permute-start.7 = (s16[144,1024]{1,0:T(8,128)(2,1)S(1)}, s16[144,1024]{1,0:T(8,128)(2,1)S(1)}, u32[]{:S(2)}, u32[]{:S(2)}) collective-permute-start(s16[144,1024]{1,0:T(8,128)(2,1)S(1)} %shard_map.75.a_h_ref), channel_id=1, source_target_pairs={{0,2},{1,3},{2,0},{3,1},{4,6},{5,7},{6,4},{7,5},{8,10},{9,11},{10,... | collective-permute-start | bytes 884744 | tf_op jit(solution)/shard_map/ppermute | solution.py:412
  23.2 6.9 %collective-permute-start.9 = (s16[144,1024]{1,0:T(8,128)(2,1)S(1)}, s16[144,1024]{1,0:T(8,128)(2,1)S(1)}, u32[]{:S(2)}, u32[]{:S(2)}) collective-permute-start(s16[144,1024]{1,0:T(8,128)(2,1)S(1)} %shard_map.75.a_h_ref), channel_id=1, source_target_pairs={{0,1},{1,0},{2,6},{3,7},{4,5},{5,4},{6,2},{7,3},{8,9},{9,8},{10,14... | collective-permute-start | bytes 884744 | tf_op jit(solution)/shard_map/ppermute | solution.py:412
  27.7 1.4 %collective-permute-start.6 = (bf16[144,512]{1,0:T(8,128)(2,1)S(1)}, bf16[144,512]{1,0:T(8,128)(2,1)S(1)}, u32[]{:S(2)}, u32[]{:S(2)}) collective-permute-start(bf16[144,512]{1,0:T(8,128)(2,1)S(1)} %shard_map.72.a_x_ref), channel_id=1, source_target_pairs={{0,2},{1,3},{2,0},{3,1},{4,6},{5,7},{6,4},{7,5},{8,10},{9,11},{10,... | collective-permute-start | bytes 442376 | tf_op jit(solution)/shard_map/ppermute | solution.py:412
  30.1 2.2 %collective-permute-start.10 = (s16[144,1024]{1,0:T(8,128)(2,1)S(1)}, s16[144,1024]{1,0:T(8,128)(2,1)S(1)}, u32[]{:S(2)}, u32[]{:S(2)}) collective-permute-start(s16[144,1024]{1,0:T(8,128)(2,1)S(1)} %collective-permute-done.9.h_ref), channel_id=1, source_target_pairs={{0,2},{1,3},{2,0},{3,1},{4,6},{5,7},{6,4},{7,5},{8,10},{9,11},{10,... | collective-permute-start | bytes 884744 | tf_op jit(solution)/shard_map/ppermute | solution.py:412
  30.4 5.1 %collective-permute-start.8 = (bf16[144,512]{1,0:T(8,128)(2,1)S(1)}, bf16[144,512]{1,0:T(8,128)(2,1)S(1)}, u32[]{:S(2)}, u32[]{:S(2)}) collective-permute-start(bf16[144,512]{1,0:T(8,128)(2,1)S(1)} %shard_map.72.a_x_ref), channel_id=1, source_target_pairs={{0,1},{1,0},{2,6},{3,7},{4,5},{5,4},{6,2},{7,3},{8,9},{9,8},{10,14... | collective-permute-start | bytes 442376 | tf_op jit(solution)/shard_map/ppermute | solution.py:412
  32.9 4.0 %copy-start = (f32[512]{0:T(512)S(1)}, f32[512]{0:T(512)}, u32[]{:S(2)}) copy-start(f32[512]{0:T(512)} %param.7) | copy-start | bytes 6148
  35.5 1.4 %collective-permute-start.11 = (bf16[144,512]{1,0:T(8,128)(2,1)S(1)}, bf16[144,512]{1,0:T(8,128)(2,1)S(1)}, u32[]{:S(2)}, u32[]{:S(2)}) collective-permute-start(bf16[144,512]{1,0:T(8,128)(2,1)S(1)} %collective-permute-done.8.b_x_ref), channel_id=1, source_target_pairs={{0,2},{1,3},{2,0},{3,1},{4,6},{5,7},{6,4},{7,5},{8,10},{9,11},{10,... | collective-permute-start | bytes 442376 | tf_op jit(solution)/shard_map/ppermute | solution.py:412
  39.1 2.1 %collective-permute-start.12 = (f32[4,16,2432]{2,1,0:T(8,128)S(1)}, f32[4,16,2432]{2,1,0:T(8,128)S(1)}, u32[]{:S(2)}, u32[]{:S(2)}) collective-permute-start(f32[4,16,2432]{2,1,0:T(8,128)S(1)} %get-tuple-element.82), channel_id=1, source_target_pairs={{0,2},{1,3},{2,0},{3,1},{4,6},{5,7},{6,4},{7,5},{8,10},{9,11},{10,... | collective-permute-start | bytes 1867784 | tf_op jit(solution)/shard_map/ppermute | solution.py:412
  41.4 10.2 %collective-permute-start.15 = (f32[1,16,2432]{2,1,0:T(8,128)S(1)}, f32[1,16,2432]{2,1,0:T(8,128)S(1)}, u32[]{:S(2)}, u32[]{:S(2)}) collective-permute-start(f32[1,16,2432]{2,1,0:T(8,128)S(1)} %get-tuple-element.102), channel_id=1, source_target_pairs={{0,4},{1,5},{2,3},{3,2},{4,0},{5,1},{6,7},{7,6},{8,12},{9,13},{10,... | collective-permute-start | bytes 466952 | tf_op jit(solution)/shard_map/ppermute | solution.py:412
  42.6 9.0 %collective-permute-start.14 = (f32[1,16,2432]{2,1,0:T(8,128)S(1)}, f32[1,16,2432]{2,1,0:T(8,128)S(1)}, u32[]{:S(2)}, u32[]{:S(2)}) collective-permute-start(f32[1,16,2432]{2,1,0:T(8,128)S(1)} %get-tuple-element.103), channel_id=1, source_target_pairs={{0,1},{1,0},{2,6},{3,7},{4,5},{5,4},{6,2},{7,3},{8,9},{9,8},{10,14... | collective-permute-start | bytes 466952 | tf_op jit(solution)/shard_map/ppermute | solution.py:412
  44.1 7.9 %collective-permute-start.13 = (f32[1,16,2432]{2,1,0:T(8,128)S(1)}, f32[1,16,2432]{2,1,0:T(8,128)S(1)}, u32[]{:S(2)}, u32[]{:S(2)}) collective-permute-start(f32[1,16,2432]{2,1,0:T(8,128)S(1)} %get-tuple-element.104), channel_id=1, source_target_pairs={{0,5},{1,4},{2,7},{3,6},{4,1},{5,0},{6,3},{7,2},{8,13},{9,12},{10,... | collective-permute-start | bytes 466952 | tf_op jit(solution)/shard_map/ppermute | solution.py:412
  52.1 5.5 %collective-permute-start.17 = (f32[1,8,2432]{2,1,0:T(8,128)S(1)}, f32[1,8,2432]{2,1,0:T(8,128)S(1)}, u32[]{:S(2)}, u32[]{:S(2)}) collective-permute-start(f32[1,8,2432]{2,1,0:T(8,128)S(1)} %get-tuple-element.107), channel_id=1, source_target_pairs={{0,8},{1,9},{2,10},{3,11},{4,12},{5,13},{6,14},{7,15},{8,0},{9,1},... | collective-permute-start | bytes 233480 | tf_op jit(solution)/shard_map/ppermute | solution.py:412
  52.3 6.1 %collective-permute-start.16 = (f32[1,8,2432]{2,1,0:T(8,128)S(1)}, f32[1,8,2432]{2,1,0:T(8,128)S(1)}, u32[]{:S(2)}, u32[]{:S(2)}) collective-permute-start(f32[1,8,2432]{2,1,0:T(8,128)S(1)} %get-tuple-element.108), channel_id=1, source_target_pairs={{0,16},{1,17},{2,18},{3,19},{4,20},{5,21},{6,22},{7,23},{8,24},{9,... | collective-permute-start | bytes 233480 | tf_op jit(solution)/shard_map/ppermute | solution.py:412
  58.4 7.1 %collective-permute-start.18 = (f32[1,8,2432]{2,1,0:T(8,128)S(1)}, f32[1,8,2432]{2,1,0:T(8,128)S(1)}, u32[]{:S(2)}, u32[]{:S(2)}) collective-permute-start(f32[1,8,2432]{2,1,0:T(8,128)S(1)} %get-tuple-element.105), channel_id=1, source_target_pairs={{0,8},{1,9},{2,10},{3,11},{4,12},{5,13},{6,14},{7,15},{8,0},{9,1},... | collective-permute-start | bytes 233480 | tf_op jit(solution)/shard_map/ppermute | solution.py:412
  60.0 6.1 %collective-permute-start.19 = (f32[1,8,2432]{2,1,0:T(8,128)S(1)}, f32[1,8,2432]{2,1,0:T(8,128)S(1)}, u32[]{:S(2)}, u32[]{:S(2)}) collective-permute-start(f32[1,8,2432]{2,1,0:T(8,128)S(1)} %get-tuple-element.106), channel_id=1, source_target_pairs={{0,16},{1,17},{2,18},{3,19},{4,20},{5,21},{6,22},{7,23},{8,24},{9,... | collective-permute-start | bytes 233480 | tf_op jit(solution)/shard_map/ppermute | solution.py:412
  66.1 7.3 %collective-permute-start.20 = (f32[1,16,2432]{2,1,0:T(8,128)S(1)}, f32[1,16,2432]{2,1,0:T(8,128)S(1)}, u32[]{:S(2)}, u32[]{:S(2)}) collective-permute-start(f32[1,16,2432]{2,1,0:T(8,128)S(1)} %pad_maximum_fusion.refs_0_), channel_id=1, source_target_pairs={{0,5},{1,4},{2,7},{3,6},{4,1},{5,0},{6,3},{7,2},{8,13},{9,12},{10,... | collective-permute-start | bytes 466952 | tf_op jit(solution)/shard_map/ppermute | solution.py:412
  68.1 6.5 %collective-permute-start.22 = (f32[1,16,2432]{2,1,0:T(8,128)S(1)}, f32[1,16,2432]{2,1,0:T(8,128)S(1)}, u32[]{:S(2)}, u32[]{:S(2)}) collective-permute-start(f32[1,16,2432]{2,1,0:T(8,128)S(1)} %pad_maximum_fusion.refs_0_), channel_id=1, source_target_pairs={{0,4},{1,5},{2,3},{3,2},{4,0},{5,1},{6,7},{7,6},{8,12},{9,13},{10,... | collective-permute-start | bytes 466952 | tf_op jit(solution)/shard_map/ppermute | solution.py:412
  69.0 6.0 %collective-permute-start.21 = (f32[1,16,2432]{2,1,0:T(8,128)S(1)}, f32[1,16,2432]{2,1,0:T(8,128)S(1)}, u32[]{:S(2)}, u32[]{:S(2)}) collective-permute-start(f32[1,16,2432]{2,1,0:T(8,128)S(1)} %pad_maximum_fusion.refs_0_), channel_id=1, source_target_pairs={{0,1},{1,0},{2,6},{3,7},{4,5},{5,4},{6,2},{7,3},{8,9},{9,8},{10,14... | collective-permute-start | bytes 466952 | tf_op jit(solution)/shard_map/ppermute | solution.py:412
  69.7 5.8 %collective-permute-start.23 = (f32[1,16,2432]{2,1,0:T(8,128)S(1)}, f32[1,16,2432]{2,1,0:T(8,128)S(1)}, u32[]{:S(2)}, u32[]{:S(2)}) collective-permute-start(f32[1,16,2432]{2,1,0:T(8,128)S(1)} %pad_maximum_fusion.refs_0_), channel_id=1, source_target_pairs={{0,2},{1,3},{2,0},{3,1},{4,6},{5,7},{6,4},{7,5},{8,10},{9,11},{10,... | collective-permute-start | bytes 466952 | tf_op jit(solution)/shard_map/ppermute | solution.py:412
  74.6 1.4 %collective-permute-start.25 = (f32[1,16,2432]{2,1,0:T(8,128)S(1)}, f32[1,16,2432]{2,1,0:T(8,128)S(1)}, u32[]{:S(2)}, u32[]{:S(2)}) collective-permute-start(f32[1,16,2432]{2,1,0:T(8,128)S(1)} %collective-permute-done.22.refs_2_), channel_id=1, source_target_pairs={{0,2},{1,3},{2,0},{3,1},{4,6},{5,7},{6,4},{7,5},{8,10},{9,11},{10,... | collective-permute-start | bytes 466952 | tf_op jit(solution)/shard_map/ppermute | solution.py:412
  74.9 1.4 %collective-permute-start.24 = (f32[1,16,2432]{2,1,0:T(8,128)S(1)}, f32[1,16,2432]{2,1,0:T(8,128)S(1)}, u32[]{:S(2)}, u32[]{:S(2)}) collective-permute-start(f32[1,16,2432]{2,1,0:T(8,128)S(1)} %collective-permute-done.21.refs_1_), channel_id=1, source_target_pairs={{0,2},{1,3},{2,0},{3,1},{4,6},{5,7},{6,4},{7,5},{8,10},{9,11},{10,... | collective-permute-start | bytes 466952 | tf_op jit(solution)/shard_map/ppermute | solution.py:412
  75.1 1.4 %collective-permute-start.26 = (f32[1,16,2432]{2,1,0:T(8,128)S(1)}, f32[1,16,2432]{2,1,0:T(8,128)S(1)}, u32[]{:S(2)}, u32[]{:S(2)}) collective-permute-start(f32[1,16,2432]{2,1,0:T(8,128)S(1)} %collective-permute-done.20.refs_3_), channel_id=1, source_target_pairs={{0,2},{1,3},{2,0},{3,1},{4,6},{5,7},{6,4},{7,5},{8,10},{9,11},{10,... | collective-permute-start | bytes 466952 | tf_op jit(solution)/shard_map/ppermute | solution.py:412
